TPU v7x, 512 devices: a whole 4x8x8 slice. The times are simulated.
512 devices in a mesh: row: 32 (over y, x), col: 16 (over z, core).
Axes of the slice: x: 4, y: 8, z: 8, core: 2. Of those that a mesh axis runs over, the one named last changes fastest.
Arguments:
- relu21_preact: bfloat16 [1024, 1024, 128], P('row', 'col'), may hold values from -6 to 6
- relu22_preact: bfloat16 [1024, 1024, 128], P('row', 'col'), may hold values from -600 to 600
- relu31_preact: bfloat16 [512, 512, 256], P('row', 'col'), may hold values from -6 to 6
- relu32_preact: bfloat16 [512, 512, 256], P('row', 'col'), may hold values from -6 to 6
- relu33_preact: bfloat16 [512, 512, 256], P('row', 'col'), may hold values from -600 to 600
- target22_preact: bfloat16 [1024, 1024, 128], P('row', 'col'), may hold values from -600 to 600
- target33_preact: bfloat16 [512, 512, 256], P('row', 'col'), may hold values from -600 to 600
- pool1_argmax: int32 [1024, 65536], P('row', 'col'), may hold values from 0 to 3
- pool2_argmax: int32 [512, 65536], P('row', 'col'), may hold values from 0 to 3
- linear2_weight: float32 [128], replicated, may hold values from 0.2 to 2
- linear3_weight: float32 [256], replicated, may hold values from 0.2 to 2
- kernel21: bfloat16 [128, 576], replicated, may hold values from -0.25 to 0.25
- kernel22: bfloat16 [128, 1152], replicated, may hold values from -0.1875 to 0.1875
- kernel31: bfloat16 [256, 1152], replicated, may hold values from -0.1875 to 0.1875
- kernel32: bfloat16 [256, 2304], replicated, may hold values from -0.125 to 0.125
- kernel33: bfloat16 [256, 2304], replicated, may hold values from -0.125 to 0.125
Outputs:
- relu12_gradient: bfloat16 [2048, 131072], P('row', 'col')
Inputs may be any that keep to these rules, and one draw needn't show every extreme that they name: `pool1_argmax`: the position of the maximum in each 2x2 window, 0 top left, 1 top right, 2 bottom left, 3 bottom right; entry [r, c * 64 + ch] belongs to pooled cell (r, c) and channel ch. `pool2_argmax`: as for pool1_argmax, with 128 channels.
All inputs are finite; a program needn't handle non-finite values.
Results may differ from a plain program's by a relative error of at most 0.0059.
Values may be sent and summed in bfloat16 or wider, within the bound.
No kernel may reach another device: no remote copies, remote signals or barrier semaphores. Data moves between devices by JAX's collectives and lax.ppermute only.
A program may use at most 64 MiB of HBM per device.

v0:
```python
import jax
import jax.numpy as jnp
from jax import lax
from jax.sharding import PartitionSpec as P

EPSILON = 1e-06


def extended(cells, sides, width):
    for axis, dim in sides:
        count = lax.axis_size(axis)
        ends = count - 1
        head = lax.slice_in_dim(cells, 0, width, axis=dim)
        tail = lax.slice_in_dim(cells, cells.shape[dim] - width, cells.shape[dim], axis=dim)
        cells = jnp.concatenate(
            [
                lax.ppermute(tail, axis, [(i, (i + 1) % count) for i in range(ends)]),
                cells,
                lax.ppermute(head, axis, [((i + 1) % count, i) for i in range(ends)]),
            ],
            axis=dim,
        )
    return cells


def inject(preact, target, weight):
    feature = jnp.maximum(preact.astype(jnp.float32), 0.0)
    wanted = jnp.maximum(target.astype(jnp.float32), 0.0)
    feature_norm = jnp.sqrt(jnp.mean(feature * feature, axis=-1, keepdims=True) + EPSILON)
    wanted_norm = jnp.sqrt(jnp.mean(wanted * wanted, axis=-1, keepdims=True) + EPSILON)
    scaled = feature / feature_norm
    excess = 2.0 * weight * (scaled - wanted / wanted_norm)
    return (excess - scaled * jnp.mean(excess * scaled, axis=-1, keepdims=True)) / feature_norm


def masked(preact, values):
    return jnp.where(preact > 0, values, 0.0).astype(jnp.bfloat16)


def unpool(values, argmax_rows):
    height, breadth, channels = values.shape
    position = argmax_rows.reshape(height, breadth, channels)
    stripes = []
    for vertical in range(2):
        halves = [
            jnp.where(position == 2 * vertical + lateral, values, 0.0) for lateral in range(2)
        ]
        stripes.append(jnp.stack(halves, axis=2))
    return jnp.stack(stripes, axis=1).reshape(2 * height, 2 * breadth, channels)


def back_conv(padded, kernel):
    out_rows = padded.shape[0] - 2
    out_cols = padded.shape[1] - 2
    amount = kernel.shape[0]
    in_width = kernel.shape[1] // 9
    shifted = [
        padded[
            2 - offset // 3 : 2 - offset // 3 + out_rows, 2 - offset % 3 : 2 - offset % 3 + out_cols
        ]
        for offset in range(9)
    ]
    patches = jnp.stack(shifted, axis=2).reshape(out_rows * out_cols, 9 * amount)
    arranged = kernel.reshape(amount, 9, in_width).transpose(1, 0, 2).reshape(9 * amount, in_width)
    result = jnp.dot(patches, arranged, preferred_element_type=jnp.float32)
    return result.reshape(out_rows, out_cols, in_width)


def shards(
    relu21_preact,
    relu22_preact,
    relu31_preact,
    relu32_preact,
    relu33_preact,
    target22_preact,
    target33_preact,
    pool1_argmax,
    pool2_argmax,
    linear2_weight,
    linear3_weight,
    kernel21,
    kernel22,
    kernel31,
    kernel32,
    kernel33,
):
    seeded = masked(relu33_preact, inject(relu33_preact, target33_preact, linear3_weight))
    border = extended(jnp.stack([relu31_preact, relu32_preact]), (("row", 1), ("col", 2)), 2)
    padded = extended(seeded, (("row", 0), ("col", 1)), 3)
    gradient32 = masked(border[1], back_conv(padded, kernel33))
    gradient31 = masked(border[0, 1:-1, 1:-1], back_conv(gradient32, kernel32))
    pooled2 = back_conv(gradient31, kernel31)
    arriving = unpool(pooled2, pool2_argmax) + inject(
        relu22_preact, target22_preact, linear2_weight
    )
    gradient = masked(relu22_preact, arriving)
    pooled1 = None
    for kernel, preact in ((kernel22, relu21_preact), (kernel21, None)):
        padded = extended(gradient, (("row", 0), ("col", 1)), 1)
        spread = back_conv(padded, kernel)
        if preact is None:
            pooled1 = spread
        else:
            gradient = masked(preact, spread)
    result = unpool(pooled1, pool1_argmax).astype(jnp.bfloat16)
    return result.reshape(result.shape[0], -1)


def solution(mesh):
    in_specs = (
        P("row", "col", None),
        P("row", "col", None),
        P("row", "col", None),
        P("row", "col", None),
        P("row", "col", None),
        P("row", "col", None),
        P("row", "col", None),
        P("row", "col"),
        P("row", "col"),
        P(),
        P(),
        P(),
        P(),
        P(),
        P(),
        P(),
    )
    out_specs = P("row", "col")
    return jax.shard_map(shards, mesh=mesh, in_specs=in_specs, out_specs=out_specs, check_vma=False)
```

profile of v0, /device:TPU:223, one launch (start us, length us, event | category | flops | bytes accessed | tf_op | source)
XLA Modules:
  0.0 119.0 jit_solution(6330283178973134178)
XLA Ops:
  6.5 4.3 %collective-permute-start.4 = (bf16[3,32,256]{2,1,0:T(8,128)(2,1)}, bf16[3,32,256]{2,1,0:T(8,128)(2,1)}, u32[]{:S(2)}, u32[]{:S(2)}) collective-permute-start(bf16[3,32,256]{2,1,0:T(8,128)(2,1)} %get-tuple-element.39), channel_id=1, source_target_pairs={{0,16},{16,32},{32,48},{48,64},{64,80},{80,96},{96,112},{112,128},... | collective-permute-start | bytes 147464 | tf_op jit(solution)/shard_map/ppermute | solution.py:17
  10.9 1.9 %collective-permute-start.5 = (bf16[3,32,256]{2,1,0:T(8,128)(2,1)}, bf16[3,32,256]{2,1,0:T(8,128)(2,1)}, u32[]{:S(2)}, u32[]{:S(2)}) collective-permute-start(bf16[3,32,256]{2,1,0:T(8,128)(2,1)} %get-tuple-element.40), channel_id=1, source_target_pairs={{16,0},{32,16},{48,32},{64,48},{80,64},{96,80},{112,96},{128,112},... | collective-permute-start | bytes 147464 | tf_op jit(solution)/shard_map/ppermute | solution.py:19
  14.3 6.7 %collective-permute-start = (bf16[2,2,32,256]{3,2,1,0:T(8,128)(2,1)}, bf16[2,2,32,256]{3,2,1,0:T(8,128)(2,1)}, u32[]{:S(2)}, u32[]{:S(2)}) collective-permute-start(bf16[2,2,32,256]{3,2,1,0:T(8,128)(2,1)} %get-tuple-element.27), channel_id=1, source_target_pairs={{0,16},{16,32},{32,48},{48,64},{64,80},{80,96},{96,112},{112,128},... | collective-permute-start | bytes 196616 | tf_op jit(solution)/shard_map/ppermute | solution.py:17
  20.9 1.9 %collective-permute-start.1 = (bf16[2,2,32,256]{3,2,1,0:T(8,128)(2,1)}, bf16[2,2,32,256]{3,2,1,0:T(8,128)(2,1)}, u32[]{:S(2)}, u32[]{:S(2)}) collective-permute-start(bf16[2,2,32,256]{3,2,1,0:T(8,128)(2,1)} %get-tuple-element.28), channel_id=1, source_target_pairs={{16,0},{32,16},{48,32},{64,48},{80,64},{96,80},{112,96},{128,112},... | collective-permute-start | bytes 196616 | tf_op jit(solution)/shard_map/ppermute | solution.py:19
  33.6 6.6 %collective-permute-start.6 = (bf16[22,3,256]{2,1,0:T(4,128)(2,1)S(1)}, bf16[22,3,256]{2,1,0:T(4,128)(2,1)S(1)}, u32[]{:S(2)}, u32[]{:S(2)}) collective-permute-start(bf16[22,3,256]{2,1,0:T(4,128)(2,1)S(1)} %get-tuple-element.29), channel_id=1, source_target_pairs={{0,1},{1,2},{2,3},{3,4},{4,5},{5,6},{6,7},{7,8},{8,9},{9,10},{10,1... | collective-permute-start | bytes 101384 | tf_op jit(solution)/shard_map/ppermute | solution.py:17
  40.2 1.9 %collective-permute-start.7 = (bf16[22,3,256]{2,1,0:T(4,128)(2,1)S(1)}, bf16[22,3,256]{2,1,0:T(4,128)(2,1)S(1)}, u32[]{:S(2)}, u32[]{:S(2)}) collective-permute-start(bf16[22,3,256]{2,1,0:T(4,128)(2,1)S(1)} %get-tuple-element.30), channel_id=1, source_target_pairs={{1,0},{2,1},{3,2},{4,3},{5,4},{6,5},{7,6},{8,7},{9,8},{10,9},{11,1... | collective-permute-start | bytes 101384 | tf_op jit(solution)/shard_map/ppermute | solution.py:19
  43.2 4.9 %collective-permute-start.2 = (bf16[2,20,2,256]{3,2,1,0:T(2,128)(2,1)S(1)}, bf16[2,20,2,256]{3,2,1,0:T(2,128)(2,1)S(1)}, u32[]{:S(2)}, u32[]{:S(2)}) collective-permute-start(bf16[2,20,2,256]{3,2,1,0:T(2,128)(2,1)S(1)} %get-tuple-element.5), channel_id=1, source_target_pairs={{0,1},{1,2},{2,3},{3,4},{4,5},{5,6},{6,7},{7,8},{8,9},{9,10},{10,1... | collective-permute-start | bytes 122888 | tf_op jit(solution)/shard_map/ppermute | solution.py:17
  48.1 1.9 %collective-permute-start.3 = (bf16[2,20,2,256]{3,2,1,0:T(2,128)(2,1)S(1)}, bf16[2,20,2,256]{3,2,1,0:T(2,128)(2,1)S(1)}, u32[]{:S(2)}, u32[]{:S(2)}) collective-permute-start(bf16[2,20,2,256]{3,2,1,0:T(2,128)(2,1)S(1)} %get-tuple-element.6), channel_id=1, source_target_pairs={{1,0},{2,1},{3,2},{4,3},{5,4},{6,5},{7,6},{8,7},{9,8},{10,9},{11,1... | collective-permute-start | bytes 122888 | tf_op jit(solution)/shard_map/ppermute | solution.py:19
  52.0 2.6 %collective-permute-done.3 = bf16[2,20,2,256]{3,2,1,0:T(2,128)(2,1)S(1)} collective-permute-done((bf16[2,20,2,256]{3,2,1,0:T(2,128)(2,1)S(1)}, bf16[2,20,2,256]{3,2,1,0:T(2,128)(2,1)S(1)}, u32[]{:S(2)}, u32[]{:S(2)}) %collective-permute-start.3) | collective-permute-done | bytes 40992 | tf_op jit(solution)/shard_map/ppermute | solution.py:19
  54.6 2.0 %select_convert_fusion.5 = bf16[20,36,256]{2,1,0:T(8,128)(2,1)S(1)} fusion(bf16[2,20,2,256]{3,2,1,0:T(2,128)(2,1)S(1)} %collective-permute-done.3, bf16[2,20,2,256]{3,2,1,0:T(2,128)(2,1)S(1)} %collective-permute-done.2, bf16[2,2,32,256]{3,2,1,0:T(8,128)(2,1)} %collective-permute-done.1, bf16[2,2,32,256]{3,2,1,0:T(8,128)(2,1)} %collective-permute-done, ...), kind=kOutput, calls=%fused_computation.24 | convolution fusion | flops 851927040 | bytes 5603328 | tf_op jit(solution)/shard_map/dot_general | solution.py:65
  57.4 1.9 %select_convert_fusion.6 = bf16[18,34,256]{2,1,0:T(8,128)(2,1)S(1)} fusion(bf16[2,20,2,256]{3,2,1,0:T(2,128)(2,1)S(1)} %collective-permute-done.3, bf16[2,20,2,256]{3,2,1,0:T(2,128)(2,1)S(1)} %collective-permute-done.2, bf16[2,2,32,256]{3,2,1,0:T(8,128)(2,1)} %collective-permute-done.1, bf16[2,2,32,256]{3,2,1,0:T(8,128)(2,1)} %collective-permute-done, ...), kind=kOutput, calls=%fused_computation.25 | convolution fusion | flops 724137984 | bytes 5050368 | tf_op jit(solution)/shard_map/dot_general | solution.py:65
  63.0 7.0 %collective-permute-start.8 = (bf16[1,64,128]{2,1,0:T(8,128)(2,1)S(1)}, bf16[1,64,128]{2,1,0:T(8,128)(2,1)S(1)}, u32[]{:S(2)}, u32[]{:S(2)}) collective-permute-start(bf16[1,64,128]{2,1,0:T(8,128)(2,1)S(1)} %get-tuple-element.25), channel_id=1, source_target_pairs={{0,16},{16,32},{32,48},{48,64},{64,80},{80,96},{96,112},{112,128},... | collective-permute-start | bytes 49160 | tf_op jit(solution)/shard_map/ppermute | solution.py:17
  70.0 1.9 %collective-permute-start.9 = (bf16[1,64,128]{2,1,0:T(8,128)(2,1)S(1)}, bf16[1,64,128]{2,1,0:T(8,128)(2,1)S(1)}, u32[]{:S(2)}, u32[]{:S(2)}) collective-permute-start(bf16[1,64,128]{2,1,0:T(8,128)(2,1)S(1)} %get-tuple-element.26), channel_id=1, source_target_pairs={{16,0},{32,16},{48,32},{64,48},{80,64},{96,80},{112,96},{128,112},... | collective-permute-start | bytes 49160 | tf_op jit(solution)/shard_map/ppermute | solution.py:19
  71.9 5.9 %collective-permute-done.9 = bf16[1,64,128]{2,1,0:T(8,128)(2,1)S(1)} collective-permute-done((bf16[1,64,128]{2,1,0:T(8,128)(2,1)S(1)}, bf16[1,64,128]{2,1,0:T(8,128)(2,1)S(1)}, u32[]{:S(2)}, u32[]{:S(2)}) %collective-permute-start.9) | collective-permute-done | bytes 16416 | tf_op jit(solution)/shard_map/ppermute | solution.py:19
  77.8 1.9 %collective-permute-start.10 = (bf16[34,1,128]{2,1,0:T(2,128)(2,1)S(1)}, bf16[34,1,128]{2,1,0:T(2,128)(2,1)S(1)}, u32[]{:S(2)}, u32[]{:S(2)}) collective-permute-start(bf16[34,1,128]{2,1,0:T(2,128)(2,1)S(1)} %get-tuple-element.14), channel_id=1, source_target_pairs={{1,0},{2,1},{3,2},{4,3},{5,4},{6,5},{7,6},{8,7},{9,8},{10,9},{11,1... | collective-permute-start | bytes 26120 | tf_op jit(solution)/shard_map/ppermute | solution.py:19
  79.8 5.0 %collective-permute-start.11 = (bf16[34,1,128]{2,1,0:T(2,128)(2,1)S(1)}, bf16[34,1,128]{2,1,0:T(2,128)(2,1)S(1)}, u32[]{:S(2)}, u32[]{:S(2)}) collective-permute-start(bf16[34,1,128]{2,1,0:T(2,128)(2,1)S(1)} %get-tuple-element.13), channel_id=1, source_target_pairs={{0,1},{1,2},{2,3},{3,4},{4,5},{5,6},{6,7},{7,8},{8,9},{9,10},{10,1... | collective-permute-start | bytes 26120 | tf_op jit(solution)/shard_map/ppermute | solution.py:17
  88.7 1.9 %collective-permute-start.12 = (bf16[1,64,128]{2,1,0:T(8,128)(2,1)S(1)}, bf16[1,64,128]{2,1,0:T(8,128)(2,1)S(1)}, u32[]{:S(2)}, u32[]{:S(2)}) collective-permute-start(bf16[1,64,128]{2,1,0:T(8,128)(2,1)S(1)} %get-tuple-element.23), channel_id=1, source_target_pairs={{0,16},{16,32},{32,48},{48,64},{64,80},{80,96},{96,112},{112,128},... | collective-permute-start | bytes 49160 | tf_op jit(solution)/shard_map/ppermute | solution.py:17
  90.6 3.4 %collective-permute-start.13 = (bf16[1,64,128]{2,1,0:T(8,128)(2,1)S(1)}, bf16[1,64,128]{2,1,0:T(8,128)(2,1)S(1)}, u32[]{:S(2)}, u32[]{:S(2)}) collective-permute-start(bf16[1,64,128]{2,1,0:T(8,128)(2,1)S(1)} %get-tuple-element.24), channel_id=1, source_target_pairs={{16,0},{32,16},{48,32},{64,48},{80,64},{96,80},{112,96},{128,112},... | collective-permute-start | bytes 49160 | tf_op jit(solution)/shard_map/ppermute | solution.py:19
  94.0 4.4 %collective-permute-done.13 = bf16[1,64,128]{2,1,0:T(8,128)(2,1)S(1)} collective-permute-done((bf16[1,64,128]{2,1,0:T(8,128)(2,1)S(1)}, bf16[1,64,128]{2,1,0:T(8,128)(2,1)S(1)}, u32[]{:S(2)}, u32[]{:S(2)}) %collective-permute-start.13) | collective-permute-done | bytes 16416 | tf_op jit(solution)/shard_map/ppermute | solution.py:19
  98.5 1.9 %collective-permute-start.14 = (bf16[34,1,128]{2,1,0:T(2,128)(2,1)S(1)}, bf16[34,1,128]{2,1,0:T(2,128)(2,1)S(1)}, u32[]{:S(2)}, u32[]{:S(2)}) collective-permute-start(bf16[34,1,128]{2,1,0:T(2,128)(2,1)S(1)} %get-tuple-element.10), channel_id=1, source_target_pairs={{1,0},{2,1},{3,2},{4,3},{5,4},{6,5},{7,6},{8,7},{9,8},{10,9},{11,1... | collective-permute-start | bytes 26120 | tf_op jit(solution)/shard_map/ppermute | solution.py:19
  100.4 6.6 %collective-permute-start.15 = (bf16[34,1,128]{2,1,0:T(2,128)(2,1)S(1)}, bf16[34,1,128]{2,1,0:T(2,128)(2,1)S(1)}, u32[]{:S(2)}, u32[]{:S(2)}) collective-permute-start(bf16[34,1,128]{2,1,0:T(2,128)(2,1)S(1)} %get-tuple-element.9), channel_id=1, source_target_pairs={{0,1},{1,2},{2,3},{3,4},{4,5},{5,6},{6,7},{7,8},{8,9},{9,10},{10,1... | collective-permute-start | bytes 26120 | tf_op jit(solution)/shard_map/ppermute | solution.py:17
  111.6 1.8 %fusion.4 = (bf16[32,64,1,64]{3,1,0,2:T(8,128)(2,1)S(1)}, bf16[32,64,1,64]{3,1,0,2:T(8,128)(2,1)S(1)}, bf16[32,64,1,64]{3,1,0,2:T(8,128)(2,1)S(1)}, bf16[32,64,1,64]{3,1,0,2:T(8,128)(2,1)S(1)}) fusion(pred[32,64,64]{2,1,0:T(32,128)(4,1)S(1)} %eq.74, pred[32,64,64]{2,1,0:T(32,128)(4,1)S(1)} %eq.95, pred[32,64,64]{2,1,0:T(32,128)(4,1)S(1)} %eq.92, ...), kind=kOutput, calls=%fused_computation.30 | convolution fusion | flops 302514176 | bytes 6438912 | tf_op jit(solution)/shard_map/dot_general | solution.py:65
  114.3 2.2 %copy.68 = bf16[32,2,64,2,64]{4,3,2,1,0:T(2,128)(2,1)S(1)} copy(bf16[32,2,64,2,64]{4,2,0,3,1:T(8,128)(2,1)S(1)} %pad_maximum_fusion) | data formatting | bytes 2097152 | tf_op jit(solution)/shard_map/stack | solution.py:49
  116.5 2.5 %convert_element_type.41 = bf16[64,8192]{1,0:T(8,128)(2,1)} reshape(bf16[32,2,64,2,64]{4,3,2,1,0:T(2,128)(2,1)S(1)} %copy.68) | data formatting | bytes 2097152 | tf_op jit(solution)/shard_map/convert_element_type | solution.py:105
  (148 shorter events, 35.1 us)
Async XLA Ops:
  0.0 111.6 %copy-start = (bf16[128,576]{0,1:T(8,128)(2,1)S(1)}, bf16[128,576]{0,1:T(8,128)(2,1)}, u32[]{:S(2)}) copy-start(bf16[128,576]{0,1:T(8,128)(2,1)} %param.27) | copy-start | bytes 442372
  0.0 24.0 %copy-start.2 = (bf16[32,64,128]{2,1,0:T(8,128)(2,1)S(1)}, bf16[32,64,128]{2,1,0:T(8,128)(2,1)}, u32[]{:S(2)}) copy-start(bf16[32,64,128]{2,1,0:T(8,128)(2,1)} %param.21) | copy-start | bytes 1572868
  0.0 24.3 %copy-start.1 = (bf16[32,64,128]{2,1,0:T(8,128)(2,1)S(1)}, bf16[32,64,128]{2,1,0:T(8,128)(2,1)}, u32[]{:S(2)}) copy-start(bf16[32,64,128]{2,1,0:T(8,128)(2,1)} %param.17) | copy-start | bytes 1572868
  0.0 24.7 %copy-start.20 = (f32[128]{0:T(128)S(1)}, f32[128]{0:T(128)}, u32[]{:S(2)}) copy-start(f32[128]{0:T(128)} %param.25) | copy-start | bytes 1540
  0.0 26.4 %copy-start.3 = (bf16[256,2304]{1,0:T(8,128)(2,1)S(1)}, bf16[256,2304]{1,0:T(8,128)(2,1)}, u32[]{:S(2)}) copy-start(bf16[256,2304]{1,0:T(8,128)(2,1)} %param.31) | copy-start | bytes 3538948
  6.5 26.3 %collective-permute-start.4 = (bf16[3,32,256]{2,1,0:T(8,128)(2,1)}, bf16[3,32,256]{2,1,0:T(8,128)(2,1)}, u32[]{:S(2)}, u32[]{:S(2)}) collective-permute-start(bf16[3,32,256]{2,1,0:T(8,128)(2,1)} %get-tuple-element.39), channel_id=1, source_target_pairs={{0,16},{16,32},{32,48},{48,64},{64,80},{80,96},{96,112},{112,128},... | collective-permute-start | bytes 147464 | tf_op jit(solution)/shard_map/ppermute | solution.py:17
  10.9 21.9 %collective-permute-start.5 = (bf16[3,32,256]{2,1,0:T(8,128)(2,1)}, bf16[3,32,256]{2,1,0:T(8,128)(2,1)}, u32[]{:S(2)}, u32[]{:S(2)}) collective-permute-start(bf16[3,32,256]{2,1,0:T(8,128)(2,1)} %get-tuple-element.40), channel_id=1, source_target_pairs={{16,0},{32,16},{48,32},{64,48},{80,64},{96,80},{112,96},{128,112},... | collective-permute-start | bytes 147464 | tf_op jit(solution)/shard_map/ppermute | solution.py:19
  14.3 27.9 %collective-permute-start = (bf16[2,2,32,256]{3,2,1,0:T(8,128)(2,1)}, bf16[2,2,32,256]{3,2,1,0:T(8,128)(2,1)}, u32[]{:S(2)}, u32[]{:S(2)}) collective-permute-start(bf16[2,2,32,256]{3,2,1,0:T(8,128)(2,1)} %get-tuple-element.27), channel_id=1, source_target_pairs={{0,16},{16,32},{32,48},{48,64},{64,80},{80,96},{96,112},{112,128},... | collective-permute-start | bytes 196616 | tf_op jit(solution)/shard_map/ppermute | solution.py:17
  20.9 21.2 %collective-permute-start.1 = (bf16[2,2,32,256]{3,2,1,0:T(8,128)(2,1)}, bf16[2,2,32,256]{3,2,1,0:T(8,128)(2,1)}, u32[]{:S(2)}, u32[]{:S(2)}) collective-permute-start(bf16[2,2,32,256]{3,2,1,0:T(8,128)(2,1)} %get-tuple-element.28), channel_id=1, source_target_pairs={{16,0},{32,16},{48,32},{64,48},{80,64},{96,80},{112,96},{128,112},... | collective-permute-start | bytes 196616 | tf_op jit(solution)/shard_map/ppermute | solution.py:19
  26.4 15.8 %copy-start.5 = (bf16[16,32,256]{2,1,0:T(8,128)(2,1)S(1)}, bf16[16,32,256]{2,1,0:T(8,128)(2,1)}, u32[]{:S(2)}) copy-start(bf16[16,32,256]{2,1,0:T(8,128)(2,1)} %param.19) | copy-start | bytes 786436
  33.6 16.4 %collective-permute-start.6 = (bf16[22,3,256]{2,1,0:T(4,128)(2,1)S(1)}, bf16[22,3,256]{2,1,0:T(4,128)(2,1)S(1)}, u32[]{:S(2)}, u32[]{:S(2)}) collective-permute-start(bf16[22,3,256]{2,1,0:T(4,128)(2,1)S(1)} %get-tuple-element.29), channel_id=1, source_target_pairs={{0,1},{1,2},{2,3},{3,4},{4,5},{5,6},{6,7},{7,8},{8,9},{9,10},{10,1... | collective-permute-start | bytes 101384 | tf_op jit(solution)/shard_map/ppermute | solution.py:17
  40.2 9.8 %collective-permute-start.7 = (bf16[22,3,256]{2,1,0:T(4,128)(2,1)S(1)}, bf16[22,3,256]{2,1,0:T(4,128)(2,1)S(1)}, u32[]{:S(2)}, u32[]{:S(2)}) collective-permute-start(bf16[22,3,256]{2,1,0:T(4,128)(2,1)S(1)} %get-tuple-element.30), channel_id=1, source_target_pairs={{1,0},{2,1},{3,2},{4,3},{5,4},{6,5},{7,6},{8,7},{9,8},{10,9},{11,1... | collective-permute-start | bytes 101384 | tf_op jit(solution)/shard_map/ppermute | solution.py:19
  43.2 8.8 %collective-permute-start.2 = (bf16[2,20,2,256]{3,2,1,0:T(2,128)(2,1)S(1)}, bf16[2,20,2,256]{3,2,1,0:T(2,128)(2,1)S(1)}, u32[]{:S(2)}, u32[]{:S(2)}) collective-permute-start(bf16[2,20,2,256]{3,2,1,0:T(2,128)(2,1)S(1)} %get-tuple-element.5), channel_id=1, source_target_pairs={{0,1},{1,2},{2,3},{3,4},{4,5},{5,6},{6,7},{7,8},{8,9},{9,10},{10,1... | collective-permute-start | bytes 122888 | tf_op jit(solution)/shard_map/ppermute | solution.py:17
  48.1 6.5 %collective-permute-start.3 = (bf16[2,20,2,256]{3,2,1,0:T(2,128)(2,1)S(1)}, bf16[2,20,2,256]{3,2,1,0:T(2,128)(2,1)S(1)}, u32[]{:S(2)}, u32[]{:S(2)}) collective-permute-start(bf16[2,20,2,256]{3,2,1,0:T(2,128)(2,1)S(1)} %get-tuple-element.6), channel_id=1, source_target_pairs={{1,0},{2,1},{3,2},{4,3},{5,4},{6,5},{7,6},{8,7},{9,8},{10,9},{11,1... | collective-permute-start | bytes 122888 | tf_op jit(solution)/shard_map/ppermute | solution.py:19
  61.0 23.8 %copy-start.8 = (bf16[128,1152]{1,0:T(8,128)(2,1)S(1)}, bf16[128,1152]{1,0:T(8,128)(2,1)}, u32[]{:S(2)}) copy-start(bf16[128,1152]{1,0:T(8,128)(2,1)} %param.28) | copy-start | bytes 884740
  63.0 8.9 %collective-permute-start.8 = (bf16[1,64,128]{2,1,0:T(8,128)(2,1)S(1)}, bf16[1,64,128]{2,1,0:T(8,128)(2,1)S(1)}, u32[]{:S(2)}, u32[]{:S(2)}) collective-permute-start(bf16[1,64,128]{2,1,0:T(8,128)(2,1)S(1)} %get-tuple-element.25), channel_id=1, source_target_pairs={{0,16},{16,32},{32,48},{48,64},{64,80},{80,96},{96,112},{112,128},... | collective-permute-start | bytes 49160 | tf_op jit(solution)/shard_map/ppermute | solution.py:17
  70.0 7.8 %collective-permute-start.9 = (bf16[1,64,128]{2,1,0:T(8,128)(2,1)S(1)}, bf16[1,64,128]{2,1,0:T(8,128)(2,1)S(1)}, u32[]{:S(2)}, u32[]{:S(2)}) collective-permute-start(bf16[1,64,128]{2,1,0:T(8,128)(2,1)S(1)} %get-tuple-element.26), channel_id=1, source_target_pairs={{16,0},{32,16},{48,32},{64,48},{80,64},{96,80},{112,96},{128,112},... | collective-permute-start | bytes 49160 | tf_op jit(solution)/shard_map/ppermute | solution.py:19
  77.8 7.2 %collective-permute-start.10 = (bf16[34,1,128]{2,1,0:T(2,128)(2,1)S(1)}, bf16[34,1,128]{2,1,0:T(2,128)(2,1)S(1)}, u32[]{:S(2)}, u32[]{:S(2)}) collective-permute-start(bf16[34,1,128]{2,1,0:T(2,128)(2,1)S(1)} %get-tuple-element.14), channel_id=1, source_target_pairs={{1,0},{2,1},{3,2},{4,3},{5,4},{6,5},{7,6},{8,7},{9,8},{10,9},{11,1... | collective-permute-start | bytes 26120 | tf_op jit(solution)/shard_map/ppermute | solution.py:19
  79.8 5.7 %collective-permute-start.11 = (bf16[34,1,128]{2,1,0:T(2,128)(2,1)S(1)}, bf16[34,1,128]{2,1,0:T(2,128)(2,1)S(1)}, u32[]{:S(2)}, u32[]{:S(2)}) collective-permute-start(bf16[34,1,128]{2,1,0:T(2,128)(2,1)S(1)} %get-tuple-element.13), channel_id=1, source_target_pairs={{0,1},{1,2},{2,3},{3,4},{4,5},{5,6},{6,7},{7,8},{8,9},{9,10},{10,1... | collective-permute-start | bytes 26120 | tf_op jit(solution)/shard_map/ppermute | solution.py:17
  87.2 19.7 %copy-start.7 = (s32[32,4096]{1,0:T(8,128)S(1)}, s32[32,4096]{1,0:T(8,128)}, u32[]{:S(2)}) copy-start(s32[32,4096]{1,0:T(8,128)} %param.23) | copy-start | bytes 1572868
  88.7 5.3 %collective-permute-start.12 = (bf16[1,64,128]{2,1,0:T(8,128)(2,1)S(1)}, bf16[1,64,128]{2,1,0:T(8,128)(2,1)S(1)}, u32[]{:S(2)}, u32[]{:S(2)}) collective-permute-start(bf16[1,64,128]{2,1,0:T(8,128)(2,1)S(1)} %get-tuple-element.23), channel_id=1, source_target_pairs={{0,16},{16,32},{32,48},{48,64},{64,80},{80,96},{96,112},{112,128},... | collective-permute-start | bytes 49160 | tf_op jit(solution)/shard_map/ppermute | solution.py:17
  90.6 7.8 %collective-permute-start.13 = (bf16[1,64,128]{2,1,0:T(8,128)(2,1)S(1)}, bf16[1,64,128]{2,1,0:T(8,128)(2,1)S(1)}, u32[]{:S(2)}, u32[]{:S(2)}) collective-permute-start(bf16[1,64,128]{2,1,0:T(8,128)(2,1)S(1)} %get-tuple-element.24), channel_id=1, source_target_pairs={{16,0},{32,16},{48,32},{64,48},{80,64},{96,80},{112,96},{128,112},... | collective-permute-start | bytes 49160 | tf_op jit(solution)/shard_map/ppermute | solution.py:19
  98.5 11.6 %collective-permute-start.14 = (bf16[34,1,128]{2,1,0:T(2,128)(2,1)S(1)}, bf16[34,1,128]{2,1,0:T(2,128)(2,1)S(1)}, u32[]{:S(2)}, u32[]{:S(2)}) collective-permute-start(bf16[34,1,128]{2,1,0:T(2,128)(2,1)S(1)} %get-tuple-element.10), channel_id=1, source_target_pairs={{1,0},{2,1},{3,2},{4,3},{5,4},{6,5},{7,6},{8,7},{9,8},{10,9},{11,1... | collective-permute-start | bytes 26120 | tf_op jit(solution)/shard_map/ppermute | solution.py:19
  100.4 9.7 %collective-permute-start.15 = (bf16[34,1,128]{2,1,0:T(2,128)(2,1)S(1)}, bf16[34,1,128]{2,1,0:T(2,128)(2,1)S(1)}, u32[]{:S(2)}, u32[]{:S(2)}) collective-permute-start(bf16[34,1,128]{2,1,0:T(2,128)(2,1)S(1)} %get-tuple-element.9), channel_id=1, source_target_pairs={{0,1},{1,2},{2,3},{3,4},{4,5},{5,6},{6,7},{7,8},{8,9},{9,10},{10,1... | collective-permute-start | bytes 26120 | tf_op jit(solution)/shard_map/ppermute | solution.py:17
  (13 other events, 32.9 us)
where the time goes:
time: 120 us; the launch traced here: 119 us
  starting transfers between devices  59.8 us (50%)
  local copies, waits for them, and re-layouts  19.9 us (17%)
  other arithmetic  17.1 us (14%)
  waiting for transfers between devices  13.4 us (11%)
  matrix products  7.82 us (7%)
    ppermute x8, starting transfers between devices, extended(): lax.ppermute(tail, axis, [(i, (i + 1) % count) for i in range(ends)])  42.9 us
    ppermute x8, starting transfers between devices, extended(): lax.ppermute(head, axis, [((i + 1) % count, i) for i in range(ends)])  16.8 us
    ppermute x8, waiting for transfers between devices, extended(): lax.ppermute(head, axis, [((i + 1) % count, i) for i in range(ends)])  12.9 us
    unnamed x86, local copies, waits for them, and re-layouts  10.8 us
    dot_general x5, matrix products, back_conv(): result = jnp.dot(patches, arranged, preferred_element_type=jnp.float32)  7.82 us
    slice x3, other arithmetic, extended(): lax.slice_in_dim(cells, cells.shape[dim] - width, cells.shape[dim], axis=...  3.28 us
    another operation x2, local copies, waits for them, and re-layouts, unpool(): return jnp.stack(stripes, axis=1).reshape(2 * height, 2 * breadth, channels)  3 us
    eq x4, local copies, waits for them, and re-layouts, unpool(): position == 2 * vertical + lateral  2.77 us
  transfers between devices with their start and end apart: 16, of which 4 were waited for; matrix products, arithmetic and copies ran while one was open for 15% of the time, Pallas kernels for 0%

commit v1 on v0

v1 whole, which is shorter than its diff:
```python
import jax
import jax.numpy as jnp
from jax import lax
from jax.experimental import pallas as pl
from jax.experimental.pallas import tpu as pltpu
from jax.sharding import PartitionSpec as P

EPSILON = 1e-06
F32 = jnp.float32
BF16 = jnp.bfloat16

ROW_SEED, ROW_M32, ROW_M31, ROW_M22, ROW_I22, ROW_M21, ROW_A2, ROW_TOTAL = (
    0, 256, 448, 576, 704, 832, 896, 928)
COL_SEED, COL_M32, COL_M31, COL_M22, COL_I22, COL_M21, COL_A2, COL_TOTAL = (
    0, 192, 336, 432, 512, 592, 632, 656)
W3 = 48
W2 = 80
WU = 96
WP = 88
LEAD = 8


def inject(preact, target, weight):
    count = preact.shape[-1]
    feature = jnp.maximum(preact.astype(F32), 0.0)
    wanted = jnp.maximum(target.astype(F32), 0.0)
    scale = lax.rsqrt(jnp.sum(feature * feature, axis=-1, keepdims=True) * (1.0 / count) + EPSILON)
    other = lax.rsqrt(jnp.sum(wanted * wanted, axis=-1, keepdims=True) * (1.0 / count) + EPSILON)
    scaled = feature * scale
    excess = (2.0 * weight) * (scaled - wanted * other)
    mean = jnp.sum(excess * scaled, axis=-1, keepdims=True) * (1.0 / count)
    return (excess - scaled * mean) * scale


def pack_rows(m33, t33, m32, m31, m22t, m22b, t22t, t22b, m21t, m21b, a2, w2, w3, seeds, up, down):
    rows, cols, ch = m33.shape
    step = 4
    for r in range(0, rows, step):
        p = m33[r : r + step].reshape(step * cols, ch)
        value = inject(p, t33[r : r + step].reshape(step * cols, ch), w3[...])
        value = jnp.where(p.astype(F32) > 0, value, 0.0).astype(BF16)
        seeds[r : r + step] = value.reshape(step, cols, ch)
    for out, first, m22, t22, m21, edge in (
        (up, 0, m22t, t22t, m21t, 0),
        (down, 1, m22b, t22b, m21b, rows - 1),
    ):
        for source, base, width in ((seeds, ROW_SEED, 4), (m32, ROW_M32, 3), (m31, ROW_M31, 2)):
            begin = rows - width if first else 0
            for k in range(width):
                for h in range(2):
                    at = base + (k * 2 + h) * cols
                    out[at : at + cols] = source[begin + k, :, h * 128 : (h + 1) * 128]
        wide = m22.shape[1]
        p = m22[...].reshape(2 * wide, 128)
        out[ROW_M22 : ROW_M22 + 2 * wide] = p
        out[ROW_I22 : ROW_I22 + 2 * wide] = inject(
            p, t22[...].reshape(2 * wide, 128), w2[...]
        ).astype(BF16)
        out[ROW_M21 : ROW_M21 + wide] = m21[0]
        line = a2[edge : edge + 1, :].astype(F32)
        line = jnp.concatenate([line[:, c * 128 : (c + 1) * 128] for c in range(cols)], axis=0)
        out[ROW_A2 : ROW_A2 + cols] = line.astype(BF16)


def own_inject(m22, t22, w2, k21, i22, k21d):
    rows, cols, ch = m22.shape
    step = 4

    @pl.loop(0, rows // step)
    def _(i):
        at = pl.ds(i * step, step)
        value = inject(m22[at].reshape(step * cols, ch), t22[at].reshape(step * cols, ch), w2[...])
        i22[at] = value.reshape(step, cols, ch)

    half = k21.shape[1] // 9
    for t in range(9):
        tap = k21[:, t * half : (t + 1) * half].astype(F32)
        k21d[:, t * 128 : (t + 1) * 128] = jnp.concatenate([tap, tap], axis=1).astype(BF16)


def pack_cols(seeds, m32, m31, m22, i22, m21, a2, above, below, left, right, s256, s128, line, sa, flat):
    rows, cols, _ = seeds.shape
    for out, at_end in ((left, False), (right, True)):
        for source, base, row_base, width in (
            (seeds, COL_SEED, ROW_SEED, 4), (m32, COL_M32, ROW_M32, 3), (m31, COL_M31, ROW_M31, 2),
        ):
            c0 = cols - 16 if at_end else 0
            pick = 16 - width if at_end else 0
            for h in range(2):
                sl = slice(h * 128, (h + 1) * 128)
                own = source[:, c0 : c0 + 16, sl].astype(F32).reshape(rows * 16, 128)
                s256[width * 16 : (width + rows) * 16] = own
                for k in range(width):
                    at = row_base + (k * 2 + h) * cols + c0
                    s256[k * 16 : (k + 1) * 16] = above[at : at + 16].astype(F32)
                    low = (width + rows + k) * 16
                    s256[low : low + 16] = below[at : at + 16].astype(F32)
                for c in range(width):
                    to = base + (c * 2 + h) * 24
                    flat[to : to + 24] = s256[pl.ds(pick + c, 24, stride=16), :]
        tall, wide, _ = m22.shape
        c0 = wide - 16 if at_end else 0
        for source, base, row_base, width in (
            (m22, COL_M22, ROW_M22, 2), (i22, COL_I22, ROW_I22, 2), (m21, COL_M21, ROW_M21, 1),
        ):
            pick = 16 - width if at_end else 0
            own = source[:, c0 : c0 + 16].astype(F32).reshape(tall * 16, 128)
            s128[width * 16 : (width + tall) * 16] = own
            for k in range(width):
                at = row_base + k * wide + c0
                s128[k * 16 : (k + 1) * 16] = above[at : at + 16].astype(F32)
                low = (width + tall + k) * 16
                s128[low : low + 16] = below[at : at + 16].astype(F32)
            for c in range(width):
                to = base + c * 40
                flat[to : to + 40] = s128[pl.ds(pick + c, 40, stride=16), :]
        edge = cols - 1 if at_end else 0
        flat[COL_A2 + 1 : COL_A2 + 1 + rows] = a2[:, edge * 128 : (edge + 1) * 128].astype(F32)
        line[...] = above[ROW_A2 : ROW_A2 + cols].astype(F32)
        flat[COL_A2 : COL_A2 + 1] = line[edge : edge + 1]
        line[...] = below[ROW_A2 : ROW_A2 + cols].astype(F32)
        flat[COL_A2 + 1 + rows : COL_A2 + 2 + rows] = line[edge : edge + 1]
        out[...] = flat[...].astype(BF16)


def conv(x, kernel, row, count):
    width, amount = x.shape[1], x.shape[2]
    span = kernel.shape[1] // 3
    total = None
    for dy in range(3):
        block = x[pl.ds(row + 2 - dy, count)].reshape(count * width, amount)
        term = jnp.dot(block, kernel[:, dy * span : (dy + 1) * span], preferred_element_type=F32)
        total = term if total is None else total + term
    n = span // 3
    size = count * width
    before = pltpu.roll(total[:, :n], size - 1, 0)
    after = pltpu.roll(total[:, 2 * n :], 1, 0)
    return before + total[:, n : 2 * n] + after


def main(seeds, m32, m31, m22, i22, m21, a2, a1, above, below, fl, fr, k33, k32, k31, k22, k21d,
         result, e33, e32, e31, ea, e22, ei, e21, x33, x32, x31, u2, g22, g21, p1, o1):
    rows, cols, _ = seeds.shape
    tall, wide, _ = m22.shape

    for source, stage, row_base, col_base, width in (
        (seeds, e33, ROW_SEED, COL_SEED, 4), (m32, e32, ROW_M32, COL_M32, 3), (m31, e31, ROW_M31, COL_M31, 2),
    ):
        for h in range(2):
            sl = slice(h * 128, (h + 1) * 128)

            @pl.loop(0, rows)
            def _(r):
                to = pl.multiple_of((r + width) * W3 + LEAD, 8)
                stage[h, pl.ds(to, cols)] = source[r, :, sl].astype(F32)

            for k in range(width):
                at = row_base + (k * 2 + h) * cols
                to = k * W3 + LEAD
                stage[h, to : to + cols] = above[at : at + cols].astype(F32)
                to = (width + rows + k) * W3 + LEAD
                stage[h, to : to + cols] = below[at : at + cols].astype(F32)
            for c in range(width):
                at = col_base + (c * 2 + h) * 24
                stage.at[h][pl.ds(LEAD - width + c, 24, stride=W3), :] = fl[at : at + 24].astype(F32)
                stage.at[h][pl.ds(LEAD + cols + c, 24, stride=W3), :] = fr[at : at + 24].astype(F32)
    for source, stage, row_base, col_base, width in (
        (m22, e22, ROW_M22, COL_M22, 2), (i22, ei, ROW_I22, COL_I22, 2), (m21, e21, ROW_M21, COL_M21, 1),
    ):

        @pl.loop(0, tall)
        def _(r):
            to = pl.multiple_of((r + width) * W2 + LEAD, 8)
            stage[pl.ds(to, wide)] = source[r].astype(F32)

        for k in range(width):
            at = row_base + k * wide
            to = k * W2 + LEAD
            stage[to : to + wide] = above[at : at + wide].astype(F32)
            to = (width + tall + k) * W2 + LEAD
            stage[to : to + wide] = below[at : at + wide].astype(F32)
        for c in range(width):
            at = col_base + c * 40
            stage[pl.ds(LEAD - width + c, 40, stride=W2), :] = fl[at : at + 40].astype(F32)
            stage[pl.ds(LEAD + wide + c, 40, stride=W2), :] = fr[at : at + 40].astype(F32)
    for c in range(cols):
        ea[pl.ds(W3 + LEAD + c, rows, stride=W3), :] = a2[:, c * 128 : (c + 1) * 128].astype(F32)
    ea[LEAD : LEAD + cols] = above[ROW_A2 : ROW_A2 + cols].astype(F32)
    to = (rows + 1) * W3 + LEAD
    ea[to : to + cols] = below[ROW_A2 : ROW_A2 + cols].astype(F32)
    ea[pl.ds(LEAD - 1, 24, stride=W3), :] = fl[COL_A2 : COL_A2 + 24].astype(F32)
    ea[pl.ds(LEAD + cols, 24, stride=W3), :] = fr[COL_A2 : COL_A2 + 24].astype(F32)

    @pl.loop(0, rows + 8)
    def _(r):
        at = pl.ds(pl.multiple_of(r * W3, W3), W3)
        for h in range(2):
            x33[r, :, h * 128 : (h + 1) * 128] = e33[h, at].astype(BF16)

    for x, kernel, stage, nxt, count in ((x33, k33, e32, x32, 2), (x32, k32, e31, x31, 2)):

        @pl.loop(0, nxt.shape[0] // count)
        def _(i):
            row = i * count
            value = conv(x, kernel, row, count)
            at = pl.ds(pl.multiple_of(row * W3, W3), count * W3)
            for h in range(2):
                part = jnp.where(stage[h, at] > 0, value[:, h * 128 : (h + 1) * 128], 0.0)
                nxt[pl.ds(row, count), :, h * 128 : (h + 1) * 128] = part.astype(BF16).reshape(
                    count, W3, 128
                )

    @pl.loop(0, (rows + 2) // 3)
    def _(i):
        row = i * 3
        value = conv(x31, k31, row, 3)
        for k in range(3):
            part = value[k * W3 : (k + 1) * W3]
            where = ea[pl.ds(pl.multiple_of((row + k) * W3, W3), W3)]
            for a in range(2):
                for b in range(2):
                    to = (2 * (row + k) + a) * WU + b
                    u2[pl.ds(to, W3, stride=2), :] = jnp.where(where == 2.0 * a + b, part, 0.0)

    @pl.loop(0, tall + 4)
    def _(r):
        at = pl.ds(pl.multiple_of(r * W2, W2), W2)
        arriving = u2[pl.ds(pl.multiple_of(r * WU + LEAD, 8), W2)] + ei[at]
        g22[r] = jnp.where(e22[at] > 0, arriving, 0.0).astype(BF16)

    @pl.loop(0, (tall + 2) // 2)
    def _(i):
        row = i * 2
        value = conv(g22, k22, row, 2)
        value = jnp.where(e21[pl.ds(pl.multiple_of(row * W2, W2), 2 * W2)] > 0, value, 0.0)
        g21[pl.ds(row, 2)] = value.astype(BF16).reshape(2, W2, 128)

    @pl.loop(0, tall // 2)
    def _(i):
        row = i * 2
        value = conv(g21, k21d, row, 2)
        for k in range(2):
            to = pl.multiple_of((row + k) * WP, 8)
            p1[pl.ds(to, W2)] = value[k * W2 : (k + 1) * W2]

    lane = lax.broadcasted_iota(jnp.int32, (tall, 128), 1)
    high = lane >= 64
    shift = jnp.where(high, 1, 0)

    @pl.loop(0, wide // 2)
    def _(t):
        where = a1[:, pl.ds(pl.multiple_of(t * 128, 128), 128)]
        turned = pltpu.roll(where, 64, 1)
        for odd in range(2):
            spread = jnp.where(high, where, turned) if odd else jnp.where(high, turned, where)
            spread = spread - shift
            value = p1[pl.ds(LEAD + 2 * t + odd, tall, stride=WP), :]
            for a in range(2):
                o1.at[odd][pl.ds(a, tall, stride=2), :] = jnp.where(spread == 2 * a, value, 0.0)
            to = pl.ds(pl.multiple_of((2 * t + odd) * 128, 128), 128)
            result[:, to] = o1[odd].astype(BF16)


def whole(array):
    zeros = (0,) * array.ndim
    return pl.BlockSpec(array.shape, lambda i: zeros)


def call(body, args, outs, scratch=(), specs=None, cost=0):
    shapes = [jax.ShapeDtypeStruct(s, d) for s, d in outs]
    return pl.pallas_call(
        body,
        grid=(1,),
        in_specs=specs or [whole(a) for a in args],
        out_specs=[whole(s) for s in shapes],
        out_shape=shapes,
        scratch_shapes=[pltpu.VMEM(s, d) for s, d in scratch],
        cost_estimate=pl.CostEstimate(flops=cost, bytes_accessed=4000000, transcendentals=0),
        compiler_params=pltpu.CompilerParams(vmem_limit_bytes=50 << 20),
    )(*args)


def swap(first, last, axis):
    count = lax.axis_size(axis)
    from_before = lax.ppermute(last, axis, [(i, i + 1) for i in range(count - 1)])
    from_after = lax.ppermute(first, axis, [(i + 1, i) for i in range(count - 1)])
    return from_before, from_after


def shards(m21, m22, m31, m32, m33, t22, t33, a1, a2, w2, w3, k21, k22, k31, k32, k33):
    rows, cols, ch3 = m33.shape
    tall, wide, ch2 = m22.shape
    w2 = w2.reshape(1, ch2)
    w3 = w3.reshape(1, ch3)

    def band(height, index):
        return pl.BlockSpec((height, wide, ch2), lambda i: (index, 0, 0))

    args = (m33, t33, m32, m31, m22, m22, t22, t22, m21, m21, a2, w2, w3)
    specs = [whole(a) for a in args]
    specs[4], specs[5] = band(2, 0), band(2, tall // 2 - 1)
    specs[6], specs[7] = band(2, 0), band(2, tall // 2 - 1)
    specs[8], specs[9] = band(1, 0), band(1, tall - 1)
    seeds, up, down = call(
        pack_rows, args,
        [((rows, cols, ch3), BF16), ((ROW_TOTAL, 128), BF16), ((ROW_TOTAL, 128), BF16)],
        specs=specs, cost=10**9,
    )
    above, below = swap(up, down, "row")
    i22, k21d = call(
        own_inject, (m22, t22, w2, k21),
        [((tall, wide, ch2), F32), ((k21.shape[0], 9 * 128), BF16)], cost=10**9,
    )
    left, right = call(
        pack_cols, (seeds, m32, m31, m22, i22, m21, a2, above, below),
        [((COL_TOTAL, 128), BF16), ((COL_TOTAL, 128), BF16)],
        scratch=[((24 * 16, 128), F32), ((40 * 16, 128), F32), ((cols, 128), F32), ((8, 128), F32),
                 ((COL_TOTAL, 128), F32)],
        cost=10**9,
    )
    fl, fr = swap(left, right, "col")
    area3, area2 = (rows + 8) * W3, (tall + 8) * W2
    (result,) = call(
        main,
        (seeds, m32, m31, m22, i22, m21, a2, a1, above, below, fl, fr, k33, k32, k31, k22, k21d),
        [((2 * tall, 2 * wide * 64), BF16)],
        scratch=[
            ((2, area3, 128), F32), ((2, area3, 128), F32), ((2, area3, 128), F32), ((area3, 128), F32),
            ((area2, 128), F32), ((area2, 128), F32), ((area2, 128), F32),
            ((rows + 8, W3, ch3), BF16), ((rows + 6, W3, ch3), BF16), ((rows + 4, W3, ch3), BF16),
            (((tall + 4) * WU, 128), F32), ((tall + 4, W2, ch2), BF16), ((tall + 2, W2, ch2), BF16),
            ((tall * WP, 128), F32), ((2, 2 * tall, 128), F32),
        ],
        cost=3 * 10**9,
    )
    return result


def solution(mesh):
    in_specs = (P("row", "col", None),) * 7 + (P("row", "col"),) * 2 + (P(),) * 7
    return jax.shard_map(
        shards, mesh=mesh, in_specs=in_specs, out_specs=P("row", "col"), check_vma=False
    )
```

time: 120 us -> 67.2 us (0.56)
  starting transfers between devices: 59.8 us -> 15.1 us
  Pallas kernels: 0 us -> 28.6 us
  other arithmetic: 17.1 us -> 0 us
  local copies, waits for them, and re-layouts: 19.9 us -> 9.42 us
  matrix products: 7.82 us -> 0 us
    ppermute x16 -> x4, starting transfers between devices: 59.8 us -> 15.1 us  [the longest x2 11.2 us: swap(): lax.ppermute(last, axis, [(i, i + 1) for i in range(count - 1)])]
    pallas_call x0 -> x4, Pallas kernels: none -> 28.6 us  [call(): pl.pallas_call(body, grid=(1,), in_specs=specs or [whole(a) for a in args...]
    dot_general x5 -> x0, matrix products: 7.82 us -> none  [back_conv(): result = jnp.dot(patches, arranged, preferred_element_type=jnp.float32)]
    reduce_sum x6 -> x0, other arithmetic: 5.45 us -> none  [the longest x2 2.42 us: inject(): jnp.mean(excess * scaled, axis=-1, keepdims=True)]
    slice x3 -> x0, other arithmetic: 3.28 us -> none  [extended(): lax.slice_in_dim(cells, cells.shape[dim] - width, cells.shape[dim], axis=...]
    another operation x7 -> x0, local copies, waits for them, and re-layouts: 3.27 us -> none  [the longest x2 3 us: unpool(): return jnp.stack(stripes, axis=1).reshape(2 * height, 2 * breadth, channels)]
    eq x4 -> x0, local copies, waits for them, and re-layouts: 2.77 us -> none  [unpool(): position == 2 * vertical + lateral]
    convert_element_type x1 -> x0, local copies, waits for them, and re-layouts: 2.49 us -> none  [shards(): result = unpool(pooled1, pool1_argmax).astype(jnp.bfloat16)]
  transfers between devices with their start and end apart: 16 -> 4, of which waited for: 4 -> 4; matrix products, arithmetic and copies ran while one was open for 15% -> 0% of each run, Pallas kernels for 0% -> 3%
where the time goes in v1:
time: 67.2 us; the launch traced here: 66.6 us
  Pallas kernels  28.6 us (43%)
  starting transfers between devices  15.1 us (22%)
  waiting for transfers between devices  13.3 us (20%)
  local copies, waits for them, and re-layouts  9.42 us (14%)
    pallas_call x4, Pallas kernels, call(): pl.pallas_call(body, grid=(1,), in_specs=specs or [whole(a) for a in args...  28.6 us
    ppermute x2, waiting for transfers between devices, swap(): lax.ppermute(first, axis, [(i + 1, i) for i in range(count - 1)])  12.8 us
    ppermute x2, starting transfers between devices, swap(): lax.ppermute(last, axis, [(i, i + 1) for i in range(count - 1)])  11.2 us
    unnamed x43, local copies, waits for them, and re-layouts  9.42 us
    ppermute x2, starting transfers between devices, swap(): lax.ppermute(first, axis, [(i + 1, i) for i in range(count - 1)])  3.84 us
  transfers between devices with their start and end apart: 4, of which 4 were waited for; matrix products, arithmetic and copies ran while one was open for 0% of the time, Pallas kernels for 3%

profile of v1, /device:TPU:223, one launch (start us, length us, event | category | flops | bytes accessed | tf_op | source)
XLA Modules:
  0.0 66.6 jit_solution(16883671842465718989)
XLA Ops:
  0.0 1.0 %copy-done = bf16[32,64,128]{2,1,0:T(8,128)(2,1)S(1)} copy-done((bf16[32,64,128]{2,1,0:T(8,128)(2,1)S(1)}, bf16[32,64,128]{2,1,0:T(8,128)(2,1)}, u32[]{:S(2)}) %copy-start) | copy-done | bytes 524312
  1.0 1.0 %copy-done.2 = bf16[32,64,128]{2,1,0:T(8,128)(2,1)S(1)} copy-done((bf16[32,64,128]{2,1,0:T(8,128)(2,1)S(1)}, bf16[32,64,128]{2,1,0:T(8,128)(2,1)}, u32[]{:S(2)}) %copy-start.2) | copy-done | bytes 524312
  2.1 1.0 %copy-done.4 = bf16[32,64,128]{2,1,0:T(8,128)(2,1)S(1)} copy-done((bf16[32,64,128]{2,1,0:T(8,128)(2,1)S(1)}, bf16[32,64,128]{2,1,0:T(8,128)(2,1)}, u32[]{:S(2)}) %copy-start.4) | copy-done | bytes 524312
  3.1 0.9 %copy-done.6 = bf16[16,32,256]{2,1,0:T(8,128)(2,1)S(1)} copy-done((bf16[16,32,256]{2,1,0:T(8,128)(2,1)S(1)}, bf16[16,32,256]{2,1,0:T(8,128)(2,1)}, u32[]{:S(2)}) %copy-start.6) | copy-done | bytes 262168
  4.1 0.9 %copy-done.7 = bf16[16,32,256]{2,1,0:T(8,128)(2,1)S(1)} copy-done((bf16[16,32,256]{2,1,0:T(8,128)(2,1)S(1)}, bf16[16,32,256]{2,1,0:T(8,128)(2,1)}, u32[]{:S(2)}) %copy-start.7) | copy-done | bytes 262168
  5.0 0.9 %copy-done.8 = bf16[16,32,256]{2,1,0:T(8,128)(2,1)S(1)} copy-done((bf16[16,32,256]{2,1,0:T(8,128)(2,1)S(1)}, bf16[16,32,256]{2,1,0:T(8,128)(2,1)}, u32[]{:S(2)}) %copy-start.8) | copy-done | bytes 262168
  6.0 0.9 %copy-done.10 = bf16[16,32,256]{2,1,0:T(8,128)(2,1)S(1)} copy-done((bf16[16,32,256]{2,1,0:T(8,128)(2,1)S(1)}, bf16[16,32,256]{2,1,0:T(8,128)(2,1)}, u32[]{:S(2)}) %copy-start.10) | copy-done | bytes 262168
  6.9 0.9 %copy-done.12 = s32[16,4096]{1,0:T(8,128)S(1)} copy-done((s32[16,4096]{1,0:T(8,128)S(1)}, s32[16,4096]{1,0:T(8,128)}, u32[]{:S(2)}) %copy-start.12) | copy-done | bytes 262168
  7.9 0.7 %copy-done.14 = f32[256]{0:T(256)S(1)} copy-done((f32[256]{0:T(256)S(1)}, f32[256]{0:T(256)}, u32[]{:S(2)}) %copy-start.14) | copy-done | bytes 1048
  8.6 0.7 copy-done.15
  9.2 0.7 %shard_map.154 = (bf16[16,32,256]{2,1,0:T(8,128)(2,1)S(1)}, bf16[928,128]{1,0:T(8,128)(2,1)S(1)}, bf16[928,128]{1,0:T(8,128)(2,1)S(1)}) custom-call(bf16[16,32,256]{2,1,0:T(8,128)(2,1)S(1)} %copy-done.6, bf16[16,32,256]{2,1,0:T(8,128)(2,1)S(1)} %copy-done.7, bf16[16,32,256]{2,1,0:T(8,128)(2,1)S(1)} %copy-done.8, bf16[16,32,256]{2,1,0:T(8,128)(2,1)S(1)} %copy-done.10, ...), custom_call_target="tpu_custom_call" | custom-call | flops 1000000000 | bytes 4000000 | tf_op jit(solution)/shard_map/pallas_call | solution.py:271
  9.9 4.3 %collective-permute-start = (bf16[928,128]{1,0:T(8,128)(2,1)S(1)}, bf16[928,128]{1,0:T(8,128)(2,1)S(1)}, u32[]{:S(2)}, u32[]{:S(2)}) collective-permute-start(bf16[928,128]{1,0:T(8,128)(2,1)S(1)} %get-tuple-element.14), channel_id=1, source_target_pairs={{0,16},{16,32},{32,48},{48,64},{64,80},{80,96},{96,112},{112,128},... | collective-permute-start | bytes 712712 | tf_op jit(solution)/shard_map/ppermute | solution.py:285
  14.3 1.9 %collective-permute-start.1 = (bf16[928,128]{1,0:T(8,128)(2,1)S(1)}, bf16[928,128]{1,0:T(8,128)(2,1)S(1)}, u32[]{:S(2)}, u32[]{:S(2)}) collective-permute-start(bf16[928,128]{1,0:T(8,128)(2,1)S(1)} %get-tuple-element.15), channel_id=1, source_target_pairs={{16,0},{32,16},{48,32},{64,48},{80,64},{96,80},{112,96},{128,112},... | collective-permute-start | bytes 712712 | tf_op jit(solution)/shard_map/ppermute | solution.py:286
  16.2 0.2 copy.17.k21
  16.4 0.0 copy-start.9
  16.4 2.0 %shard_map.155 = (f32[32,64,128]{2,1,0:T(8,128)S(1)}, bf16[128,1152]{1,0:T(8,128)(2,1)S(1)}) custom-call(bf16[32,64,128]{2,1,0:T(8,128)(2,1)S(1)} %copy-done.3, bf16[32,64,128]{2,1,0:T(8,128)(2,1)S(1)} %copy-done.1, f32[1,128]{1,0:T(1,128)S(1)} %bitcast.4, bf16[128,576]{1,0:T(8,128)(2,1)S(1)} %copy.17.k21), custom_call_target="tpu_custom_call" | custom-call | flops 1000000000 | bytes 4000000 | tf_op jit(solution)/shard_map/pallas_call | solution.py:271
  18.5 0.2 collective-permute-done.above
  18.7 7.2 %collective-permute-done.1.below = bf16[928,128]{1,0:T(8,128)(2,1)S(1)} collective-permute-done((bf16[928,128]{1,0:T(8,128)(2,1)S(1)}, bf16[928,128]{1,0:T(8,128)(2,1)S(1)}, u32[]{:S(2)}, u32[]{:S(2)}) %collective-permute-start.1) | collective-permute-done | bytes 237600 | tf_op jit(solution)/shard_map/ppermute | solution.py:286
  25.9 0.5 shard_map.156
  26.4 6.9 %collective-permute-start.2 = (bf16[656,128]{1,0:T(8,128)(2,1)S(1)}, bf16[656,128]{1,0:T(8,128)(2,1)S(1)}, u32[]{:S(2)}, u32[]{:S(2)}) collective-permute-start(bf16[656,128]{1,0:T(8,128)(2,1)S(1)} %get-tuple-element.16), channel_id=1, source_target_pairs={{0,1},{1,2},{2,3},{3,4},{4,5},{5,6},{6,7},{7,8},{8,9},{9,10},{10,1... | collective-permute-start | bytes 503816 | tf_op jit(solution)/shard_map/ppermute | solution.py:285
  33.3 1.9 %collective-permute-start.3 = (bf16[656,128]{1,0:T(8,128)(2,1)S(1)}, bf16[656,128]{1,0:T(8,128)(2,1)S(1)}, u32[]{:S(2)}, u32[]{:S(2)}) collective-permute-start(bf16[656,128]{1,0:T(8,128)(2,1)S(1)} %get-tuple-element.17), channel_id=1, source_target_pairs={{1,0},{2,1},{3,2},{4,3},{5,4},{6,5},{7,6},{8,7},{9,8},{10,9},{11,1... | collective-permute-start | bytes 503816 | tf_op jit(solution)/shard_map/ppermute | solution.py:286
  35.2 0.4 collective-permute-done.2.fl
  35.6 5.6 %collective-permute-done.3.fr = bf16[656,128]{1,0:T(8,128)(2,1)S(1)} collective-permute-done((bf16[656,128]{1,0:T(8,128)(2,1)S(1)}, bf16[656,128]{1,0:T(8,128)(2,1)S(1)}, u32[]{:S(2)}, u32[]{:S(2)}) %collective-permute-start.3) | collective-permute-done | bytes 167968 | tf_op jit(solution)/shard_map/ppermute | solution.py:286
  41.2 25.4 %shard_map.157 = bf16[64,8192]{1,0:T(8,128)(2,1)} custom-call(bf16[16,32,256]{2,1,0:T(8,128)(2,1)S(1)} %get-tuple-element.12.seeds, bf16[16,32,256]{2,1,0:T(8,128)(2,1)S(1)} %copy-done.9, bf16[16,32,256]{2,1,0:T(8,128)(2,1)S(1)} %copy-done.11, bf16[32,64,128]{2,1,0:T(8,128)(2,1)S(1)} %copy-done.3, f32[32,64,128]{2,1,0:T(8,128)} %copy-done.19, ...), custom_call_target="tpu_custom_call" | custom-call | flops 3000000000 | bytes 4000000 | tf_op jit(solution)/shard_map/pallas_call | solution.py:271
  (31 shorter events, 0.1 us)
Async XLA Ops:
  0.0 1.0 %copy-start = (bf16[32,64,128]{2,1,0:T(8,128)(2,1)S(1)}, bf16[32,64,128]{2,1,0:T(8,128)(2,1)}, u32[]{:S(2)}) copy-start(bf16[32,64,128]{2,1,0:T(8,128)(2,1)} %t22.1) | copy-start | bytes 1572868
  1.0 1.0 %copy-start.2 = (bf16[32,64,128]{2,1,0:T(8,128)(2,1)S(1)}, bf16[32,64,128]{2,1,0:T(8,128)(2,1)}, u32[]{:S(2)}) copy-start(bf16[32,64,128]{2,1,0:T(8,128)(2,1)} %m22.5) | copy-start | bytes 1572868
  2.1 1.0 %copy-start.4 = (bf16[32,64,128]{2,1,0:T(8,128)(2,1)S(1)}, bf16[32,64,128]{2,1,0:T(8,128)(2,1)}, u32[]{:S(2)}) copy-start(bf16[32,64,128]{2,1,0:T(8,128)(2,1)} %m21.3) | copy-start | bytes 1572868
  3.1 0.9 %copy-start.6 = (bf16[16,32,256]{2,1,0:T(8,128)(2,1)S(1)}, bf16[16,32,256]{2,1,0:T(8,128)(2,1)}, u32[]{:S(2)}) copy-start(bf16[16,32,256]{2,1,0:T(8,128)(2,1)} %m33.1) | copy-start | bytes 786436
  4.1 0.9 %copy-start.7 = (bf16[16,32,256]{2,1,0:T(8,128)(2,1)S(1)}, bf16[16,32,256]{2,1,0:T(8,128)(2,1)}, u32[]{:S(2)}) copy-start(bf16[16,32,256]{2,1,0:T(8,128)(2,1)} %t33.1) | copy-start | bytes 786436
  5.0 0.9 %copy-start.8 = (bf16[16,32,256]{2,1,0:T(8,128)(2,1)S(1)}, bf16[16,32,256]{2,1,0:T(8,128)(2,1)}, u32[]{:S(2)}) copy-start(bf16[16,32,256]{2,1,0:T(8,128)(2,1)} %m32.5) | copy-start | bytes 786436
  6.0 0.9 %copy-start.10 = (bf16[16,32,256]{2,1,0:T(8,128)(2,1)S(1)}, bf16[16,32,256]{2,1,0:T(8,128)(2,1)}, u32[]{:S(2)}) copy-start(bf16[16,32,256]{2,1,0:T(8,128)(2,1)} %m31.5) | copy-start | bytes 786436
  6.9 0.9 %copy-start.12 = (s32[16,4096]{1,0:T(8,128)S(1)}, s32[16,4096]{1,0:T(8,128)}, u32[]{:S(2)}) copy-start(s32[16,4096]{1,0:T(8,128)} %a2.5) | copy-start | bytes 786436
  7.9 0.7 %copy-start.14 = (f32[256]{0:T(256)S(1)}, f32[256]{0:T(256)}, u32[]{:S(2)}) copy-start(f32[256]{0:T(256)} %param.26) | copy-start | bytes 3076
  9.2 7.0 %copy-start.20 = (bf16[128,576]{0,1:T(8,128)(2,1)S(1)}, bf16[128,576]{0,1:T(8,128)(2,1)}, u32[]{:S(2)}) copy-start(bf16[128,576]{0,1:T(8,128)(2,1)} %param.27) | copy-start | bytes 442372
  9.2 7.1 %copy-start.1 = (bf16[32,64,128]{2,1,0:T(8,128)(2,1)S(1)}, bf16[32,64,128]{2,1,0:T(8,128)(2,1)}, u32[]{:S(2)}) copy-start(bf16[32,64,128]{2,1,0:T(8,128)(2,1)} %t22.1) | copy-start | bytes 1572868
  9.2 7.2 %copy-start.3 = (bf16[32,64,128]{2,1,0:T(8,128)(2,1)S(1)}, bf16[32,64,128]{2,1,0:T(8,128)(2,1)}, u32[]{:S(2)}) copy-start(bf16[32,64,128]{2,1,0:T(8,128)(2,1)} %m22.5) | copy-start | bytes 1572868
  9.2 7.2 %copy-start.16 = (f32[128]{0:T(128)S(1)}, f32[128]{0:T(128)}, u32[]{:S(2)}) copy-start(f32[128]{0:T(128)} %param.25) | copy-start | bytes 1540
  9.9 8.8 %collective-permute-start = (bf16[928,128]{1,0:T(8,128)(2,1)S(1)}, bf16[928,128]{1,0:T(8,128)(2,1)S(1)}, u32[]{:S(2)}, u32[]{:S(2)}) collective-permute-start(bf16[928,128]{1,0:T(8,128)(2,1)S(1)} %get-tuple-element.14), channel_id=1, source_target_pairs={{0,16},{16,32},{32,48},{48,64},{64,80},{80,96},{96,112},{112,128},... | collective-permute-start | bytes 712712 | tf_op jit(solution)/shard_map/ppermute | solution.py:285
  14.3 11.6 %collective-permute-start.1 = (bf16[928,128]{1,0:T(8,128)(2,1)S(1)}, bf16[928,128]{1,0:T(8,128)(2,1)S(1)}, u32[]{:S(2)}, u32[]{:S(2)}) collective-permute-start(bf16[928,128]{1,0:T(8,128)(2,1)S(1)} %get-tuple-element.15), channel_id=1, source_target_pairs={{16,0},{32,16},{48,32},{64,48},{80,64},{96,80},{112,96},{128,112},... | collective-permute-start | bytes 712712 | tf_op jit(solution)/shard_map/ppermute | solution.py:286
  16.4 9.5 %copy-start.5 = (bf16[32,64,128]{2,1,0:T(8,128)(2,1)S(1)}, bf16[32,64,128]{2,1,0:T(8,128)(2,1)}, u32[]{:S(2)}) copy-start(bf16[32,64,128]{2,1,0:T(8,128)(2,1)} %m21.3) | copy-start | bytes 1572868
  16.4 9.5 %copy-start.9 = (bf16[16,32,256]{2,1,0:T(8,128)(2,1)S(1)}, bf16[16,32,256]{2,1,0:T(8,128)(2,1)}, u32[]{:S(2)}) copy-start(bf16[16,32,256]{2,1,0:T(8,128)(2,1)} %m32.5) | copy-start | bytes 786436
  16.4 9.4 %copy-start.11 = (bf16[16,32,256]{2,1,0:T(8,128)(2,1)S(1)}, bf16[16,32,256]{2,1,0:T(8,128)(2,1)}, u32[]{:S(2)}) copy-start(bf16[16,32,256]{2,1,0:T(8,128)(2,1)} %m31.5) | copy-start | bytes 786436
  16.4 9.4 %copy-start.13 = (s32[16,4096]{1,0:T(8,128)S(1)}, s32[16,4096]{1,0:T(8,128)}, u32[]{:S(2)}) copy-start(s32[16,4096]{1,0:T(8,128)} %a2.5) | copy-start | bytes 786436
  18.5 7.9 %copy-start.19 = (f32[32,64,128]{2,1,0:T(8,128)}, f32[32,64,128]{2,1,0:T(8,128)S(1)}, u32[]{:S(2)}) copy-start(f32[32,64,128]{2,1,0:T(8,128)S(1)} %get-tuple-element.13.i22) | copy-start | bytes 3145732
  25.9 15.3 %copy-start.17 = (s32[32,4096]{1,0:T(8,128)S(1)}, s32[32,4096]{1,0:T(8,128)}, u32[]{:S(2)}) copy-start(s32[32,4096]{1,0:T(8,128)} %a1.1) | copy-start | bytes 1572868
  25.9 15.3 %copy-start.18 = (bf16[128,1152]{1,0:T(8,128)(2,1)S(1)}, bf16[128,1152]{1,0:T(8,128)(2,1)}, u32[]{:S(2)}) copy-start(bf16[128,1152]{1,0:T(8,128)(2,1)} %k22.1) | copy-start | bytes 884740
  26.4 9.2 %collective-permute-start.2 = (bf16[656,128]{1,0:T(8,128)(2,1)S(1)}, bf16[656,128]{1,0:T(8,128)(2,1)S(1)}, u32[]{:S(2)}, u32[]{:S(2)}) collective-permute-start(bf16[656,128]{1,0:T(8,128)(2,1)S(1)} %get-tuple-element.16), channel_id=1, source_target_pairs={{0,1},{1,2},{2,3},{3,4},{4,5},{5,6},{6,7},{7,8},{8,9},{9,10},{10,1... | collective-permute-start | bytes 503816 | tf_op jit(solution)/shard_map/ppermute | solution.py:285
  33.3 7.9 %collective-permute-start.3 = (bf16[656,128]{1,0:T(8,128)(2,1)S(1)}, bf16[656,128]{1,0:T(8,128)(2,1)S(1)}, u32[]{:S(2)}, u32[]{:S(2)}) collective-permute-start(bf16[656,128]{1,0:T(8,128)(2,1)S(1)} %get-tuple-element.17), channel_id=1, source_target_pairs={{1,0},{2,1},{3,2},{4,3},{5,4},{6,5},{7,6},{8,7},{9,8},{10,9},{11,1... | collective-permute-start | bytes 503816 | tf_op jit(solution)/shard_map/ppermute | solution.py:286
  (1 other events, 0.7 us)

commit v2 on v1

--- a/solution.py
+++ b/solution.py
@@ -18,6 +18,8 @@
 WU = 96
 WP = 88
 LEAD = 8
+N33, N32, N31, N22, N21 = 11, 10, 9, 17, 16
+LIM = (8, 8, 8, 30)
 
 
 def inject(preact, target, weight):
@@ -32,20 +34,36 @@
     return (excess - scaled * mean) * scale
 
 
-def pack_rows(m33, t33, m32, m31, m22t, m22b, t22t, t22b, m21t, m21b, a2, w2, w3, seeds, up, down):
+def pack_rows(hm33, ht33, hm32, hm31, hm22, ht22, hm21, ha2, hw2, hw3, seeds, up, down,
+              m33, t33, m32, m31, m22e, t22e, m21e, a2, w2, w3, sems):
     rows, cols, ch = m33.shape
+    tall = hm22.shape[0]
+    moves = []
+    for source, target in (
+        (hm33.at[0:8], m33.at[0:8]), (ht33.at[0:8], t33.at[0:8]),
+        (hm33.at[8:rows], m33.at[8:rows]), (ht33.at[8:rows], t33.at[8:rows]),
+        (hm22.at[0:2], m22e.at[0]), (hm22.at[tall - 2 : tall], m22e.at[1]),
+        (ht22.at[0:2], t22e.at[0]), (ht22.at[tall - 2 : tall], t22e.at[1]),
+        (hm32.at[0:3], m32.at[0:3]), (hm32.at[rows - 3 : rows], m32.at[3:6]),
+        (hm31.at[0:2], m31.at[0:2]), (hm31.at[rows - 2 : rows], m31.at[2:4]),
+        (hm21.at[0], m21e.at[0]), (hm21.at[tall - 1], m21e.at[1]),
+        (ha2, a2), (hw2, w2), (hw3, w3),
+    ):
+        moves.append(pltpu.make_async_copy(source, target, sems.at[len(moves)]))
+        moves[-1].start()
+    for move in moves:
+        move.wait()
     step = 4
     for r in range(0, rows, step):
         p = m33[r : r + step].reshape(step * cols, ch)
         value = inject(p, t33[r : r + step].reshape(step * cols, ch), w3[...])
         value = jnp.where(p.astype(F32) > 0, value, 0.0).astype(BF16)
         seeds[r : r + step] = value.reshape(step, cols, ch)
-    for out, first, m22, t22, m21, edge in (
-        (up, 0, m22t, t22t, m21t, 0),
-        (down, 1, m22b, t22b, m21b, rows - 1),
-    ):
-        for source, base, width in ((seeds, ROW_SEED, 4), (m32, ROW_M32, 3), (m31, ROW_M31, 2)):
-            begin = rows - width if first else 0
+    for out, side, edge in ((up, 0, 0), (down, 1, rows - 1)):
+        m22, t22 = m22e.at[side], t22e.at[side]
+        for source, base, width, begin in (
+            (seeds, ROW_SEED, 4, side * (rows - 4)), (m32, ROW_M32, 3, side * 3), (m31, ROW_M31, 2, side * 2),
+        ):
             for k in range(width):
                 for h in range(2):
                     at = base + (k * 2 + h) * cols
@@ -56,7 +74,7 @@
         out[ROW_I22 : ROW_I22 + 2 * wide] = inject(
             p, t22[...].reshape(2 * wide, 128), w2[...]
         ).astype(BF16)
-        out[ROW_M21 : ROW_M21 + wide] = m21[0]
+        out[ROW_M21 : ROW_M21 + wide] = m21e[side]
         line = a2[edge : edge + 1, :].astype(F32)
         line = jnp.concatenate([line[:, c * 128 : (c + 1) * 128] for c in range(cols)], axis=0)
         out[ROW_A2 : ROW_A2 + cols] = line.astype(BF16)
@@ -72,10 +90,10 @@
         value = inject(m22[at].reshape(step * cols, ch), t22[at].reshape(step * cols, ch), w2[...])
         i22[at] = value.reshape(step, cols, ch)
 
-    half = k21.shape[1] // 9
+    half = k21.shape[0] // 9
     for t in range(9):
-        tap = k21[:, t * half : (t + 1) * half].astype(F32)
-        k21d[:, t * 128 : (t + 1) * 128] = jnp.concatenate([tap, tap], axis=1).astype(BF16)
+        tap = k21[t * half : (t + 1) * half].astype(F32)
+        k21d[:, t * 128 : (t + 1) * 128] = jnp.concatenate([tap, tap], axis=0).T.astype(BF16)
 
 
 def pack_cols(seeds, m32, m31, m22, i22, m21, a2, above, below, left, right, s256, s128, line, sa, flat):
@@ -197,7 +215,7 @@
         for h in range(2):
             x33[r, :, h * 128 : (h + 1) * 128] = e33[h, at].astype(BF16)
 
-    for x, kernel, stage, nxt, count in ((x33, k33, e32, x32, 2), (x32, k32, e31, x31, 2)):
+    for x, kernel, stage, nxt, count in ((x33, k33, e32, x32, N33), (x32, k32, e31, x31, N32)):
 
         @pl.loop(0, nxt.shape[0] // count)
         def _(i):
@@ -210,11 +228,11 @@
                     count, W3, 128
                 )
 
-    @pl.loop(0, (rows + 2) // 3)
+    @pl.loop(0, (rows + 2) // N31)
     def _(i):
-        row = i * 3
-        value = conv(x31, k31, row, 3)
-        for k in range(3):
+        row = i * N31
+        value = conv(x31, k31, row, N31)
+        for k in range(N31):
             part = value[k * W3 : (k + 1) * W3]
             where = ea[pl.ds(pl.multiple_of((row + k) * W3, W3), W3)]
             for a in range(2):
@@ -228,18 +246,18 @@
         arriving = u2[pl.ds(pl.multiple_of(r * WU + LEAD, 8), W2)] + ei[at]
         g22[r] = jnp.where(e22[at] > 0, arriving, 0.0).astype(BF16)
 
-    @pl.loop(0, (tall + 2) // 2)
+    @pl.loop(0, (tall + 2) // N22)
     def _(i):
-        row = i * 2
-        value = conv(g22, k22, row, 2)
-        value = jnp.where(e21[pl.ds(pl.multiple_of(row * W2, W2), 2 * W2)] > 0, value, 0.0)
-        g21[pl.ds(row, 2)] = value.astype(BF16).reshape(2, W2, 128)
-
-    @pl.loop(0, tall // 2)
+        row = i * N22
+        value = conv(g22, k22, row, N22)
+        value = jnp.where(e21[pl.ds(pl.multiple_of(row * W2, W2), N22 * W2)] > 0, value, 0.0)
+        g21[pl.ds(row, N22)] = value.astype(BF16).reshape(N22, W2, 128)
+
+    @pl.loop(0, tall // N21)
     def _(i):
-        row = i * 2
-        value = conv(g21, k21d, row, 2)
-        for k in range(2):
+        row = i * N21
+        value = conv(g21, k21d, row, N21)
+        for k in range(N21):
             to = pl.multiple_of((row + k) * WP, 8)
             p1[pl.ds(to, W2)] = value[k * W2 : (k + 1) * W2]
 
@@ -266,7 +284,7 @@
     return pl.BlockSpec(array.shape, lambda i: zeros)
 
 
-def call(body, args, outs, scratch=(), specs=None, cost=0):
+def call(body, args, outs, scratch=(), specs=None, cost=0, limit=8):
     shapes = [jax.ShapeDtypeStruct(s, d) for s, d in outs]
     return pl.pallas_call(
         body,
@@ -274,9 +292,9 @@
         in_specs=specs or [whole(a) for a in args],
         out_specs=[whole(s) for s in shapes],
         out_shape=shapes,
-        scratch_shapes=[pltpu.VMEM(s, d) for s, d in scratch],
+        scratch_shapes=[pltpu.VMEM(*s) if isinstance(s, tuple) else s for s in scratch],
         cost_estimate=pl.CostEstimate(flops=cost, bytes_accessed=4000000, transcendentals=0),
-        compiler_params=pltpu.CompilerParams(vmem_limit_bytes=50 << 20),
+        compiler_params=pltpu.CompilerParams(vmem_limit_bytes=limit << 20),
     )(*args)
 
 
@@ -293,30 +311,30 @@
     w2 = w2.reshape(1, ch2)
     w3 = w3.reshape(1, ch3)
 
-    def band(height, index):
-        return pl.BlockSpec((height, wide, ch2), lambda i: (index, 0, 0))
-
-    args = (m33, t33, m32, m31, m22, m22, t22, t22, m21, m21, a2, w2, w3)
-    specs = [whole(a) for a in args]
-    specs[4], specs[5] = band(2, 0), band(2, tall // 2 - 1)
-    specs[6], specs[7] = band(2, 0), band(2, tall // 2 - 1)
-    specs[8], specs[9] = band(1, 0), band(1, tall - 1)
+    stored = pl.BlockSpec(memory_space=pltpu.MemorySpace.HBM)
+    args = tuple(pltpu.with_memory_space_constraint(x, pltpu.MemorySpace.HBM) for x in (m33, t33, m32, m31, m22, t22, m21, a2, w2, w3))
     seeds, up, down = call(
         pack_rows, args,
         [((rows, cols, ch3), BF16), ((ROW_TOTAL, 128), BF16), ((ROW_TOTAL, 128), BF16)],
-        specs=specs, cost=10**9,
+        scratch=[
+            ((rows, cols, ch3), BF16), ((rows, cols, ch3), BF16), ((6, cols, ch3), BF16),
+            ((4, cols, ch3), BF16), ((2, 2, wide, ch2), BF16), ((2, 2, wide, ch2), BF16),
+            ((2, wide, ch2), BF16), (a2.shape, a2.dtype), (w2.shape, F32), (w3.shape, F32),
+            pltpu.SemaphoreType.DMA((17,)),
+        ],
+        specs=[stored] * 10, cost=10**9, limit=LIM[0],
     )
     above, below = swap(up, down, "row")
     i22, k21d = call(
-        own_inject, (m22, t22, w2, k21),
-        [((tall, wide, ch2), F32), ((k21.shape[0], 9 * 128), BF16)], cost=10**9,
+        own_inject, (m22, t22, w2, k21.T),
+        [((tall, wide, ch2), F32), ((k21.shape[0], 9 * 128), BF16)], cost=10**9, limit=LIM[1],
     )
     left, right = call(
         pack_cols, (seeds, m32, m31, m22, i22, m21, a2, above, below),
         [((COL_TOTAL, 128), BF16), ((COL_TOTAL, 128), BF16)],
         scratch=[((24 * 16, 128), F32), ((40 * 16, 128), F32), ((cols, 128), F32), ((8, 128), F32),
                  ((COL_TOTAL, 128), F32)],
-        cost=10**9,
+        cost=10**9, limit=LIM[2],
     )
     fl, fr = swap(left, right, "col")
     area3, area2 = (rows + 8) * W3, (tall + 8) * W2
@@ -331,7 +349,7 @@
             (((tall + 4) * WU, 128), F32), ((tall + 4, W2, ch2), BF16), ((tall + 2, W2, ch2), BF16),
             ((tall * WP, 128), F32), ((2, 2 * tall, 128), F32),
         ],
-        cost=3 * 10**9,
+        cost=3 * 10**9, limit=LIM[3],
     )
     return result
 

time: 67.2 us -> 48.4 us (0.72)
  Pallas kernels: 28.6 us -> 19.2 us
  local copies, waits for them, and re-layouts: 9.42 us -> 0.07 us
    pallas_call x4, Pallas kernels: 28.6 us -> 19.2 us  [call(): pl.pallas_call(body, grid=(1,), in_specs=specs or [whole(a) for a in args...]
    unnamed x43 -> x26, local copies, waits for them, and re-layouts: 9.42 us -> 0.07 us
  transfers between devices with their start and end apart: 4 -> 4, of which waited for: 4 -> 4; matrix products, arithmetic and copies ran while one was open for 0% -> 0% of each run, Pallas kernels for 3% -> 4%
where the time goes in v2:
time: 48.4 us; the launch traced here: 48.2 us
  Pallas kernels  19.2 us (40%)
  starting transfers between devices  15.2 us (31%)
  waiting for transfers between devices  13.5 us (28%)
    pallas_call x4, Pallas kernels, call(): pl.pallas_call(body, grid=(1,), in_specs=specs or [whole(a) for a in args...  19.2 us
    ppermute x2, waiting for transfers between devices, swap(): lax.ppermute(first, axis, [(i + 1, i) for i in range(count - 1)])  12.8 us
    ppermute x2, starting transfers between devices, swap(): lax.ppermute(last, axis, [(i, i + 1) for i in range(count - 1)])  11.4 us
    ppermute x2, starting transfers between devices, swap(): lax.ppermute(first, axis, [(i + 1, i) for i in range(count - 1)])  3.84 us
  transfers between devices with their start and end apart: 4, of which 4 were waited for; matrix products, arithmetic and copies ran while one was open for 0% of the time, Pallas kernels for 4%

profile of v2, /device:TPU:223, one launch (start us, length us, event | category | flops | bytes accessed | tf_op | source)
XLA Modules:
  0.0 48.2 jit_solution(17479675302704779064)
XLA Ops:
  0.0 2.3 %shard_map.154 = (bf16[16,32,256]{2,1,0:T(8,128)(2,1)S(1)}, bf16[928,128]{1,0:T(8,128)(2,1)S(1)}, bf16[928,128]{1,0:T(8,128)(2,1)S(1)}) custom-call(bf16[16,32,256]{2,1,0:T(8,128)(2,1)} %hm33.1, bf16[16,32,256]{2,1,0:T(8,128)(2,1)} %ht33.1, bf16[16,32,256]{2,1,0:T(8,128)(2,1)} %m32.3, bf16[16,32,256]{2,1,0:T(8,128)(2,1)} %m31.3, bf16[32,64,128]{2,1,0:T(8,128)(2,1)} %m22.5, ...), custom_call_target="tpu_custom_call" | custom-call | flops 1000000000 | bytes 4000000 | tf_op jit(solution)/shard_map/pallas_call | solution.py:289
  2.3 4.3 %collective-permute-start = (bf16[928,128]{1,0:T(8,128)(2,1)S(1)}, bf16[928,128]{1,0:T(8,128)(2,1)S(1)}, u32[]{:S(2)}, u32[]{:S(2)}) collective-permute-start(bf16[928,128]{1,0:T(8,128)(2,1)S(1)} %get-tuple-element.14), channel_id=1, source_target_pairs={{0,16},{16,32},{32,48},{48,64},{64,80},{80,96},{96,112},{112,128},... | collective-permute-start | bytes 712712 | tf_op jit(solution)/shard_map/ppermute | solution.py:303
  6.6 1.9 %collective-permute-start.1 = (bf16[928,128]{1,0:T(8,128)(2,1)S(1)}, bf16[928,128]{1,0:T(8,128)(2,1)S(1)}, u32[]{:S(2)}, u32[]{:S(2)}) collective-permute-start(bf16[928,128]{1,0:T(8,128)(2,1)S(1)} %get-tuple-element.15), channel_id=1, source_target_pairs={{16,0},{32,16},{48,32},{64,48},{80,64},{96,80},{112,96},{128,112},... | collective-permute-start | bytes 712712 | tf_op jit(solution)/shard_map/ppermute | solution.py:304
  8.6 0.0 copy-start.5
  8.6 0.0 copy-start.8
  8.6 0.0 copy-start.9
  8.6 0.0 copy-start.10
  8.7 0.0 copy-start.7
  8.7 2.1 %shard_map.155 = (f32[32,64,128]{2,1,0:T(8,128)S(1)}, bf16[128,1152]{1,0:T(8,128)(2,1)S(1)}) custom-call(bf16[32,64,128]{2,1,0:T(8,128)(2,1)S(1)} %copy-done.4, bf16[32,64,128]{2,1,0:T(8,128)(2,1)S(1)} %copy-done.3, f32[1,128]{1,0:T(1,128)S(1)} %bitcast.5, bf16[576,128]{1,0:T(8,128)(2,1)S(1)} %bitcast.3), custom_call_target="tpu_custom_call" | custom-call | flops 1000000000 | bytes 4000000 | tf_op jit(solution)/shard_map/pallas_call | solution.py:289
  10.7 0.3 collective-permute-done.above
  11.1 7.2 %collective-permute-done.1.below = bf16[928,128]{1,0:T(8,128)(2,1)S(1)} collective-permute-done((bf16[928,128]{1,0:T(8,128)(2,1)S(1)}, bf16[928,128]{1,0:T(8,128)(2,1)S(1)}, u32[]{:S(2)}, u32[]{:S(2)}) %collective-permute-start.1) | collective-permute-done | bytes 237600 | tf_op jit(solution)/shard_map/ppermute | solution.py:304
  18.2 0.0 copy-done.10
  18.3 0.0 copy-start
  18.3 0.0 copy-start.1
  18.3 0.0 copy-start.2
  18.3 0.0 copy-start.6
  18.3 0.5 shard_map.156
  18.8 7.0 %collective-permute-start.2 = (bf16[656,128]{1,0:T(8,128)(2,1)S(1)}, bf16[656,128]{1,0:T(8,128)(2,1)S(1)}, u32[]{:S(2)}, u32[]{:S(2)}) collective-permute-start(bf16[656,128]{1,0:T(8,128)(2,1)S(1)} %get-tuple-element.16), channel_id=1, source_target_pairs={{0,1},{1,2},{2,3},{3,4},{4,5},{5,6},{6,7},{7,8},{8,9},{9,10},{10,1... | collective-permute-start | bytes 503816 | tf_op jit(solution)/shard_map/ppermute | solution.py:303
  25.8 1.9 %collective-permute-start.3 = (bf16[656,128]{1,0:T(8,128)(2,1)S(1)}, bf16[656,128]{1,0:T(8,128)(2,1)S(1)}, u32[]{:S(2)}, u32[]{:S(2)}) collective-permute-start(bf16[656,128]{1,0:T(8,128)(2,1)S(1)} %get-tuple-element.17), channel_id=1, source_target_pairs={{1,0},{2,1},{3,2},{4,3},{5,4},{6,5},{7,6},{8,7},{9,8},{10,9},{11,1... | collective-permute-start | bytes 503816 | tf_op jit(solution)/shard_map/ppermute | solution.py:304
  27.7 0.4 collective-permute-done.2.fl
  28.1 5.6 %collective-permute-done.3.fr = bf16[656,128]{1,0:T(8,128)(2,1)S(1)} collective-permute-done((bf16[656,128]{1,0:T(8,128)(2,1)S(1)}, bf16[656,128]{1,0:T(8,128)(2,1)S(1)}, u32[]{:S(2)}, u32[]{:S(2)}) %collective-permute-start.3) | collective-permute-done | bytes 167968 | tf_op jit(solution)/shard_map/ppermute | solution.py:304
  33.7 0.0 copy-done.1
  33.7 0.0 copy-done.2
  33.7 14.4 %shard_map.157 = bf16[64,8192]{1,0:T(8,128)(2,1)} custom-call(bf16[16,32,256]{2,1,0:T(8,128)(2,1)S(1)} %get-tuple-element.12.seeds, bf16[16,32,256]{2,1,0:T(8,128)(2,1)S(1)} %copy-done.8, bf16[16,32,256]{2,1,0:T(8,128)(2,1)S(1)} %copy-done.9, bf16[32,64,128]{2,1,0:T(8,128)(2,1)S(1)} %copy-done.4, f32[32,64,128]{2,1,0:T(8,128)S(1)} %get-tuple-element.13.i22, ...), custom_call_target="tpu_custom_call" | custom-call | flops 3000000000 | bytes 4000000 | tf_op jit(solution)/shard_map/pallas_call | solution.py:289
  (14 shorter events, 0.0 us)
Async XLA Ops:
  0.0 8.6 %copy-start.3 = (bf16[32,64,128]{2,1,0:T(8,128)(2,1)S(1)}, bf16[32,64,128]{2,1,0:T(8,128)(2,1)}, u32[]{:S(2)}) copy-start(bf16[32,64,128]{2,1,0:T(8,128)(2,1)} %t22.1) | copy-start | bytes 1572868
  0.0 8.6 %copy-start.4 = (bf16[32,64,128]{2,1,0:T(8,128)(2,1)S(1)}, bf16[32,64,128]{2,1,0:T(8,128)(2,1)}, u32[]{:S(2)}) copy-start(bf16[32,64,128]{2,1,0:T(8,128)(2,1)} %m22.5) | copy-start | bytes 1572868
  0.0 8.6 %copy-start.11 = (bf16[128,576]{0,1:T(8,128)(2,1)S(1)}, bf16[128,576]{0,1:T(8,128)(2,1)}, u32[]{:S(2)}) copy-start(bf16[128,576]{0,1:T(8,128)(2,1)} %param.27) | copy-start | bytes 442372
  0.0 8.6 %copy-start.12 = (f32[128]{0:T(128)S(1)}, f32[128]{0:T(128)}, u32[]{:S(2)}) copy-start(f32[128]{0:T(128)} %param.25) | copy-start | bytes 1540
  2.3 8.8 %collective-permute-start = (bf16[928,128]{1,0:T(8,128)(2,1)S(1)}, bf16[928,128]{1,0:T(8,128)(2,1)S(1)}, u32[]{:S(2)}, u32[]{:S(2)}) collective-permute-start(bf16[928,128]{1,0:T(8,128)(2,1)S(1)} %get-tuple-element.14), channel_id=1, source_target_pairs={{0,16},{16,32},{32,48},{48,64},{64,80},{80,96},{96,112},{112,128},... | collective-permute-start | bytes 712712 | tf_op jit(solution)/shard_map/ppermute | solution.py:303
  6.6 11.6 %collective-permute-start.1 = (bf16[928,128]{1,0:T(8,128)(2,1)S(1)}, bf16[928,128]{1,0:T(8,128)(2,1)S(1)}, u32[]{:S(2)}, u32[]{:S(2)}) collective-permute-start(bf16[928,128]{1,0:T(8,128)(2,1)S(1)} %get-tuple-element.15), channel_id=1, source_target_pairs={{16,0},{32,16},{48,32},{64,48},{80,64},{96,80},{112,96},{128,112},... | collective-permute-start | bytes 712712 | tf_op jit(solution)/shard_map/ppermute | solution.py:304
  8.6 9.6 %copy-start.5 = (bf16[32,64,128]{2,1,0:T(8,128)(2,1)S(1)}, bf16[32,64,128]{2,1,0:T(8,128)(2,1)}, u32[]{:S(2)}) copy-start(bf16[32,64,128]{2,1,0:T(8,128)(2,1)} %m21.3) | copy-start | bytes 1572868
  8.6 9.6 %copy-start.8 = (bf16[16,32,256]{2,1,0:T(8,128)(2,1)S(1)}, bf16[16,32,256]{2,1,0:T(8,128)(2,1)}, u32[]{:S(2)}) copy-start(bf16[16,32,256]{2,1,0:T(8,128)(2,1)} %m32.3) | copy-start | bytes 786436
  8.6 9.6 %copy-start.9 = (bf16[16,32,256]{2,1,0:T(8,128)(2,1)S(1)}, bf16[16,32,256]{2,1,0:T(8,128)(2,1)}, u32[]{:S(2)}) copy-start(bf16[16,32,256]{2,1,0:T(8,128)(2,1)} %m31.3) | copy-start | bytes 786436
  8.6 9.6 %copy-start.10 = (s32[16,4096]{1,0:T(8,128)S(1)}, s32[16,4096]{1,0:T(8,128)}, u32[]{:S(2)}) copy-start(s32[16,4096]{1,0:T(8,128)} %a2.3) | copy-start | bytes 786436
  8.7 25.1 %copy-start.7 = (bf16[128,1152]{1,0:T(8,128)(2,1)S(1)}, bf16[128,1152]{1,0:T(8,128)(2,1)}, u32[]{:S(2)}) copy-start(bf16[128,1152]{1,0:T(8,128)(2,1)} %k22.1) | copy-start | bytes 884740
  18.3 15.5 %copy-start = (bf16[256,2304]{1,0:T(8,128)(2,1)S(1)}, bf16[256,2304]{1,0:T(8,128)(2,1)}, u32[]{:S(2)}) copy-start(bf16[256,2304]{1,0:T(8,128)(2,1)} %k33.1) | copy-start | bytes 3538948
  18.3 15.5 %copy-start.1 = (bf16[256,2304]{1,0:T(8,128)(2,1)S(1)}, bf16[256,2304]{1,0:T(8,128)(2,1)}, u32[]{:S(2)}) copy-start(bf16[256,2304]{1,0:T(8,128)(2,1)} %k32.1) | copy-start | bytes 3538948
  18.3 15.4 %copy-start.2 = (bf16[256,1152]{1,0:T(8,128)(2,1)S(1)}, bf16[256,1152]{1,0:T(8,128)(2,1)}, u32[]{:S(2)}) copy-start(bf16[256,1152]{1,0:T(8,128)(2,1)} %k31.1) | copy-start | bytes 1769476
  18.3 15.4 %copy-start.6 = (s32[32,4096]{1,0:T(8,128)S(1)}, s32[32,4096]{1,0:T(8,128)}, u32[]{:S(2)}) copy-start(s32[32,4096]{1,0:T(8,128)} %a1.1) | copy-start | bytes 1572868
  18.8 9.3 %collective-permute-start.2 = (bf16[656,128]{1,0:T(8,128)(2,1)S(1)}, bf16[656,128]{1,0:T(8,128)(2,1)S(1)}, u32[]{:S(2)}, u32[]{:S(2)}) collective-permute-start(bf16[656,128]{1,0:T(8,128)(2,1)S(1)} %get-tuple-element.16), channel_id=1, source_target_pairs={{0,1},{1,2},{2,3},{3,4},{4,5},{5,6},{6,7},{7,8},{8,9},{9,10},{10,1... | collective-permute-start | bytes 503816 | tf_op jit(solution)/shard_map/ppermute | solution.py:303
  25.8 7.9 %collective-permute-start.3 = (bf16[656,128]{1,0:T(8,128)(2,1)S(1)}, bf16[656,128]{1,0:T(8,128)(2,1)S(1)}, u32[]{:S(2)}, u32[]{:S(2)}) collective-permute-start(bf16[656,128]{1,0:T(8,128)(2,1)S(1)} %get-tuple-element.17), channel_id=1, source_target_pairs={{1,0},{2,1},{3,2},{4,3},{5,4},{6,5},{7,6},{8,7},{9,8},{10,9},{11,1... | collective-permute-start | bytes 503816 | tf_op jit(solution)/shard_map/ppermute | solution.py:304

commit v3 on v2

v3 whole, which is shorter than its diff:
```python
import jax
import jax.numpy as jnp
from jax import lax
from jax.experimental import pallas as pl
from jax.experimental.pallas import tpu as pltpu
from jax.sharding import PartitionSpec as P

EPSILON = 1e-06
F32 = jnp.float32
BF16 = jnp.bfloat16

COL_SEED, COL_M32, COL_M31, COL_M22, COL_I22, COL_M21, COL_A2, COL_TOTAL = (
    0, 128, 224, 288, 352, 416, 448, 464)
ROW_SEED, ROW_M32, ROW_M31, ROW_A2, ROW_M22, ROW_I22, ROW_M21, ROW_TOTAL = (
    0, 320, 560, 720, 760, 904, 1048, 1120)
T3, T2 = 40, 72
W3, W2, WU, WP = 48, 80, 96, 88
LEAD = 8
LIM = (8, 8, 8, 26, 26)


def inject(preact, target, weight):
    count = preact.shape[-1]
    feature = jnp.maximum(preact.astype(F32), 0.0)
    wanted = jnp.maximum(target.astype(F32), 0.0)
    scale = lax.rsqrt(jnp.sum(feature * feature, axis=-1, keepdims=True) * (1.0 / count) + EPSILON)
    other = lax.rsqrt(jnp.sum(wanted * wanted, axis=-1, keepdims=True) * (1.0 / count) + EPSILON)
    scaled = feature * scale
    excess = (2.0 * weight) * (scaled - wanted * other)
    mean = jnp.sum(excess * scaled, axis=-1, keepdims=True) * (1.0 / count)
    return (excess - scaled * mean) * scale


def pack_cols(hm33, ht33, hm32, hm31, hm22, ht22, hm21, ha2, hw2, hw3, seeds, left, right,
              m33, t33, m32, m31, m22, t22, m21, a2, w2, w3, st3, st2, flat, sems):
    rows, cols, ch = m33.shape
    tall, wide, _ = hm22.shape
    moves = []
    for source, target in (
        (hm33.at[0:8], m33.at[0:8]), (ht33.at[0:8], t33.at[0:8]),
        (hm33.at[8:rows], m33.at[8:rows]), (ht33.at[8:rows], t33.at[8:rows]),
        (hm22.at[:, 0:8], m22.at[0]), (hm22.at[:, wide - 8 : wide], m22.at[1]),
        (ht22.at[:, 0:8], t22.at[0]), (ht22.at[:, wide - 8 : wide], t22.at[1]),
        (hm32.at[:, 0:8], m32.at[0]), (hm32.at[:, cols - 8 : cols], m32.at[1]),
        (hm31.at[:, 0:8], m31.at[0]), (hm31.at[:, cols - 8 : cols], m31.at[1]),
        (hm21.at[:, 0:8], m21.at[0]), (hm21.at[:, wide - 8 : wide], m21.at[1]),
        (ha2.at[:, 0:128], a2.at[0]), (ha2.at[:, (cols - 1) * 128 : cols * 128], a2.at[1]),
        (hw2, w2), (hw3, w3),
    ):
        moves.append(pltpu.make_async_copy(source, target, sems.at[len(moves)]))
        moves[-1].start()
    for move in moves:
        move.wait()
    step = 4
    for r in range(0, rows, step):
        p = m33[r : r + step].reshape(step * cols, ch)
        value = inject(p, t33[r : r + step].reshape(step * cols, ch), w3[...])
        value = jnp.where(p.astype(F32) > 0, value, 0.0).astype(BF16)
        seeds[r : r + step] = value.reshape(step, cols, ch)
    for side, out in enumerate((left, right)):
        edge = slice(cols - 8, cols) if side else slice(0, 8)
        for g, (base, width) in enumerate(((COL_SEED, 4), (COL_M32, 3), (COL_M31, 2))):
            pick = 8 - width if side else 0
            for h in range(2):
                lanes = slice(h * 128, (h + 1) * 128)
                own = (seeds[:, edge, lanes], m32[side, :, :, lanes], m31[side, :, :, lanes])[g]
                stage = st3.at[(g * 2 + side) * 2 + h]
                stage[...] = own.astype(F32).reshape(rows * 8, 128)
                for c in range(width):
                    to = base + (c * 2 + h) * rows
                    flat[side, to : to + rows] = stage[pl.ds(pick + c, rows, stride=8), :]
        p = m22[side].reshape(tall * 8, 128)
        groups = (
            (COL_M22, 2, p.astype(F32)),
            (COL_I22, 2, inject(p, t22[side].reshape(tall * 8, 128), w2[...])),
            (COL_M21, 1, m21[side].astype(F32).reshape(tall * 8, 128)),
        )
        for g, (base, width, own) in enumerate(groups):
            pick = 8 - width if side else 0
            stage = st2.at[g * 2 + side]
            stage[...] = own
            for c in range(width):
                to = base + c * tall
                flat[side, to : to + tall] = stage[pl.ds(pick + c, tall, stride=8), :]
        flat[side, COL_A2 : COL_A2 + rows] = a2[side].astype(F32)
        out[...] = flat[side].astype(BF16)

def own_inject(m22, t22, w2, k21, i22, k21d):
    rows, cols, ch = m22.shape
    step = 4

    @pl.loop(0, rows // step)
    def _(i):
        at = pl.ds(i * step, step)
        value = inject(m22[at].reshape(step * cols, ch), t22[at].reshape(step * cols, ch), w2[...])
        i22[at] = value.reshape(step, cols, ch)

    half = k21.shape[0] // 9
    for t in range(9):
        tap = k21[t * half : (t + 1) * half].astype(F32)
        k21d[:, t * 128 : (t + 1) * 128] = jnp.concatenate([tap, tap], axis=0).T.astype(BF16)


def pack_rows(seeds, m32, m31, m22, i22, m21, a2, fl, fr, up, down, side_l, side_r, flat):
    rows, cols, _ = seeds.shape
    tall, wide, _ = m22.shape
    side_l[...] = fl[...].astype(F32)
    side_r[...] = fr[...].astype(F32)
    for side, out in enumerate((up, down)):
        for source, base, col_base, width in (
            (seeds, ROW_SEED, COL_SEED, 4), (m32, ROW_M32, COL_M32, 3), (m31, ROW_M31, COL_M31, 2),
        ):
            r0 = rows - width if side else 0
            for h in range(2):
                for k in range(width):
                    to = base + (k * 2 + h) * T3 + 4
                    flat[side, to : to + cols] = source[r0 + k, :, h * 128 : (h + 1) * 128].astype(F32)
                for c in range(width):
                    at = col_base + (c * 2 + h) * rows + r0
                    to = base + h * T3
                    flat.at[side][pl.ds(to + 4 - width + c, width, stride=2 * T3), :] = side_l[at : at + width]
                    flat.at[side][pl.ds(to + 4 + cols + c, width, stride=2 * T3), :] = side_r[at : at + width]
        for source, base, col_base, width in (
            (m22, ROW_M22, COL_M22, 2), (i22, ROW_I22, COL_I22, 2), (m21, ROW_M21, COL_M21, 1),
        ):
            r0 = tall - width if side else 0
            for k in range(width):
                to = base + k * T2 + 4
                flat[side, to : to + wide] = source[r0 + k].astype(F32)
                for c in range(width):
                    at = col_base + c * tall + r0 + k
                    flat[side, to - width + c : to - width + c + 1] = side_l[at : at + 1]
                    flat[side, to + wide + c : to + wide + c + 1] = side_r[at : at + 1]
        r0 = rows - 1 if side else 0
        line = a2[r0 : r0 + 1, :].astype(F32)
        to = ROW_A2 + 4
        for c in range(cols):
            flat[side, to + c : to + c + 1] = line[:, c * 128 : (c + 1) * 128]
        at = COL_A2 + r0
        flat[side, to - 1 : to] = side_l[at : at + 1]
        flat[side, to + cols : to + cols + 1] = side_r[at : at + 1]
        out[...] = flat[side].astype(BF16)


def conv(pick, kernel):
    span = kernel.shape[1] // 3
    total = None
    for dy in range(3):
        term = jnp.dot(pick(dy), kernel[:, dy * span : (dy + 1) * span], preferred_element_type=F32)
        total = term if total is None else total + term
    n = span // 3
    before = pltpu.roll(total[:, :n], total.shape[0] - 1, 0)
    after = pltpu.roll(total[:, 2 * n :], 1, 0)
    return before + total[:, n : 2 * n] + after


def block(x, row, count):
    def pick(dy):
        return x[pl.ds(row + 2 - dy, count)].reshape(count * x.shape[1], x.shape[2])

    return pick


def spread(part, where, u2, row):
    for a in range(2):
        for b in range(2):
            to = (2 * row + a) * WU + b
            u2[pl.ds(to, W3, stride=2), :] = jnp.where(where == 2.0 * a + b, part, 0.0)


def emit(a1, pieces, o1):
    tiles = a1.shape[1] // 128
    group = 4

    @pl.loop(0, tiles // group)
    def _(i):
        for first, count, p1, out in pieces:
            high = lax.broadcasted_iota(jnp.int32, (count, 128), 1) >= 64
            shift = jnp.where(high, 1, 0)
            for j in range(group):
                t = i * group + j
                where = a1[first : first + count, pl.ds(pl.multiple_of(t * 128, 128), 128)]
                turned = pltpu.roll(where, 64, 1)
                for odd in range(2):
                    own = (jnp.where(high, where, turned) if odd else jnp.where(high, turned, where)) - shift
                    value = p1[pl.ds(LEAD + 2 * t + odd, count, stride=WP), :]
                    slot = o1.at[2 * j + odd]
                    for a in range(2):
                        slot[pl.ds(a, count, stride=2), :] = jnp.where(own == 2 * a, value, 0.0)
                    to = pl.ds(pl.multiple_of((2 * t + odd) * 128, 128), 128)
                    out[:, to] = slot[0 : 2 * count].astype(BF16)


def inner(seeds, m32, m31, m22, i22, m21, a2, a1, fl, fr, k33, k32, k31, k22, k21d,
          result, t33, t32, t31, ta, t22, ti, t21, y32, y31, y22, y21,
          e33, e32, e31, ea, e22, ei, e21, x33, x32, x31, u2, g22, g21, p1, o1, obuf, sem):
    rows, cols, _ = seeds.shape
    tall, wide, _ = m22.shape
    for source, stage, col_base, width in (
        (seeds, e33, COL_SEED, 4), (m32, e32, COL_M32, 3), (m31, e31, COL_M31, 2),
    ):

        @pl.loop(0, rows // 4)
        def _(i):
            for j in range(4):
                r = i * 4 + j
                to = pl.multiple_of(r * W3 + LEAD, 8)
                for h in range(2):
                    stage[h, pl.ds(to, cols)] = source[r, :, h * 128 : (h + 1) * 128].astype(F32)

        for h in range(2):
            for c in range(width):
                at = col_base + (c * 2 + h) * rows
                stage.at[h][pl.ds(LEAD - width + c, rows, stride=W3), :] = fl[at : at + rows].astype(F32)
                stage.at[h][pl.ds(LEAD + cols + c, rows, stride=W3), :] = fr[at : at + rows].astype(F32)
    for source, stage, col_base, width in (
        (m22, e22, COL_M22, 2), (i22, ei, COL_I22, 2), (m21, e21, COL_M21, 1),
    ):

        @pl.loop(0, tall // 4)
        def _(i):
            for j in range(4):
                r = i * 4 + j
                stage[pl.ds(pl.multiple_of(r * W2 + LEAD, 8), wide)] = source[r].astype(F32)

        for c in range(width):
            at = col_base + c * tall
            stage[pl.ds(LEAD - width + c, tall, stride=W2), :] = fl[at : at + tall].astype(F32)
            stage[pl.ds(LEAD + wide + c, tall, stride=W2), :] = fr[at : at + tall].astype(F32)
    for c in range(cols):
        ea[pl.ds(LEAD + c, rows, stride=W3), :] = a2[:, c * 128 : (c + 1) * 128].astype(F32)
    ea[pl.ds(LEAD - 1, rows, stride=W3), :] = fl[COL_A2 : COL_A2 + rows].astype(F32)
    ea[pl.ds(LEAD + cols, rows, stride=W3), :] = fr[COL_A2 : COL_A2 + rows].astype(F32)

    @pl.loop(0, rows // 2)
    def _(i):
        for j in range(2):
            at = pl.ds(pl.multiple_of((i * 2 + j) * W3, W3), W3)
            for h in range(2):
                x33[i * 2 + j, :, h * 128 : (h + 1) * 128] = e33[h, at].astype(BF16)

    for x, kernel, stage, nxt, skip in ((x33, k33, e32, x32, 1), (x32, k32, e31, x31, 2)):
        count = nxt.shape[0] // 2

        @pl.loop(0, 2)
        def _(i):
            row = i * count
            value = conv(block(x, row, count), kernel)
            at = pl.ds(pl.multiple_of((row + skip) * W3, W3), count * W3)
            for h in range(2):
                part = jnp.where(stage[h, at] > 0, value[:, h * 128 : (h + 1) * 128], 0.0)
                nxt[pl.ds(row, count), :, h * 128 : (h + 1) * 128] = part.astype(BF16).reshape(
                    count, W3, 128
                )

    count = (rows - 6) // 2

    @pl.loop(0, 2)
    def _(i):
        row = i * count
        value = conv(block(x31, row, count), k31)
        for k in range(count):
            where = ea[pl.ds(pl.multiple_of((row + k + 3) * W3, W3), W3)]
            spread(value[k * W3 : (k + 1) * W3], where, u2, row + k)

    @pl.loop(0, g22.shape[0] // 2)
    def _(i):
        for j in range(2):
            r = i * 2 + j
            at = pl.ds(pl.multiple_of((r + 6) * W2, W2), W2)
            arriving = u2[pl.ds(pl.multiple_of(r * WU + LEAD, 8), W2)] + ei[at]
            g22[r] = jnp.where(e22[at] > 0, arriving, 0.0).astype(BF16)

    count = g21.shape[0] // 2

    @pl.loop(0, 2)
    def _(i):
        row = i * count
        value = conv(block(g22, row, count), k22)
        at = pl.ds(pl.multiple_of((row + 7) * W2, W2), count * W2)
        value = jnp.where(e21[at] > 0, value, 0.0)
        g21[pl.ds(row, count)] = value.astype(BF16).reshape(count, W2, 128)

    half = (tall - 16) // 2

    @pl.loop(0, 2)
    def _(i):
        row = i * half
        value = conv(block(g21, row, half), k21d)
        for k in range(half):
            p1[pl.ds(pl.multiple_of((row + k) * WP, 8), W2)] = value[k * W2 : (k + 1) * W2]

    emit(a1, ((8, tall - 16, p1, obuf),), o1)
    move = pltpu.make_async_copy(obuf, result.at[16 : 2 * tall - 16], sem)
    move.start()
    for side in range(2):
        for target, stage, count, width in (
            (t33, e33, 2, W3), (t32, e32, 1, W3), (t31, e31, 2, W3),
        ):
            r0 = (rows - count) * side
            target[side] = stage[:, r0 * width : (r0 + count) * width]
        for target, stage, count, width, total in (
            (ta, ea, 3, W3, rows), (t22, e22, 6, W2, tall), (ti, ei, 6, W2, tall), (t21, e21, 7, W2, tall),
        ):
            r0 = (total - count) * side
            target[side] = stage[r0 * width : (r0 + count) * width]
        for target, source in ((y32, x32), (y31, x31), (y22, g22), (y21, g21)):
            r0 = (source.shape[0] - 2) * side
            target[side] = source[r0 : r0 + 2]
    move.wait()


def outer(t33, t32, t31, ta, t22, ti, t21, y32, y31, y22, y21, above, below, a1,
          k33, k32, k31, k22, k21d, partial, result,
          halo, e33, e32, e31, ea, e22, ei, e21, x33, x32, x31, u2, g22, g21, p1, o1, obuf, sem):
    del partial
    tall = result.shape[0] // 2
    halo[0] = above[...].astype(F32)
    halo[1] = below[...].astype(F32)
    for side in range(2):
        for own, stage, base, width in (
            (t33, e33, ROW_SEED, 4), (t32, e32, ROW_M32, 3), (t31, e31, ROW_M31, 2),
        ):
            keep = own.shape[2]
            for h in range(2):
                to = 0 if side else width * W3
                stage[side, h, to : to + keep] = own[side, h]
                for k in range(width):
                    at = base + (k * 2 + h) * T3
                    to = k * W3 + 4 + (keep if side else 0)
                    stage[side, h, to : to + T3] = halo[side, at : at + T3]
        for own, stage, base, width, narrow, full in (
            (ta, ea, ROW_A2, 1, T3, W3), (t22, e22, ROW_M22, 2, T2, W2),
            (ti, ei, ROW_I22, 2, T2, W2), (t21, e21, ROW_M21, 1, T2, W2),
        ):
            keep = own.shape[1]
            to = 0 if side else width * full
            stage[side, to : to + keep] = own[side]
            for k in range(width):
                at = base + k * narrow
                to = k * full + 4 + (keep if side else 0)
                stage[side, to : to + narrow] = halo[side, at : at + narrow]
        for r in range(6):
            for h in range(2):
                x33[side, r, :, h * 128 : (h + 1) * 128] = e33[side, h, r * W3 : (r + 1) * W3].astype(BF16)
        fresh, kept = (2, 0) if side else (0, 4)
        x32[side, kept : kept + 2] = y32[side]
        x31[side, kept : kept + 2] = y31[side]
        fresh, kept = (2, 0) if side else (0, 8)
        g22[side, kept : kept + 2] = y22[side]
        g21[side, kept : kept + 2] = y21[side]

    def pick_both(x, count):
        return lambda dy: x[:, 2 - dy : 2 - dy + count].reshape(2 * count * x.shape[2], x.shape[3])

    for x, kernel, stage, nxt in ((x33, k33, e32, x32), (x32, k32, e31, x31)):
        value = conv(pick_both(x, 4), kernel)
        for side in range(2):
            for h in range(2):
                part = value[side * 4 * W3 : (side + 1) * 4 * W3, h * 128 : (h + 1) * 128]
                part = jnp.where(stage[side, h] > 0, part, 0.0).astype(BF16).reshape(4, W3, 128)
                nxt[side, 2 * side : 2 * side + 4, :, h * 128 : (h + 1) * 128] = part
    value = conv(pick_both(x31, 4), k31)
    for side in range(2):
        for k in range(4):
            at = (side * 4 + k) * W3
            spread(value[at : at + W3], ea[side, k * W3 : (k + 1) * W3], u2.at[side], k)
        for r in range(8):
            at = slice(r * W2, (r + 1) * W2)
            arriving = u2[side, r * WU + LEAD : r * WU + LEAD + W2] + ei[side, at]
            g22[side, 2 * side + r] = jnp.where(e22[side, at] > 0, arriving, 0.0).astype(BF16)

    @pl.loop(0, 2)
    def _(side):
        value = conv(block(g22.at[side], 0, 8), k22)
        value = jnp.where(e21[side] > 0, value, 0.0).astype(BF16)
        g21[side, pl.ds(2 * side, 8)] = value.reshape(8, W2, 128)

    @pl.loop(0, 2)
    def _(side):
        value = conv(block(g21.at[side], 0, 8), k21d)
        for k in range(8):
            p1[side, k * WP : k * WP + W2] = value[k * W2 : (k + 1) * W2]

    emit(a1, ((0, 8, p1.at[0], obuf.at[0]), (tall - 8, 8, p1.at[1], obuf.at[1])), o1)
    moves = [
        pltpu.make_async_copy(obuf.at[0], result.at[0:16], sem.at[0]),
        pltpu.make_async_copy(obuf.at[1], result.at[2 * tall - 16 : 2 * tall], sem.at[1]),
    ]
    for move in moves:
        move.start()
    for move in moves:
        move.wait()


def whole(array):
    zeros = (0,) * len(array.shape)
    return pl.BlockSpec(array.shape, lambda i: zeros)


STORED = pl.BlockSpec(memory_space=pltpu.MemorySpace.HBM)


def call(body, args, outs, scratch=(), specs=None, out_specs=None, aliases=None, cost=0, limit=8):
    shapes = [jax.ShapeDtypeStruct(s, d) for s, d in outs]
    return pl.pallas_call(
        body,
        grid=(1,),
        in_specs=specs or [whole(a) for a in args],
        out_specs=out_specs or [whole(s) for s in shapes],
        out_shape=shapes,
        input_output_aliases=aliases or {},
        scratch_shapes=[pltpu.VMEM(*s) if isinstance(s, tuple) else s for s in scratch],
        cost_estimate=pl.CostEstimate(flops=cost, bytes_accessed=4000000, transcendentals=0),
        compiler_params=pltpu.CompilerParams(vmem_limit_bytes=limit << 20),
    )(*args)


def swap(first, last, axis):
    count = lax.axis_size(axis)
    from_before = lax.ppermute(last, axis, [(i, i + 1) for i in range(count - 1)])
    from_after = lax.ppermute(first, axis, [(i + 1, i) for i in range(count - 1)])
    return from_before, from_after


def shards(m21, m22, m31, m32, m33, t22, t33, a1, a2, w2, w3, k21, k22, k31, k32, k33):
    rows, cols, ch3 = m33.shape
    tall, wide, ch2 = m22.shape
    w2 = w2.reshape(1, ch2)
    w3 = w3.reshape(1, ch3)
    args = tuple(
        pltpu.with_memory_space_constraint(x, pltpu.MemorySpace.HBM)
        for x in (m33, t33, m32, m31, m22, t22, m21, a2, w2, w3)
    )
    seeds, left, right = call(
        pack_cols, args,
        [((rows, cols, ch3), BF16), ((COL_TOTAL, 128), BF16), ((COL_TOTAL, 128), BF16)],
        scratch=[
            ((rows, cols, ch3), BF16), ((rows, cols, ch3), BF16), ((2, rows, 8, ch3), BF16),
            ((2, rows, 8, ch3), BF16), ((2, tall, 8, ch2), BF16), ((2, tall, 8, ch2), BF16),
            ((2, tall, 8, ch2), BF16), ((2, rows, 128), a2.dtype), (w2.shape, F32), (w3.shape, F32),
            ((12, rows * 8, 128), F32), ((6, tall * 8, 128), F32), ((2, COL_TOTAL, 128), F32),
            pltpu.SemaphoreType.DMA((18,)),
        ],
        specs=[STORED] * 10, cost=10**9, limit=LIM[0],
    )
    fl, fr = swap(left, right, "col")
    i22, k21d = call(
        own_inject, (m22, t22, w2, k21.T),
        [((tall, wide, ch2), F32), ((k21.shape[0], 9 * 128), BF16)], cost=10**9, limit=LIM[1],
    )
    up, down = call(
        pack_rows, (seeds, m32, m31, m22, i22, m21, a2, fl, fr),
        [((ROW_TOTAL, 128), BF16), ((ROW_TOTAL, 128), BF16)],
        scratch=[((COL_TOTAL, 128), F32), ((COL_TOTAL, 128), F32), ((2, ROW_TOTAL, 128), F32)],
        cost=10**9, limit=LIM[2],
    )
    above, below = swap(up, down, "row")
    area3, area2 = rows * W3, tall * W2
    edges = [
        ((2, 2, 2 * W3, 128), F32), ((2, 2, W3, 128), F32), ((2, 2, 2 * W3, 128), F32), ((2, 3 * W3, 128), F32),
        ((2, 6 * W2, 128), F32), ((2, 6 * W2, 128), F32), ((2, 7 * W2, 128), F32),
        ((2, 2, W3, ch3), BF16), ((2, 2, W3, ch3), BF16), ((2, 2, W2, ch2), BF16), ((2, 2, W2, ch2), BF16),
    ]
    shape = (2 * tall, 2 * wide * 64)
    partial, *state = call(
        inner,
        (seeds, m32, m31, m22, i22, m21, a2, a1, fl, fr, k33, k32, k31, k22, k21d),
        [(shape, BF16)] + edges,
        out_specs=[STORED] + [whole(jax.ShapeDtypeStruct(s, d)) for s, d in edges],
        scratch=[
            ((2, area3, 128), F32), ((2, area3, 128), F32), ((2, area3, 128), F32), ((area3, 128), F32),
            ((area2, 128), F32), ((area2, 128), F32), ((area2, 128), F32),
            ((rows, W3, ch3), BF16), ((rows - 2, W3, ch3), BF16), ((rows - 4, W3, ch3), BF16),
            (((tall - 12) * WU, 128), F32), ((tall - 12, W2, ch2), BF16), ((tall - 14, W2, ch2), BF16),
            (((tall - 16) * WP, 128), F32), ((8, 2 * tall, 128), F32), ((2 * tall - 32, shape[1]), BF16),
            pltpu.SemaphoreType.DMA(()),
        ],
        cost=10**10, limit=LIM[3],
    )
    args = (*state, above, below, a1, k33, k32, k31, k22, k21d)
    (result,) = call(
        outer, (*args, partial), [(shape, BF16)],
        specs=[whole(a) for a in args] + [STORED], out_specs=[STORED], aliases={len(args): 0},
        scratch=[
            ((2, ROW_TOTAL, 128), F32),
            ((2, 2, 6 * W3, 128), F32), ((2, 2, 4 * W3, 128), F32), ((2, 2, 4 * W3, 128), F32),
            ((2, 4 * W3, 128), F32), ((2, 8 * W2, 128), F32), ((2, 8 * W2, 128), F32), ((2, 8 * W2, 128), F32),
            ((2, 6, W3, ch3), BF16), ((2, 6, W3, ch3), BF16), ((2, 6, W3, ch3), BF16),
            ((2, 8 * WU, 128), F32), ((2, 10, W2, ch2), BF16), ((2, 10, W2, ch2), BF16),
            ((2, 8 * WP, 128), F32), ((8, 16, 128), F32), ((2, 16, shape[1]), BF16),
            pltpu.SemaphoreType.DMA((2,)),
        ],
        cost=10**9, limit=LIM[4],
    )
    return result


def solution(mesh):
    in_specs = (P("row", "col", None),) * 7 + (P("row", "col"),) * 2 + (P(),) * 7
    return jax.shard_map(
        shards, mesh=mesh, in_specs=in_specs, out_specs=P("row", "col"), check_vma=False
    )
```

time: 48.4 us -> 39.7 us (0.82)
  the two profiles are of different devices: /device:TPU:223 before, /device:TPU:225 now
where the time goes in v3:
time: 39.7 us; the launch traced here: 39.5 us
  Pallas kernels  19.3 us (49%)
  starting transfers between devices  16.6 us (42%)
  waiting for transfers between devices  3.27 us (8%)
    pallas_call x5, Pallas kernels, call(): pl.pallas_call(body, grid=(1,), in_specs=specs or [whole(a) for a in args...  19.3 us
    ppermute x2, starting transfers between devices, swap(): lax.ppermute(last, axis, [(i, i + 1) for i in range(count - 1)])  9.15 us
    ppermute x2, starting transfers between devices, swap(): lax.ppermute(first, axis, [(i + 1, i) for i in range(count - 1)])  7.4 us
    ppermute x2, waiting for transfers between devices, swap(): lax.ppermute(first, axis, [(i + 1, i) for i in range(count - 1)])  3.27 us
  transfers between devices with their start and end apart: 4, of which 1 were waited for; matrix products, arithmetic and copies ran while one was open for 0% of the time, Pallas kernels for 26%

profile of v3, /device:TPU:225, one launch (start us, length us, event | category | flops | bytes accessed | tf_op | source)
XLA Modules:
  0.0 39.5 jit_solution(9074780063903746112)
XLA Ops:
  0.0 0.0 copy-start.12
  0.0 2.5 %shard_map.154 = (bf16[16,32,256]{2,1,0:T(8,128)(2,1)S(1)}, bf16[464,128]{1,0:T(8,128)(2,1)S(1)}, bf16[464,128]{1,0:T(8,128)(2,1)S(1)}) custom-call(bf16[16,32,256]{2,1,0:T(8,128)(2,1)} %hm33.1, bf16[16,32,256]{2,1,0:T(8,128)(2,1)} %ht33.1, bf16[16,32,256]{2,1,0:T(8,128)(2,1)} %m32.3, bf16[16,32,256]{2,1,0:T(8,128)(2,1)} %m31.3, bf16[32,64,128]{2,1,0:T(8,128)(2,1)} %m22.5, ...), custom_call_target="tpu_custom_call" | custom-call | flops 1000000000 | bytes 4000000 | tf_op jit(solution)/shard_map/pallas_call | solution.py:406
  2.5 5.8 %collective-permute-start = (bf16[464,128]{1,0:T(8,128)(2,1)S(1)}, bf16[464,128]{1,0:T(8,128)(2,1)S(1)}, u32[]{:S(2)}, u32[]{:S(2)}) collective-permute-start(bf16[464,128]{1,0:T(8,128)(2,1)S(1)} %get-tuple-element.26), channel_id=1, source_target_pairs={{0,1},{1,2},{2,3},{3,4},{4,5},{5,6},{6,7},{7,8},{8,9},{9,10},{10,1... | collective-permute-start | bytes 356360 | tf_op jit(solution)/shard_map/ppermute | solution.py:421
  8.3 1.9 %collective-permute-start.1 = (bf16[464,128]{1,0:T(8,128)(2,1)S(1)}, bf16[464,128]{1,0:T(8,128)(2,1)S(1)}, u32[]{:S(2)}, u32[]{:S(2)}) collective-permute-start(bf16[464,128]{1,0:T(8,128)(2,1)S(1)} %get-tuple-element.27), channel_id=1, source_target_pairs={{1,0},{2,1},{3,2},{4,3},{5,4},{6,5},{7,6},{8,7},{9,8},{10,9},{11,1... | collective-permute-start | bytes 356360 | tf_op jit(solution)/shard_map/ppermute | solution.py:422
  10.3 0.0 copy-start.7
  10.3 0.0 copy-start.8
  10.3 0.0 copy-start.9
  10.3 0.0 copy-start.10
  10.3 0.0 copy-start.4
  10.3 2.1 %shard_map.155 = (f32[32,64,128]{2,1,0:T(8,128)S(1)}, bf16[128,1152]{1,0:T(8,128)(2,1)S(1)}) custom-call(bf16[32,64,128]{2,1,0:T(8,128)(2,1)S(1)} %copy-done.6, bf16[32,64,128]{2,1,0:T(8,128)(2,1)S(1)} %copy-done.5, f32[1,128]{1,0:T(1,128)S(1)} %bitcast.5, bf16[576,128]{1,0:T(8,128)(2,1)S(1)} %bitcast.3), custom_call_target="tpu_custom_call" | custom-call | flops 1000000000 | bytes 4000000 | tf_op jit(solution)/shard_map/pallas_call | solution.py:406
  12.4 0.0 collective-permute-done.fl
  12.4 3.3 %collective-permute-done.1.fr = bf16[464,128]{1,0:T(8,128)(2,1)S(1)} collective-permute-done((bf16[464,128]{1,0:T(8,128)(2,1)S(1)}, bf16[464,128]{1,0:T(8,128)(2,1)S(1)}, u32[]{:S(2)}, u32[]{:S(2)}) %collective-permute-start.1) | collective-permute-done | bytes 118816 | tf_op jit(solution)/shard_map/ppermute | solution.py:422
  15.7 0.0 copy-done.10
  15.7 0.0 copy-start
  15.7 0.0 copy-start.1
  15.7 0.0 copy-start.2
  15.7 0.0 copy-start.3
  15.7 0.2 shard_map.157
  16.0 3.4 %collective-permute-start.2 = (bf16[1120,128]{1,0:T(8,128)(2,1)S(1)}, bf16[1120,128]{1,0:T(8,128)(2,1)S(1)}, u32[]{:S(2)}, u32[]{:S(2)}) collective-permute-start(bf16[1120,128]{1,0:T(8,128)(2,1)S(1)} %get-tuple-element.40), channel_id=1, source_target_pairs={{0,16},{16,32},{32,48},{48,64},{64,80},{80,96},{96,112},{112,128},... | collective-permute-start | bytes 860168 | tf_op jit(solution)/shard_map/ppermute | solution.py:421
  19.3 5.5 %collective-permute-start.3 = (bf16[1120,128]{1,0:T(8,128)(2,1)S(1)}, bf16[1120,128]{1,0:T(8,128)(2,1)S(1)}, u32[]{:S(2)}, u32[]{:S(2)}) collective-permute-start(bf16[1120,128]{1,0:T(8,128)(2,1)S(1)} %get-tuple-element.41), channel_id=1, source_target_pairs={{16,0},{32,16},{48,32},{64,48},{80,64},{96,80},{112,96},{128,112},... | collective-permute-start | bytes 860168 | tf_op jit(solution)/shard_map/ppermute | solution.py:422
  24.9 8.1 %shard_map.156 = (bf16[64,8192]{1,0:T(8,128)(2,1)}, f32[2,2,96,128]{3,2,1,0:T(8,128)S(1)}, f32[2,2,48,128]{3,2,1,0:T(8,128)S(1)}, f32[2,2,96,128]{3,2,1,0:T(8,12...) custom-call(bf16[16,32,256]{2,1,0:T(8,128)(2,1)S(1)} %get-tuple-elem, ...), custom_call_target="tpu_custom_call" | custom-call | flops 10000000000 | bytes 4000000 | tf_op jit(solution)/shard_map/pallas_call | solution.py:406
  33.0 0.0 collective-permute-done.2.above
  33.0 0.0 collective-permute-done.3.below
  33.0 6.5 %shard_map.158 = bf16[64,8192]{1,0:T(8,128)(2,1)} custom-call(f32[2,2,96,128]{3,2,1,0:T(8,128)S(1)} %get-tuple-element.29.t33, f32[2,2,48,128]{3,2,1,0:T(8,128)S(1)} %get-tuple-element.30.t32, f32[2,2,96,128]{3,2,1,0:T(8,128)S(1)} %get-tuple-element.31.t31, f32[2,144,128]{2,1,0:T(8,128)S(1)} %get-tuple-element.32.ta, ...), custom_call_target="tpu_custom_call", output_to_operand_aliasing={{}: (19, {})} | custom-call | flops 1000000000 | bytes 4000000 | tf_op jit(solution)/shard_map/pallas_call | solution.py:406
  (15 shorter events, 0.0 us)
Async XLA Ops:
  0.0 10.2 %copy-start.5 = (bf16[32,64,128]{2,1,0:T(8,128)(2,1)S(1)}, bf16[32,64,128]{2,1,0:T(8,128)(2,1)}, u32[]{:S(2)}) copy-start(bf16[32,64,128]{2,1,0:T(8,128)(2,1)} %t22.1) | copy-start | bytes 1572868
  0.0 10.3 %copy-start.6 = (bf16[32,64,128]{2,1,0:T(8,128)(2,1)S(1)}, bf16[32,64,128]{2,1,0:T(8,128)(2,1)}, u32[]{:S(2)}) copy-start(bf16[32,64,128]{2,1,0:T(8,128)(2,1)} %m22.5) | copy-start | bytes 1572868
  0.0 10.3 %copy-start.11 = (bf16[128,576]{0,1:T(8,128)(2,1)S(1)}, bf16[128,576]{0,1:T(8,128)(2,1)}, u32[]{:S(2)}) copy-start(bf16[128,576]{0,1:T(8,128)(2,1)} %param.27) | copy-start | bytes 442372
  0.0 10.3 %copy-start.12 = (f32[128]{0:T(128)S(1)}, f32[128]{0:T(128)}, u32[]{:S(2)}) copy-start(f32[128]{0:T(128)} %param.25) | copy-start | bytes 1540
  2.5 9.9 %collective-permute-start = (bf16[464,128]{1,0:T(8,128)(2,1)S(1)}, bf16[464,128]{1,0:T(8,128)(2,1)S(1)}, u32[]{:S(2)}, u32[]{:S(2)}) collective-permute-start(bf16[464,128]{1,0:T(8,128)(2,1)S(1)} %get-tuple-element.26), channel_id=1, source_target_pairs={{0,1},{1,2},{2,3},{3,4},{4,5},{5,6},{6,7},{7,8},{8,9},{9,10},{10,1... | collective-permute-start | bytes 356360 | tf_op jit(solution)/shard_map/ppermute | solution.py:421
  8.3 7.4 %collective-permute-start.1 = (bf16[464,128]{1,0:T(8,128)(2,1)S(1)}, bf16[464,128]{1,0:T(8,128)(2,1)S(1)}, u32[]{:S(2)}, u32[]{:S(2)}) collective-permute-start(bf16[464,128]{1,0:T(8,128)(2,1)S(1)} %get-tuple-element.27), channel_id=1, source_target_pairs={{1,0},{2,1},{3,2},{4,3},{5,4},{6,5},{7,6},{8,7},{9,8},{10,9},{11,1... | collective-permute-start | bytes 356360 | tf_op jit(solution)/shard_map/ppermute | solution.py:422
  10.3 5.4 %copy-start.7 = (bf16[32,64,128]{2,1,0:T(8,128)(2,1)S(1)}, bf16[32,64,128]{2,1,0:T(8,128)(2,1)}, u32[]{:S(2)}) copy-start(bf16[32,64,128]{2,1,0:T(8,128)(2,1)} %m21.3) | copy-start | bytes 1572868
  10.3 5.4 %copy-start.8 = (bf16[16,32,256]{2,1,0:T(8,128)(2,1)S(1)}, bf16[16,32,256]{2,1,0:T(8,128)(2,1)}, u32[]{:S(2)}) copy-start(bf16[16,32,256]{2,1,0:T(8,128)(2,1)} %m32.3) | copy-start | bytes 786436
  10.3 5.4 %copy-start.9 = (bf16[16,32,256]{2,1,0:T(8,128)(2,1)S(1)}, bf16[16,32,256]{2,1,0:T(8,128)(2,1)}, u32[]{:S(2)}) copy-start(bf16[16,32,256]{2,1,0:T(8,128)(2,1)} %m31.3) | copy-start | bytes 786436
  10.3 5.4 %copy-start.10 = (s32[16,4096]{1,0:T(8,128)S(1)}, s32[16,4096]{1,0:T(8,128)}, u32[]{:S(2)}) copy-start(s32[16,4096]{1,0:T(8,128)} %a2.3) | copy-start | bytes 786436
  10.3 14.5 %copy-start.4 = (bf16[128,1152]{1,0:T(8,128)(2,1)S(1)}, bf16[128,1152]{1,0:T(8,128)(2,1)}, u32[]{:S(2)}) copy-start(bf16[128,1152]{1,0:T(8,128)(2,1)} %k22.3) | copy-start | bytes 884740
  15.7 9.1 %copy-start = (bf16[256,2304]{1,0:T(8,128)(2,1)S(1)}, bf16[256,2304]{1,0:T(8,128)(2,1)}, u32[]{:S(2)}) copy-start(bf16[256,2304]{1,0:T(8,128)(2,1)} %k33.3) | copy-start | bytes 3538948
  15.7 9.1 %copy-start.1 = (bf16[256,2304]{1,0:T(8,128)(2,1)S(1)}, bf16[256,2304]{1,0:T(8,128)(2,1)}, u32[]{:S(2)}) copy-start(bf16[256,2304]{1,0:T(8,128)(2,1)} %k32.3) | copy-start | bytes 3538948
  15.7 9.1 %copy-start.2 = (bf16[256,1152]{1,0:T(8,128)(2,1)S(1)}, bf16[256,1152]{1,0:T(8,128)(2,1)}, u32[]{:S(2)}) copy-start(bf16[256,1152]{1,0:T(8,128)(2,1)} %k31.3) | copy-start | bytes 1769476
  15.7 9.1 %copy-start.3 = (s32[32,4096]{1,0:T(8,128)S(1)}, s32[32,4096]{1,0:T(8,128)}, u32[]{:S(2)}) copy-start(s32[32,4096]{1,0:T(8,128)} %a1.3) | copy-start | bytes 1572868
  16.0 17.0 %collective-permute-start.2 = (bf16[1120,128]{1,0:T(8,128)(2,1)S(1)}, bf16[1120,128]{1,0:T(8,128)(2,1)S(1)}, u32[]{:S(2)}, u32[]{:S(2)}) collective-permute-start(bf16[1120,128]{1,0:T(8,128)(2,1)S(1)} %get-tuple-element.40), channel_id=1, source_target_pairs={{0,16},{16,32},{32,48},{48,64},{64,80},{80,96},{96,112},{112,128},... | collective-permute-start | bytes 860168 | tf_op jit(solution)/shard_map/ppermute | solution.py:421
  19.3 13.6 %collective-permute-start.3 = (bf16[1120,128]{1,0:T(8,128)(2,1)S(1)}, bf16[1120,128]{1,0:T(8,128)(2,1)S(1)}, u32[]{:S(2)}, u32[]{:S(2)}) collective-permute-start(bf16[1120,128]{1,0:T(8,128)(2,1)S(1)} %get-tuple-element.41), channel_id=1, source_target_pairs={{16,0},{32,16},{48,32},{64,48},{80,64},{96,80},{112,96},{128,112},... | collective-permute-start | bytes 860168 | tf_op jit(solution)/shard_map/ppermute | solution.py:422

commit v4 on v3

--- a/solution.py
+++ b/solution.py
@@ -16,7 +16,11 @@
 T3, T2 = 40, 72
 W3, W2, WU, WP = 48, 80, 96, 88
 LEAD = 8
-LIM = (8, 8, 8, 26, 26)
+LIM = (8, 10, 8, 26, 26)
+STEP2, STEP3 = 16, 8
+GROUP = 8
+SPLIT3, SPLIT31, SPLIT2 = 2, 2, 2
+SIDES = 2
 
 
 def inject(preact, target, weight):
@@ -31,14 +35,14 @@
     return (excess - scaled * mean) * scale
 
 
-def pack_cols(hm33, ht33, hm32, hm31, hm22, ht22, hm21, ha2, hw2, hw3, seeds, left, right,
+def pack_cols(hm33, ht33, hm32, hm31, hm22, ht22, hm21, ha2, hw2, hw3, left, right,
               m33, t33, m32, m31, m22, t22, m21, a2, w2, w3, st3, st2, flat, sems):
-    rows, cols, ch = m33.shape
+    rows, cols, ch = hm33.shape
     tall, wide, _ = hm22.shape
     moves = []
     for source, target in (
-        (hm33.at[0:8], m33.at[0:8]), (ht33.at[0:8], t33.at[0:8]),
-        (hm33.at[8:rows], m33.at[8:rows]), (ht33.at[8:rows], t33.at[8:rows]),
+        (hm33.at[:, 0:8], m33.at[0]), (hm33.at[:, cols - 8 : cols], m33.at[1]),
+        (ht33.at[:, 0:8], t33.at[0]), (ht33.at[:, cols - 8 : cols], t33.at[1]),
         (hm22.at[:, 0:8], m22.at[0]), (hm22.at[:, wide - 8 : wide], m22.at[1]),
         (ht22.at[:, 0:8], t22.at[0]), (ht22.at[:, wide - 8 : wide], t22.at[1]),
         (hm32.at[:, 0:8], m32.at[0]), (hm32.at[:, cols - 8 : cols], m32.at[1]),
@@ -51,19 +55,15 @@
         moves[-1].start()
     for move in moves:
         move.wait()
-    step = 4
-    for r in range(0, rows, step):
-        p = m33[r : r + step].reshape(step * cols, ch)
-        value = inject(p, t33[r : r + step].reshape(step * cols, ch), w3[...])
-        value = jnp.where(p.astype(F32) > 0, value, 0.0).astype(BF16)
-        seeds[r : r + step] = value.reshape(step, cols, ch)
     for side, out in enumerate((left, right)):
-        edge = slice(cols - 8, cols) if side else slice(0, 8)
+        p = m33[side].reshape(rows * 8, ch)
+        seeds = inject(p, t33[side].reshape(rows * 8, ch), w3[...])
+        seeds = jnp.where(p.astype(F32) > 0, seeds, 0.0).reshape(rows, 8, ch)
         for g, (base, width) in enumerate(((COL_SEED, 4), (COL_M32, 3), (COL_M31, 2))):
             pick = 8 - width if side else 0
             for h in range(2):
                 lanes = slice(h * 128, (h + 1) * 128)
-                own = (seeds[:, edge, lanes], m32[side, :, :, lanes], m31[side, :, :, lanes])[g]
+                own = (seeds[:, :, lanes], m32[side, :, :, lanes], m31[side, :, :, lanes])[g]
                 stage = st3.at[(g * 2 + side) * 2 + h]
                 stage[...] = own.astype(F32).reshape(rows * 8, 128)
                 for c in range(width):
@@ -85,20 +85,31 @@
         flat[side, COL_A2 : COL_A2 + rows] = a2[side].astype(F32)
         out[...] = flat[side].astype(BF16)
 
-def own_inject(m22, t22, w2, k21, i22, k21d):
-    rows, cols, ch = m22.shape
-    step = 4
-
-    @pl.loop(0, rows // step)
-    def _(i):
-        at = pl.ds(i * step, step)
-        value = inject(m22[at].reshape(step * cols, ch), t22[at].reshape(step * cols, ch), w2[...])
-        i22[at] = value.reshape(step, cols, ch)
+def own_inject(m22, t22, m33, t33, w2, w3, k21, k22, i22, seeds, k21p, k22p):
+    tall, wide, _ = m22.shape
+    rows, cols, ch = m33.shape
+
+    @pl.loop(0, tall // STEP2)
+    def _(i):
+        at = pl.ds(i * STEP2, STEP2)
+        p = m22[at].reshape(STEP2 * wide, 128)
+        i22[at] = inject(p, t22[at].reshape(STEP2 * wide, 128), w2[...]).reshape(STEP2, wide, 128)
+
+    @pl.loop(0, rows // STEP3)
+    def _(i):
+        at = pl.ds(i * STEP3, STEP3)
+        p = m33[at].reshape(STEP3 * cols, ch)
+        value = inject(p, t33[at].reshape(STEP3 * cols, ch), w3[...])
+        seeds[at] = jnp.where(p.astype(F32) > 0, value, 0.0).astype(BF16).reshape(STEP3, cols, ch)
 
     half = k21.shape[0] // 9
-    for t in range(9):
-        tap = k21[t * half : (t + 1) * half].astype(F32)
-        k21d[:, t * 128 : (t + 1) * 128] = jnp.concatenate([tap, tap], axis=0).T.astype(BF16)
+    span = k22.shape[1] // 3
+    for dy in range(3):
+        taps = [k21[(3 * dy + dx) * half : (3 * dy + dx + 1) * half].astype(F32) for dx in (0, 2, 1, 1)]
+        rows_of = slice(dy * 128, (dy + 1) * 128)
+        k21p[rows_of, 0:128] = jnp.concatenate(taps[:2], axis=0).T.astype(BF16)
+        k21p[rows_of, 128:256] = jnp.concatenate(taps[2:], axis=0).T.astype(BF16)
+        k22p[rows_of] = k22[:, dy * span : (dy + 1) * span]
 
 
 def pack_rows(seeds, m32, m31, m22, i22, m21, a2, fl, fr, up, down, side_l, side_r, flat):
@@ -148,10 +159,36 @@
     for dy in range(3):
         term = jnp.dot(pick(dy), kernel[:, dy * span : (dy + 1) * span], preferred_element_type=F32)
         total = term if total is None else total + term
-    n = span // 3
+    return shifted(total)
+
+
+def shifted(total):
+    n = total.shape[1] // 3
     before = pltpu.roll(total[:, :n], total.shape[0] - 1, 0)
     after = pltpu.roll(total[:, 2 * n :], 1, 0)
     return before + total[:, n : 2 * n] + after
+
+
+def paired(x, kernel, row, count):
+    size = count * x.shape[1]
+    upper = x[pl.ds(row + 2, count)].reshape(size, 256)
+    lower = x[pl.ds(row, count), :, 0:128].reshape(size, 128)
+    return jnp.dot(upper, kernel[0:256], preferred_element_type=F32) + jnp.dot(
+        lower, kernel[256:384], preferred_element_type=F32
+    )
+
+
+def doubled(total):
+    size = total.shape[0]
+    sides = total[:, 0:128]
+    low = lax.broadcasted_iota(jnp.int32, sides.shape, 1) < 64
+    sides = jnp.where(low, pltpu.roll(sides, size - 1, 0), pltpu.roll(sides, 1, 0))
+    return total[:, 128:256] + sides + pltpu.roll(sides, 64, 1)
+
+
+def store_pair(x, row, count, value):
+    x[pl.ds(row, count), :, 0:128] = value
+    x[pl.ds(row + 1, count), :, 128:256] = value
 
 
 def block(x, row, count):
@@ -168,27 +205,35 @@
             u2[pl.ds(to, W3, stride=2), :] = jnp.where(where == 2.0 * a + b, part, 0.0)
 
 
-def emit(a1, pieces, o1):
+def emit(a1, pieces, o1, result, sems):
     tiles = a1.shape[1] // 128
-    group = 4
-
-    @pl.loop(0, tiles // group)
-    def _(i):
-        for first, count, p1, out in pieces:
+    group = GROUP
+
+    moves = []
+    for i in range(tiles // group):
+        for part, (first, count, p1, out, top) in enumerate(pieces):
             high = lax.broadcasted_iota(jnp.int32, (count, 128), 1) >= 64
             shift = jnp.where(high, 1, 0)
             for j in range(group):
                 t = i * group + j
-                where = a1[first : first + count, pl.ds(pl.multiple_of(t * 128, 128), 128)]
+                where = a1[first : first + count, t * 128 : (t + 1) * 128]
                 turned = pltpu.roll(where, 64, 1)
                 for odd in range(2):
                     own = (jnp.where(high, where, turned) if odd else jnp.where(high, turned, where)) - shift
                     value = p1[pl.ds(LEAD + 2 * t + odd, count, stride=WP), :]
-                    slot = o1.at[2 * j + odd]
+                    slot = o1.at[(part * group + j) * 2 + odd]
                     for a in range(2):
                         slot[pl.ds(a, count, stride=2), :] = jnp.where(own == 2 * a, value, 0.0)
-                    to = pl.ds(pl.multiple_of((2 * t + odd) * 128, 128), 128)
-                    out[:, to] = slot[0 : 2 * count].astype(BF16)
+                    to = (2 * t + odd) * 128
+                    out[:, to : to + 128] = slot[0 : 2 * count].astype(BF16)
+            lanes = slice(2 * i * group * 128, 2 * (i + 1) * group * 128)
+            moves.append(
+                pltpu.make_async_copy(
+                    out.at[:, lanes], result.at[top : top + 2 * count, lanes], sems.at[len(moves)]
+                )
+            )
+            moves[-1].start()
+    return moves
 
 
 def inner(seeds, m32, m31, m22, i22, m21, a2, a1, fl, fr, k33, k32, k31, k22, k21d,
@@ -240,9 +285,9 @@
                 x33[i * 2 + j, :, h * 128 : (h + 1) * 128] = e33[h, at].astype(BF16)
 
     for x, kernel, stage, nxt, skip in ((x33, k33, e32, x32, 1), (x32, k32, e31, x31, 2)):
-        count = nxt.shape[0] // 2
-
-        @pl.loop(0, 2)
+        count = nxt.shape[0] // SPLIT3
+
+        @pl.loop(0, SPLIT3)
         def _(i):
             row = i * count
             value = conv(block(x, row, count), kernel)
@@ -253,9 +298,9 @@
                     count, W3, 128
                 )
 
-    count = (rows - 6) // 2
-
-    @pl.loop(0, 2)
+    count = (rows - 6) // SPLIT31
+
+    @pl.loop(0, SPLIT31)
     def _(i):
         row = i * count
         value = conv(block(x31, row, count), k31)
@@ -263,36 +308,34 @@
             where = ea[pl.ds(pl.multiple_of((row + k + 3) * W3, W3), W3)]
             spread(value[k * W3 : (k + 1) * W3], where, u2, row + k)
 
-    @pl.loop(0, g22.shape[0] // 2)
+    @pl.loop(0, (tall - 12) // 2)
     def _(i):
         for j in range(2):
             r = i * 2 + j
             at = pl.ds(pl.multiple_of((r + 6) * W2, W2), W2)
             arriving = u2[pl.ds(pl.multiple_of(r * WU + LEAD, 8), W2)] + ei[at]
-            g22[r] = jnp.where(e22[at] > 0, arriving, 0.0).astype(BF16)
-
-    count = g21.shape[0] // 2
-
-    @pl.loop(0, 2)
+            store_pair(g22, r, 1, jnp.where(e22[at] > 0, arriving, 0.0).astype(BF16).reshape(1, W2, 128))
+
+    count = (tall - 14) // SPLIT2
+
+    @pl.loop(0, SPLIT2)
     def _(i):
         row = i * count
-        value = conv(block(g22, row, count), k22)
+        value = shifted(paired(g22, k22, row, count))
         at = pl.ds(pl.multiple_of((row + 7) * W2, W2), count * W2)
         value = jnp.where(e21[at] > 0, value, 0.0)
-        g21[pl.ds(row, count)] = value.astype(BF16).reshape(count, W2, 128)
-
-    half = (tall - 16) // 2
-
-    @pl.loop(0, 2)
+        store_pair(g21, row, count, value.astype(BF16).reshape(count, W2, 128))
+
+    half = (tall - 16) // SPLIT2
+
+    @pl.loop(0, SPLIT2)
     def _(i):
         row = i * half
-        value = conv(block(g21, row, half), k21d)
+        value = doubled(paired(g21, k21d, row, half))
         for k in range(half):
             p1[pl.ds(pl.multiple_of((row + k) * WP, 8), W2)] = value[k * W2 : (k + 1) * W2]
 
-    emit(a1, ((8, tall - 16, p1, obuf),), o1)
-    move = pltpu.make_async_copy(obuf, result.at[16 : 2 * tall - 16], sem)
-    move.start()
+    moves = emit(a1, ((8, tall - 16, p1, obuf, 16),), o1, result, sem)
     for side in range(2):
         for target, stage, count, width in (
             (t33, e33, 2, W3), (t32, e32, 1, W3), (t31, e31, 2, W3),
@@ -304,10 +347,13 @@
         ):
             r0 = (total - count) * side
             target[side] = stage[r0 * width : (r0 + count) * width]
-        for target, source in ((y32, x32), (y31, x31), (y22, g22), (y21, g21)):
-            r0 = (source.shape[0] - 2) * side
-            target[side] = source[r0 : r0 + 2]
-    move.wait()
+        for target, source, count in (
+            (y32, x32, rows - 2), (y31, x31, rows - 4), (y22, g22, tall - 12), (y21, g21, tall - 14),
+        ):
+            r0 = (count - 2) * side
+            target[side] = source[r0 : r0 + 2, :, 0 : target.shape[3]]
+    for move in moves:
+        move.wait()
 
 
 def outer(t33, t32, t31, ta, t22, ti, t21, y32, y31, y22, y21, above, below, a1,
@@ -347,8 +393,8 @@
         x32[side, kept : kept + 2] = y32[side]
         x31[side, kept : kept + 2] = y31[side]
         fresh, kept = (2, 0) if side else (0, 8)
-        g22[side, kept : kept + 2] = y22[side]
-        g21[side, kept : kept + 2] = y21[side]
+        store_pair(g22.at[side], kept, 2, y22[side])
+        store_pair(g21.at[side], kept, 2, y21[side])
 
     def pick_both(x, count):
         return lambda dy: x[:, 2 - dy : 2 - dy + count].reshape(2 * count * x.shape[2], x.shape[3])
@@ -368,27 +414,31 @@
         for r in range(8):
             at = slice(r * W2, (r + 1) * W2)
             arriving = u2[side, r * WU + LEAD : r * WU + LEAD + W2] + ei[side, at]
-            g22[side, 2 * side + r] = jnp.where(e22[side, at] > 0, arriving, 0.0).astype(BF16)
-
-    @pl.loop(0, 2)
-    def _(side):
-        value = conv(block(g22.at[side], 0, 8), k22)
+            arriving = jnp.where(e22[side, at] > 0, arriving, 0.0).astype(BF16)
+            store_pair(g22.at[side], 2 * side + r, 1, arriving.reshape(1, W2, 128))
+
+    def second(side):
+        value = shifted(paired(g22.at[side], k22, 0, 8))
         value = jnp.where(e21[side] > 0, value, 0.0).astype(BF16)
-        g21[side, pl.ds(2 * side, 8)] = value.reshape(8, W2, 128)
-
-    @pl.loop(0, 2)
-    def _(side):
-        value = conv(block(g21.at[side], 0, 8), k21d)
+        store_pair(g21.at[side], 2 * side, 8, value.reshape(8, W2, 128))
+
+    def first(side):
+        value = doubled(paired(g21.at[side], k21d, 0, 8))
         for k in range(8):
             p1[side, k * WP : k * WP + W2] = value[k * W2 : (k + 1) * W2]
 
-    emit(a1, ((0, 8, p1.at[0], obuf.at[0]), (tall - 8, 8, p1.at[1], obuf.at[1])), o1)
-    moves = [
-        pltpu.make_async_copy(obuf.at[0], result.at[0:16], sem.at[0]),
-        pltpu.make_async_copy(obuf.at[1], result.at[2 * tall - 16 : 2 * tall], sem.at[1]),
-    ]
-    for move in moves:
-        move.start()
+    for step in (second, first):
+        if SIDES == 1:
+            pl.loop(0, 2)(step)
+        else:
+            for side in range(2):
+                step(side)
+
+    moves = emit(
+        a1,
+        ((0, 8, p1.at[0], obuf.at[0], 0), (tall - 8, 8, p1.at[1], obuf.at[1], 2 * tall - 16)),
+        o1, result, sem,
+    )
     for move in moves:
         move.wait()
 
@@ -432,11 +482,11 @@
         pltpu.with_memory_space_constraint(x, pltpu.MemorySpace.HBM)
         for x in (m33, t33, m32, m31, m22, t22, m21, a2, w2, w3)
     )
-    seeds, left, right = call(
+    left, right = call(
         pack_cols, args,
-        [((rows, cols, ch3), BF16), ((COL_TOTAL, 128), BF16), ((COL_TOTAL, 128), BF16)],
+        [((COL_TOTAL, 128), BF16), ((COL_TOTAL, 128), BF16)],
         scratch=[
-            ((rows, cols, ch3), BF16), ((rows, cols, ch3), BF16), ((2, rows, 8, ch3), BF16),
+            ((2, rows, 8, ch3), BF16), ((2, rows, 8, ch3), BF16), ((2, rows, 8, ch3), BF16),
             ((2, rows, 8, ch3), BF16), ((2, tall, 8, ch2), BF16), ((2, tall, 8, ch2), BF16),
             ((2, tall, 8, ch2), BF16), ((2, rows, 128), a2.dtype), (w2.shape, F32), (w3.shape, F32),
             ((12, rows * 8, 128), F32), ((6, tall * 8, 128), F32), ((2, COL_TOTAL, 128), F32),
@@ -445,9 +495,10 @@
         specs=[STORED] * 10, cost=10**9, limit=LIM[0],
     )
     fl, fr = swap(left, right, "col")
-    i22, k21d = call(
-        own_inject, (m22, t22, w2, k21.T),
-        [((tall, wide, ch2), F32), ((k21.shape[0], 9 * 128), BF16)], cost=10**9, limit=LIM[1],
+    i22, seeds, k21d, k22 = call(
+        own_inject, (m22, t22, m33, t33, w2, w3, k21.T, k22),
+        [((tall, wide, ch2), F32), ((rows, cols, ch3), BF16), ((3 * ch2, 256), BF16), ((3 * ch2, 384), BF16)],
+        cost=10**9, limit=LIM[1],
     )
     up, down = call(
         pack_rows, (seeds, m32, m31, m22, i22, m21, a2, fl, fr),
@@ -472,9 +523,9 @@
             ((2, area3, 128), F32), ((2, area3, 128), F32), ((2, area3, 128), F32), ((area3, 128), F32),
             ((area2, 128), F32), ((area2, 128), F32), ((area2, 128), F32),
             ((rows, W3, ch3), BF16), ((rows - 2, W3, ch3), BF16), ((rows - 4, W3, ch3), BF16),
-            (((tall - 12) * WU, 128), F32), ((tall - 12, W2, ch2), BF16), ((tall - 14, W2, ch2), BF16),
-            (((tall - 16) * WP, 128), F32), ((8, 2 * tall, 128), F32), ((2 * tall - 32, shape[1]), BF16),
-            pltpu.SemaphoreType.DMA(()),
+            (((tall - 12) * WU, 128), F32), ((tall - 11, W2, 256), BF16), ((tall - 13, W2, 256), BF16),
+            (((tall - 16) * WP, 128), F32), ((2 * GROUP, 2 * tall - 32, 128), F32), ((2 * tall - 32, shape[1]), BF16),
+            pltpu.SemaphoreType.DMA((wide // 2 // GROUP,)),
         ],
         cost=10**10, limit=LIM[3],
     )
@@ -487,9 +538,9 @@
             ((2, 2, 6 * W3, 128), F32), ((2, 2, 4 * W3, 128), F32), ((2, 2, 4 * W3, 128), F32),
             ((2, 4 * W3, 128), F32), ((2, 8 * W2, 128), F32), ((2, 8 * W2, 128), F32), ((2, 8 * W2, 128), F32),
             ((2, 6, W3, ch3), BF16), ((2, 6, W3, ch3), BF16), ((2, 6, W3, ch3), BF16),
-            ((2, 8 * WU, 128), F32), ((2, 10, W2, ch2), BF16), ((2, 10, W2, ch2), BF16),
-            ((2, 8 * WP, 128), F32), ((8, 16, 128), F32), ((2, 16, shape[1]), BF16),
-            pltpu.SemaphoreType.DMA((2,)),
+            ((2, 8 * WU, 128), F32), ((2, 11, W2, 256), BF16), ((2, 11, W2, 256), BF16),
+            ((2, 8 * WP, 128), F32), ((4 * GROUP, 16, 128), F32), ((2, 16, shape[1]), BF16),
+            pltpu.SemaphoreType.DMA((2 * (wide // 2 // GROUP),)),
         ],
         cost=10**9, limit=LIM[4],
     )

time: 39.7 us -> 36.5 us (0.919)
  Pallas kernels: 19.3 us -> 15.8 us
    pallas_call x5, Pallas kernels: 19.3 us -> 15.8 us  [call(): pl.pallas_call(body, grid=(1,), in_specs=specs or [whole(a) for a in args...]
  transfers between devices with their start and end apart: 4 -> 4, of which waited for: 1 -> 1; matrix products, arithmetic and copies ran while one was open for 0% -> 0% of each run, Pallas kernels for 26% -> 23%
where the time goes in v4:
time: 36.5 us; the launch traced here: 36.3 us
  starting transfers between devices  16.6 us (45%)
  Pallas kernels  15.8 us (43%)
  waiting for transfers between devices  3.65 us (10%)
    pallas_call x5, Pallas kernels, call(): pl.pallas_call(body, grid=(1,), in_specs=specs or [whole(a) for a in args...  15.8 us
    ppermute x2, starting transfers between devices, swap(): lax.ppermute(last, axis, [(i, i + 1) for i in range(count - 1)])  9.15 us
    ppermute x2, starting transfers between devices, swap(): lax.ppermute(first, axis, [(i + 1, i) for i in range(count - 1)])  7.4 us
    ppermute x2, waiting for transfers between devices, swap(): lax.ppermute(first, axis, [(i + 1, i) for i in range(count - 1)])  3.65 us
  transfers between devices with their start and end apart: 4, of which 1 were waited for; matrix products, arithmetic and copies ran while one was open for 0% of the time, Pallas kernels for 23%

profile of v4, /device:TPU:225, one launch (start us, length us, event | category | flops | bytes accessed | tf_op | source)
XLA Modules:
  0.0 36.3 jit_solution(13439177983720757528)
XLA Ops:
  0.1 2.2 %shard_map.155 = (bf16[464,128]{1,0:T(8,128)(2,1)S(1)}, bf16[464,128]{1,0:T(8,128)(2,1)S(1)}) custom-call(bf16[16,32,256]{2,1,0:T(8,128)(2,1)} %hm33.1, bf16[16,32,256]{2,1,0:T(8,128)(2,1)} %ht33.1, bf16[16,32,256]{2,1,0:T(8,128)(2,1)} %m32.3, bf16[16,32,256]{2,1,0:T(8,128)(2,1)} %m31.3, bf16[32,64,128]{2,1,0:T(8,128)(2,1)} %m22.5, ...), custom_call_target="tpu_custom_call" | custom-call | flops 1000000000 | bytes 4000000 | tf_op jit(solution)/shard_map/pallas_call | solution.py:456
  2.3 5.8 %collective-permute-start = (bf16[464,128]{1,0:T(8,128)(2,1)S(1)}, bf16[464,128]{1,0:T(8,128)(2,1)S(1)}, u32[]{:S(2)}, u32[]{:S(2)}) collective-permute-start(bf16[464,128]{1,0:T(8,128)(2,1)S(1)} %get-tuple-element.27), channel_id=1, source_target_pairs={{0,1},{1,2},{2,3},{3,4},{4,5},{5,6},{6,7},{7,8},{8,9},{9,10},{10,1... | collective-permute-start | bytes 356360 | tf_op jit(solution)/shard_map/ppermute | solution.py:471
  8.1 1.9 %collective-permute-start.1 = (bf16[464,128]{1,0:T(8,128)(2,1)S(1)}, bf16[464,128]{1,0:T(8,128)(2,1)S(1)}, u32[]{:S(2)}, u32[]{:S(2)}) collective-permute-start(bf16[464,128]{1,0:T(8,128)(2,1)S(1)} %get-tuple-element.28), channel_id=1, source_target_pairs={{1,0},{2,1},{3,2},{4,3},{5,4},{6,5},{7,6},{8,7},{9,8},{10,9},{11,1... | collective-permute-start | bytes 356360 | tf_op jit(solution)/shard_map/ppermute | solution.py:472
  10.0 0.0 copy-done.4
  10.0 0.0 copy-done.5
  10.0 0.0 copy-done.7
  10.1 0.0 copy-start.6
  10.1 0.0 copy-start.10
  10.1 0.0 copy-start.11
  10.1 0.0 copy-start.12
  10.1 1.6 %shard_map.154 = (f32[32,64,128]{2,1,0:T(8,128)S(1)}, bf16[16,32,256]{2,1,0:T(8,128)(2,1)S(1)}, bf16[384,256]{1,0:T(8,128)(2,1)S(1)}, bf16[384,384]{1,0:T(8,128)(2,1)S(1)}) custom-call(bf16[32,64,128]{2,1,0:T(8,128)(2,1)S(1)} %copy-done.5, bf16[32,64,128]{2,1,0:T(8,128)(2,1)S(1)} %copy-done.4, bf16[16,32,256]{2,1,0:T(8,128)(2,1)S(1)} %copy-done.8, ...), custom_call_target="tpu_custom_call" | custom-call | flops 1000000000 | bytes 4000000 | tf_op jit(solution)/shard_map/pallas_call | solution.py:456
  11.8 0.0 collective-permute-done.fl
  11.8 3.6 %collective-permute-done.1.fr = bf16[464,128]{1,0:T(8,128)(2,1)S(1)} collective-permute-done((bf16[464,128]{1,0:T(8,128)(2,1)S(1)}, bf16[464,128]{1,0:T(8,128)(2,1)S(1)}, u32[]{:S(2)}, u32[]{:S(2)}) %collective-permute-start.1) | collective-permute-done | bytes 118816 | tf_op jit(solution)/shard_map/ppermute | solution.py:472
  15.5 0.0 copy-start
  15.5 0.0 copy-start.1
  15.5 0.0 copy-start.2
  15.5 0.0 copy-start.3
  15.5 0.2 shard_map.157
  15.7 3.4 %collective-permute-start.2 = (bf16[1120,128]{1,0:T(8,128)(2,1)S(1)}, bf16[1120,128]{1,0:T(8,128)(2,1)S(1)}, u32[]{:S(2)}, u32[]{:S(2)}) collective-permute-start(bf16[1120,128]{1,0:T(8,128)(2,1)S(1)} %get-tuple-element.42), channel_id=1, source_target_pairs={{0,16},{16,32},{32,48},{48,64},{64,80},{80,96},{96,112},{112,128},... | collective-permute-start | bytes 860168 | tf_op jit(solution)/shard_map/ppermute | solution.py:471
  19.1 5.5 %collective-permute-start.3 = (bf16[1120,128]{1,0:T(8,128)(2,1)S(1)}, bf16[1120,128]{1,0:T(8,128)(2,1)S(1)}, u32[]{:S(2)}, u32[]{:S(2)}) collective-permute-start(bf16[1120,128]{1,0:T(8,128)(2,1)S(1)} %get-tuple-element.43), channel_id=1, source_target_pairs={{16,0},{32,16},{48,32},{64,48},{80,64},{96,80},{112,96},{128,112},... | collective-permute-start | bytes 860168 | tf_op jit(solution)/shard_map/ppermute | solution.py:472
  24.6 6.9 %shard_map.156 = (bf16[64,8192]{1,0:T(8,128)(2,1)}, f32[2,2,96,128]{3,2,1,0:T(8,128)S(1)}, f32[2,2,48,128]{3,2,1,0:T(8,128)S(1)}, f32[2,2,96,128]{3,2,1,0:T(8,12...) custom-call(bf16[16,32,256]{2,1,0:T(8,128)(2,1)S(1)} %get-tuple-elem, ...), custom_call_target="tpu_custom_call" | custom-call | flops 10000000000 | bytes 4000000 | tf_op jit(solution)/shard_map/pallas_call | solution.py:456
  31.5 0.0 collective-permute-done.2.above
  31.5 0.0 collective-permute-done.3.below
  31.5 4.8 %shard_map.158 = bf16[64,8192]{1,0:T(8,128)(2,1)} custom-call(f32[2,2,96,128]{3,2,1,0:T(8,128)S(1)} %get-tuple-element.31.t33, f32[2,2,48,128]{3,2,1,0:T(8,128)S(1)} %get-tuple-element.32.t32, f32[2,2,96,128]{3,2,1,0:T(8,128)S(1)} %get-tuple-element.33.t31, f32[2,144,128]{2,1,0:T(8,128)S(1)} %get-tuple-element.34.ta, ...), custom_call_target="tpu_custom_call", output_to_operand_aliasing={{}: (19, {})} | custom-call | flops 1000000000 | bytes 4000000 | tf_op jit(solution)/shard_map/pallas_call | solution.py:456
  (21 shorter events, 0.0 us)
Async XLA Ops:
  0.0 10.0 %copy-start.4 = (bf16[32,64,128]{2,1,0:T(8,128)(2,1)S(1)}, bf16[32,64,128]{2,1,0:T(8,128)(2,1)}, u32[]{:S(2)}) copy-start(bf16[32,64,128]{2,1,0:T(8,128)(2,1)} %ht22.1) | copy-start | bytes 1572868
  0.0 10.0 %copy-start.5 = (bf16[32,64,128]{2,1,0:T(8,128)(2,1)S(1)}, bf16[32,64,128]{2,1,0:T(8,128)(2,1)}, u32[]{:S(2)}) copy-start(bf16[32,64,128]{2,1,0:T(8,128)(2,1)} %m22.5) | copy-start | bytes 1572868
  0.0 10.0 %copy-start.7 = (bf16[128,1152]{1,0:T(8,128)(2,1)S(1)}, bf16[128,1152]{1,0:T(8,128)(2,1)}, u32[]{:S(2)}) copy-start(bf16[128,1152]{1,0:T(8,128)(2,1)} %k22.1) | copy-start | bytes 884740
  0.0 10.0 %copy-start.8 = (bf16[16,32,256]{2,1,0:T(8,128)(2,1)S(1)}, bf16[16,32,256]{2,1,0:T(8,128)(2,1)}, u32[]{:S(2)}) copy-start(bf16[16,32,256]{2,1,0:T(8,128)(2,1)} %hm33.1) | copy-start | bytes 786436
  0.0 10.0 %copy-start.9 = (bf16[16,32,256]{2,1,0:T(8,128)(2,1)S(1)}, bf16[16,32,256]{2,1,0:T(8,128)(2,1)}, u32[]{:S(2)}) copy-start(bf16[16,32,256]{2,1,0:T(8,128)(2,1)} %ht33.1) | copy-start | bytes 786436
  0.0 10.0 %copy-start.13 = (bf16[128,576]{0,1:T(8,128)(2,1)S(1)}, bf16[128,576]{0,1:T(8,128)(2,1)}, u32[]{:S(2)}) copy-start(bf16[128,576]{0,1:T(8,128)(2,1)} %param.27) | copy-start | bytes 442372
  0.0 10.0 %copy-start.14 = (f32[256]{0:T(256)S(1)}, f32[256]{0:T(256)}, u32[]{:S(2)}) copy-start(f32[256]{0:T(256)} %param.26) | copy-start | bytes 3076
  0.0 10.0 %copy-start.15 = (f32[128]{0:T(128)S(1)}, f32[128]{0:T(128)}, u32[]{:S(2)}) copy-start(f32[128]{0:T(128)} %param.25) | copy-start | bytes 1540
  2.3 9.5 %collective-permute-start = (bf16[464,128]{1,0:T(8,128)(2,1)S(1)}, bf16[464,128]{1,0:T(8,128)(2,1)S(1)}, u32[]{:S(2)}, u32[]{:S(2)}) collective-permute-start(bf16[464,128]{1,0:T(8,128)(2,1)S(1)} %get-tuple-element.27), channel_id=1, source_target_pairs={{0,1},{1,2},{2,3},{3,4},{4,5},{5,6},{6,7},{7,8},{8,9},{9,10},{10,1... | collective-permute-start | bytes 356360 | tf_op jit(solution)/shard_map/ppermute | solution.py:471
  8.1 7.4 %collective-permute-start.1 = (bf16[464,128]{1,0:T(8,128)(2,1)S(1)}, bf16[464,128]{1,0:T(8,128)(2,1)S(1)}, u32[]{:S(2)}, u32[]{:S(2)}) collective-permute-start(bf16[464,128]{1,0:T(8,128)(2,1)S(1)} %get-tuple-element.28), channel_id=1, source_target_pairs={{1,0},{2,1},{3,2},{4,3},{5,4},{6,5},{7,6},{8,7},{9,8},{10,9},{11,1... | collective-permute-start | bytes 356360 | tf_op jit(solution)/shard_map/ppermute | solution.py:472
  10.1 5.4 %copy-start.6 = (bf16[32,64,128]{2,1,0:T(8,128)(2,1)S(1)}, bf16[32,64,128]{2,1,0:T(8,128)(2,1)}, u32[]{:S(2)}) copy-start(bf16[32,64,128]{2,1,0:T(8,128)(2,1)} %m21.3) | copy-start | bytes 1572868
  10.1 5.4 %copy-start.10 = (bf16[16,32,256]{2,1,0:T(8,128)(2,1)S(1)}, bf16[16,32,256]{2,1,0:T(8,128)(2,1)}, u32[]{:S(2)}) copy-start(bf16[16,32,256]{2,1,0:T(8,128)(2,1)} %m32.3) | copy-start | bytes 786436
  10.1 5.3 %copy-start.11 = (bf16[16,32,256]{2,1,0:T(8,128)(2,1)S(1)}, bf16[16,32,256]{2,1,0:T(8,128)(2,1)}, u32[]{:S(2)}) copy-start(bf16[16,32,256]{2,1,0:T(8,128)(2,1)} %m31.3) | copy-start | bytes 786436
  10.1 5.3 %copy-start.12 = (s32[16,4096]{1,0:T(8,128)S(1)}, s32[16,4096]{1,0:T(8,128)}, u32[]{:S(2)}) copy-start(s32[16,4096]{1,0:T(8,128)} %a2.3) | copy-start | bytes 786436
  15.5 9.1 %copy-start = (bf16[256,2304]{1,0:T(8,128)(2,1)S(1)}, bf16[256,2304]{1,0:T(8,128)(2,1)}, u32[]{:S(2)}) copy-start(bf16[256,2304]{1,0:T(8,128)(2,1)} %k33.3) | copy-start | bytes 3538948
  15.5 9.1 %copy-start.1 = (bf16[256,2304]{1,0:T(8,128)(2,1)S(1)}, bf16[256,2304]{1,0:T(8,128)(2,1)}, u32[]{:S(2)}) copy-start(bf16[256,2304]{1,0:T(8,128)(2,1)} %k32.3) | copy-start | bytes 3538948
  15.5 9.1 %copy-start.2 = (bf16[256,1152]{1,0:T(8,128)(2,1)S(1)}, bf16[256,1152]{1,0:T(8,128)(2,1)}, u32[]{:S(2)}) copy-start(bf16[256,1152]{1,0:T(8,128)(2,1)} %k31.3) | copy-start | bytes 1769476
  15.5 9.1 %copy-start.3 = (s32[32,4096]{1,0:T(8,128)S(1)}, s32[32,4096]{1,0:T(8,128)}, u32[]{:S(2)}) copy-start(s32[32,4096]{1,0:T(8,128)} %a1.3) | copy-start | bytes 1572868
  15.7 15.8 %collective-permute-start.2 = (bf16[1120,128]{1,0:T(8,128)(2,1)S(1)}, bf16[1120,128]{1,0:T(8,128)(2,1)S(1)}, u32[]{:S(2)}, u32[]{:S(2)}) collective-permute-start(bf16[1120,128]{1,0:T(8,128)(2,1)S(1)} %get-tuple-element.42), channel_id=1, source_target_pairs={{0,16},{16,32},{32,48},{48,64},{64,80},{80,96},{96,112},{112,128},... | collective-permute-start | bytes 860168 | tf_op jit(solution)/shard_map/ppermute | solution.py:471
  19.1 12.4 %collective-permute-start.3 = (bf16[1120,128]{1,0:T(8,128)(2,1)S(1)}, bf16[1120,128]{1,0:T(8,128)(2,1)S(1)}, u32[]{:S(2)}, u32[]{:S(2)}) collective-permute-start(bf16[1120,128]{1,0:T(8,128)(2,1)S(1)} %get-tuple-element.43), channel_id=1, source_target_pairs={{16,0},{32,16},{48,32},{64,48},{80,64},{96,80},{112,96},{128,112},... | collective-permute-start | bytes 860168 | tf_op jit(solution)/shard_map/ppermute | solution.py:472

commit v5 on v4

--- a/solution.py
+++ b/solution.py
@@ -19,6 +19,9 @@
 LIM = (8, 10, 8, 26, 26)
 STEP2, STEP3 = 16, 8
 GROUP = 8
+FLAGS = [None] * 5
+UNROLL = (1, 1, 1, 1)
+PERSIDE = 1
 SPLIT3, SPLIT31, SPLIT2 = 2, 2, 2
 SIDES = 2
 
@@ -53,12 +56,16 @@
     ):
         moves.append(pltpu.make_async_copy(source, target, sems.at[len(moves)]))
         moves[-1].start()
-    for move in moves:
+    for move in moves[0:4] + moves[-2:]:
         move.wait()
+    rest = moves[4:-2]
     for side, out in enumerate((left, right)):
         p = m33[side].reshape(rows * 8, ch)
         seeds = inject(p, t33[side].reshape(rows * 8, ch), w3[...])
         seeds = jnp.where(p.astype(F32) > 0, seeds, 0.0).reshape(rows, 8, ch)
+        if side == 0:
+            for move in rest:
+                move.wait()
         for g, (base, width) in enumerate(((COL_SEED, 4), (COL_M32, 3), (COL_M31, 2))):
             pick = 8 - width if side else 0
             for h in range(2):
@@ -236,6 +243,17 @@
     return moves
 
 
+def steps(count, static):
+    def run(body):
+        if static:
+            for i in range(count):
+                body(i)
+        else:
+            pl.loop(0, count)(body)
+
+    return run
+
+
 def inner(seeds, m32, m31, m22, i22, m21, a2, a1, fl, fr, k33, k32, k31, k22, k21d,
           result, t33, t32, t31, ta, t22, ti, t21, y32, y31, y22, y21,
           e33, e32, e31, ea, e22, ei, e21, x33, x32, x31, u2, g22, g21, p1, o1, obuf, sem):
@@ -277,7 +295,7 @@
     ea[pl.ds(LEAD - 1, rows, stride=W3), :] = fl[COL_A2 : COL_A2 + rows].astype(F32)
     ea[pl.ds(LEAD + cols, rows, stride=W3), :] = fr[COL_A2 : COL_A2 + rows].astype(F32)
 
-    @pl.loop(0, rows // 2)
+    @steps(rows // 2, True)
     def _(i):
         for j in range(2):
             at = pl.ds(pl.multiple_of((i * 2 + j) * W3, W3), W3)
@@ -287,7 +305,7 @@
     for x, kernel, stage, nxt, skip in ((x33, k33, e32, x32, 1), (x32, k32, e31, x31, 2)):
         count = nxt.shape[0] // SPLIT3
 
-        @pl.loop(0, SPLIT3)
+        @steps(SPLIT3, UNROLL[0])
         def _(i):
             row = i * count
             value = conv(block(x, row, count), kernel)
@@ -300,7 +318,7 @@
 
     count = (rows - 6) // SPLIT31
 
-    @pl.loop(0, SPLIT31)
+    @steps(SPLIT31, UNROLL[1])
     def _(i):
         row = i * count
         value = conv(block(x31, row, count), k31)
@@ -308,7 +326,7 @@
             where = ea[pl.ds(pl.multiple_of((row + k + 3) * W3, W3), W3)]
             spread(value[k * W3 : (k + 1) * W3], where, u2, row + k)
 
-    @pl.loop(0, (tall - 12) // 2)
+    @steps((tall - 12) // 2, True)
     def _(i):
         for j in range(2):
             r = i * 2 + j
@@ -318,7 +336,7 @@
 
     count = (tall - 14) // SPLIT2
 
-    @pl.loop(0, SPLIT2)
+    @steps(SPLIT2, UNROLL[2])
     def _(i):
         row = i * count
         value = shifted(paired(g22, k22, row, count))
@@ -328,7 +346,7 @@
 
     half = (tall - 16) // SPLIT2
 
-    @pl.loop(0, SPLIT2)
+    @steps(SPLIT2, UNROLL[3])
     def _(i):
         row = i * half
         value = doubled(paired(g21, k21d, row, half))
@@ -396,21 +414,17 @@
         store_pair(g22.at[side], kept, 2, y22[side])
         store_pair(g21.at[side], kept, 2, y21[side])
 
-    def pick_both(x, count):
-        return lambda dy: x[:, 2 - dy : 2 - dy + count].reshape(2 * count * x.shape[2], x.shape[3])
-
     for x, kernel, stage, nxt in ((x33, k33, e32, x32), (x32, k32, e31, x31)):
-        value = conv(pick_both(x, 4), kernel)
         for side in range(2):
-            for h in range(2):
-                part = value[side * 4 * W3 : (side + 1) * 4 * W3, h * 128 : (h + 1) * 128]
+            value = conv(block(x.at[side], 0, 4), kernel)
+            for h in range(2):
+                part = value[:, h * 128 : (h + 1) * 128]
                 part = jnp.where(stage[side, h] > 0, part, 0.0).astype(BF16).reshape(4, W3, 128)
                 nxt[side, 2 * side : 2 * side + 4, :, h * 128 : (h + 1) * 128] = part
-    value = conv(pick_both(x31, 4), k31)
     for side in range(2):
+        value = conv(block(x31.at[side], 0, 4), k31)
         for k in range(4):
-            at = (side * 4 + k) * W3
-            spread(value[at : at + W3], ea[side, k * W3 : (k + 1) * W3], u2.at[side], k)
+            spread(value[k * W3 : (k + 1) * W3], ea[side, k * W3 : (k + 1) * W3], u2.at[side], k)
         for r in range(8):
             at = slice(r * W2, (r + 1) * W2)
             arriving = u2[side, r * WU + LEAD : r * WU + LEAD + W2] + ei[side, at]
@@ -451,7 +465,7 @@
 STORED = pl.BlockSpec(memory_space=pltpu.MemorySpace.HBM)
 
 
-def call(body, args, outs, scratch=(), specs=None, out_specs=None, aliases=None, cost=0, limit=8):
+def call(body, args, outs, scratch=(), specs=None, out_specs=None, aliases=None, cost=0, limit=8, flags=None):
     shapes = [jax.ShapeDtypeStruct(s, d) for s, d in outs]
     return pl.pallas_call(
         body,
@@ -462,7 +476,7 @@
         input_output_aliases=aliases or {},
         scratch_shapes=[pltpu.VMEM(*s) if isinstance(s, tuple) else s for s in scratch],
         cost_estimate=pl.CostEstimate(flops=cost, bytes_accessed=4000000, transcendentals=0),
-        compiler_params=pltpu.CompilerParams(vmem_limit_bytes=limit << 20),
+        compiler_params=pltpu.CompilerParams(vmem_limit_bytes=limit << 20, flags=flags),
     )(*args)
 
 
@@ -492,19 +506,19 @@
             ((12, rows * 8, 128), F32), ((6, tall * 8, 128), F32), ((2, COL_TOTAL, 128), F32),
             pltpu.SemaphoreType.DMA((18,)),
         ],
-        specs=[STORED] * 10, cost=10**9, limit=LIM[0],
+        specs=[STORED] * 10, cost=10**9, limit=LIM[0], flags=FLAGS[0],
     )
     fl, fr = swap(left, right, "col")
     i22, seeds, k21d, k22 = call(
         own_inject, (m22, t22, m33, t33, w2, w3, k21.T, k22),
         [((tall, wide, ch2), F32), ((rows, cols, ch3), BF16), ((3 * ch2, 256), BF16), ((3 * ch2, 384), BF16)],
-        cost=10**9, limit=LIM[1],
+        cost=10**9, limit=LIM[1], flags=FLAGS[1],
     )
     up, down = call(
         pack_rows, (seeds, m32, m31, m22, i22, m21, a2, fl, fr),
         [((ROW_TOTAL, 128), BF16), ((ROW_TOTAL, 128), BF16)],
         scratch=[((COL_TOTAL, 128), F32), ((COL_TOTAL, 128), F32), ((2, ROW_TOTAL, 128), F32)],
-        cost=10**9, limit=LIM[2],
+        cost=10**9, limit=LIM[2], flags=FLAGS[2],
     )
     above, below = swap(up, down, "row")
     area3, area2 = rows * W3, tall * W2
@@ -527,7 +541,7 @@
             (((tall - 16) * WP, 128), F32), ((2 * GROUP, 2 * tall - 32, 128), F32), ((2 * tall - 32, shape[1]), BF16),
             pltpu.SemaphoreType.DMA((wide // 2 // GROUP,)),
         ],
-        cost=10**10, limit=LIM[3],
+        cost=10**10, limit=LIM[3], flags=FLAGS[3],
     )
     args = (*state, above, below, a1, k33, k32, k31, k22, k21d)
     (result,) = call(
@@ -542,7 +556,7 @@
             ((2, 8 * WP, 128), F32), ((4 * GROUP, 16, 128), F32), ((2, 16, shape[1]), BF16),
             pltpu.SemaphoreType.DMA((2 * (wide // 2 // GROUP),)),
         ],
-        cost=10**9, limit=LIM[4],
+        cost=10**9, limit=LIM[4], flags=FLAGS[4],
     )
     return result
 

time: 36.5 us -> 35.2 us (0.964)
  the two profiles are of different devices: /device:TPU:225 before, /device:TPU:223 now
where the time goes in v5:
time: 35.2 us; the launch traced here: 35 us
  starting transfers between devices  14.2 us (40%)
  Pallas kernels  13.8 us (39%)
  waiting for transfers between devices  6.62 us (19%)
    pallas_call x5, Pallas kernels, call(): pl.pallas_call(body, grid=(1,), in_specs=specs or [whole(a) for a in args...  13.8 us
    ppermute x2, starting transfers between devices, swap(): lax.ppermute(last, axis, [(i, i + 1) for i in range(count - 1)])  10.4 us
    ppermute x2, waiting for transfers between devices, swap(): lax.ppermute(first, axis, [(i + 1, i) for i in range(count - 1)])  6.62 us
    ppermute x2, starting transfers between devices, swap(): lax.ppermute(first, axis, [(i + 1, i) for i in range(count - 1)])  3.84 us
  transfers between devices with their start and end apart: 4, of which 2 were waited for; matrix products, arithmetic and copies ran while one was open for 0% of the time, Pallas kernels for 21%

profile of v5, /device:TPU:223, one launch (start us, length us, event | category | flops | bytes accessed | tf_op | source)
XLA Modules:
  0.0 35.0 jit_solution(17682284276406678375)
XLA Ops:
  0.1 2.2 %shard_map.155 = (bf16[464,128]{1,0:T(8,128)(2,1)S(1)}, bf16[464,128]{1,0:T(8,128)(2,1)S(1)}) custom-call(bf16[16,32,256]{2,1,0:T(8,128)(2,1)} %hm33.1, bf16[16,32,256]{2,1,0:T(8,128)(2,1)} %ht33.1, bf16[16,32,256]{2,1,0:T(8,128)(2,1)} %m32.3, bf16[16,32,256]{2,1,0:T(8,128)(2,1)} %m31.3, bf16[32,64,128]{2,1,0:T(8,128)(2,1)} %m22.5, ...), custom_call_target="tpu_custom_call" | custom-call | flops 1000000000 | bytes 4000000 | tf_op jit(solution)/shard_map/pallas_call | solution.py:470
  2.3 5.8 %collective-permute-start = (bf16[464,128]{1,0:T(8,128)(2,1)S(1)}, bf16[464,128]{1,0:T(8,128)(2,1)S(1)}, u32[]{:S(2)}, u32[]{:S(2)}) collective-permute-start(bf16[464,128]{1,0:T(8,128)(2,1)S(1)} %get-tuple-element.27), channel_id=1, source_target_pairs={{0,1},{1,2},{2,3},{3,4},{4,5},{5,6},{6,7},{7,8},{8,9},{9,10},{10,1... | collective-permute-start | bytes 356360 | tf_op jit(solution)/shard_map/ppermute | solution.py:485
  8.1 1.9 %collective-permute-start.1 = (bf16[464,128]{1,0:T(8,128)(2,1)S(1)}, bf16[464,128]{1,0:T(8,128)(2,1)S(1)}, u32[]{:S(2)}, u32[]{:S(2)}) collective-permute-start(bf16[464,128]{1,0:T(8,128)(2,1)S(1)} %get-tuple-element.28), channel_id=1, source_target_pairs={{1,0},{2,1},{3,2},{4,3},{5,4},{6,5},{7,6},{8,7},{9,8},{10,9},{11,1... | collective-permute-start | bytes 356360 | tf_op jit(solution)/shard_map/ppermute | solution.py:486
  10.1 0.0 copy-start.6
  10.1 0.0 copy-start.10
  10.1 0.0 copy-start.11
  10.1 0.0 copy-start.12
  10.1 1.6 %shard_map.154 = (f32[32,64,128]{2,1,0:T(8,128)S(1)}, bf16[16,32,256]{2,1,0:T(8,128)(2,1)S(1)}, bf16[384,256]{1,0:T(8,128)(2,1)S(1)}, bf16[384,384]{1,0:T(8,128)(2,1)S(1)}) custom-call(bf16[32,64,128]{2,1,0:T(8,128)(2,1)S(1)} %copy-done.5, bf16[32,64,128]{2,1,0:T(8,128)(2,1)S(1)} %copy-done.4, bf16[16,32,256]{2,1,0:T(8,128)(2,1)S(1)} %copy-done.8, ...), custom_call_target="tpu_custom_call" | custom-call | flops 1000000000 | bytes 4000000 | tf_op jit(solution)/shard_map/pallas_call | solution.py:470
  11.8 0.0 collective-permute-done.fl
  11.8 3.6 %collective-permute-done.1.fr = bf16[464,128]{1,0:T(8,128)(2,1)S(1)} collective-permute-done((bf16[464,128]{1,0:T(8,128)(2,1)S(1)}, bf16[464,128]{1,0:T(8,128)(2,1)S(1)}, u32[]{:S(2)}, u32[]{:S(2)}) %collective-permute-start.1) | collective-permute-done | bytes 118816 | tf_op jit(solution)/shard_map/ppermute | solution.py:486
  15.4 0.0 copy-done.6
  15.5 0.0 copy-start
  15.5 0.0 copy-start.1
  15.5 0.0 copy-start.2
  15.5 0.0 copy-start.3
  15.5 0.2 shard_map.157
  15.7 4.6 %collective-permute-start.2 = (bf16[1120,128]{1,0:T(8,128)(2,1)S(1)}, bf16[1120,128]{1,0:T(8,128)(2,1)S(1)}, u32[]{:S(2)}, u32[]{:S(2)}) collective-permute-start(bf16[1120,128]{1,0:T(8,128)(2,1)S(1)} %get-tuple-element.42), channel_id=1, source_target_pairs={{0,16},{16,32},{32,48},{48,64},{64,80},{80,96},{96,112},{112,128},... | collective-permute-start | bytes 860168 | tf_op jit(solution)/shard_map/ppermute | solution.py:485
  20.3 1.9 %collective-permute-start.3 = (bf16[1120,128]{1,0:T(8,128)(2,1)S(1)}, bf16[1120,128]{1,0:T(8,128)(2,1)S(1)}, u32[]{:S(2)}, u32[]{:S(2)}) collective-permute-start(bf16[1120,128]{1,0:T(8,128)(2,1)S(1)} %get-tuple-element.43), channel_id=1, source_target_pairs={{16,0},{32,16},{48,32},{64,48},{80,64},{96,80},{112,96},{128,112},... | collective-permute-start | bytes 860168 | tf_op jit(solution)/shard_map/ppermute | solution.py:486
  22.3 0.0 copy-done
  22.3 0.0 copy-done.1
  22.3 5.7 %shard_map.156 = (bf16[64,8192]{1,0:T(8,128)(2,1)}, f32[2,2,96,128]{3,2,1,0:T(8,128)S(1)}, f32[2,2,48,128]{3,2,1,0:T(8,128)S(1)}, f32[2,2,96,128]{3,2,1,0:T(8,12...) custom-call(bf16[16,32,256]{2,1,0:T(8,128)(2,1)S(1)} %get-tuple-elem, ...), custom_call_target="tpu_custom_call" | custom-call | flops 10000000000 | bytes 4000000 | tf_op jit(solution)/shard_map/pallas_call | solution.py:470
  28.0 0.0 collective-permute-done.2.above
  28.1 3.0 %collective-permute-done.3.below = bf16[1120,128]{1,0:T(8,128)(2,1)S(1)} collective-permute-done((bf16[1120,128]{1,0:T(8,128)(2,1)S(1)}, bf16[1120,128]{1,0:T(8,128)(2,1)S(1)}, u32[]{:S(2)}, u32[]{:S(2)}) %collective-permute-start.3) | collective-permute-done | bytes 286752 | tf_op jit(solution)/shard_map/ppermute | solution.py:486
  31.0 4.0 %shard_map.158 = bf16[64,8192]{1,0:T(8,128)(2,1)} custom-call(f32[2,2,96,128]{3,2,1,0:T(8,128)S(1)} %get-tuple-element.31.t33, f32[2,2,48,128]{3,2,1,0:T(8,128)S(1)} %get-tuple-element.32.t32, f32[2,2,96,128]{3,2,1,0:T(8,128)S(1)} %get-tuple-element.33.t31, f32[2,144,128]{2,1,0:T(8,128)S(1)} %get-tuple-element.34.ta, ...), custom_call_target="tpu_custom_call", output_to_operand_aliasing={{}: (19, {})} | custom-call | flops 1000000000 | bytes 4000000 | tf_op jit(solution)/shard_map/pallas_call | solution.py:470
  (21 shorter events, 0.0 us)
Async XLA Ops:
  0.0 10.0 %copy-start.4 = (bf16[32,64,128]{2,1,0:T(8,128)(2,1)S(1)}, bf16[32,64,128]{2,1,0:T(8,128)(2,1)}, u32[]{:S(2)}) copy-start(bf16[32,64,128]{2,1,0:T(8,128)(2,1)} %ht22.1) | copy-start | bytes 1572868
  0.0 10.0 %copy-start.5 = (bf16[32,64,128]{2,1,0:T(8,128)(2,1)S(1)}, bf16[32,64,128]{2,1,0:T(8,128)(2,1)}, u32[]{:S(2)}) copy-start(bf16[32,64,128]{2,1,0:T(8,128)(2,1)} %m22.5) | copy-start | bytes 1572868
  0.0 10.0 %copy-start.7 = (bf16[128,1152]{1,0:T(8,128)(2,1)S(1)}, bf16[128,1152]{1,0:T(8,128)(2,1)}, u32[]{:S(2)}) copy-start(bf16[128,1152]{1,0:T(8,128)(2,1)} %k22.1) | copy-start | bytes 884740
  0.0 10.0 %copy-start.8 = (bf16[16,32,256]{2,1,0:T(8,128)(2,1)S(1)}, bf16[16,32,256]{2,1,0:T(8,128)(2,1)}, u32[]{:S(2)}) copy-start(bf16[16,32,256]{2,1,0:T(8,128)(2,1)} %hm33.1) | copy-start | bytes 786436
  0.0 10.0 %copy-start.9 = (bf16[16,32,256]{2,1,0:T(8,128)(2,1)S(1)}, bf16[16,32,256]{2,1,0:T(8,128)(2,1)}, u32[]{:S(2)}) copy-start(bf16[16,32,256]{2,1,0:T(8,128)(2,1)} %ht33.1) | copy-start | bytes 786436
  0.0 10.0 %copy-start.13 = (bf16[128,576]{0,1:T(8,128)(2,1)S(1)}, bf16[128,576]{0,1:T(8,128)(2,1)}, u32[]{:S(2)}) copy-start(bf16[128,576]{0,1:T(8,128)(2,1)} %param.27) | copy-start | bytes 442372
  0.0 10.0 %copy-start.14 = (f32[256]{0:T(256)S(1)}, f32[256]{0:T(256)}, u32[]{:S(2)}) copy-start(f32[256]{0:T(256)} %param.26) | copy-start | bytes 3076
  0.0 10.0 %copy-start.15 = (f32[128]{0:T(128)S(1)}, f32[128]{0:T(128)}, u32[]{:S(2)}) copy-start(f32[128]{0:T(128)} %param.25) | copy-start | bytes 1540
  2.3 9.5 %collective-permute-start = (bf16[464,128]{1,0:T(8,128)(2,1)S(1)}, bf16[464,128]{1,0:T(8,128)(2,1)S(1)}, u32[]{:S(2)}, u32[]{:S(2)}) collective-permute-start(bf16[464,128]{1,0:T(8,128)(2,1)S(1)} %get-tuple-element.27), channel_id=1, source_target_pairs={{0,1},{1,2},{2,3},{3,4},{4,5},{5,6},{6,7},{7,8},{8,9},{9,10},{10,1... | collective-permute-start | bytes 356360 | tf_op jit(solution)/shard_map/ppermute | solution.py:485
  8.1 7.4 %collective-permute-start.1 = (bf16[464,128]{1,0:T(8,128)(2,1)S(1)}, bf16[464,128]{1,0:T(8,128)(2,1)S(1)}, u32[]{:S(2)}, u32[]{:S(2)}) collective-permute-start(bf16[464,128]{1,0:T(8,128)(2,1)S(1)} %get-tuple-element.28), channel_id=1, source_target_pairs={{1,0},{2,1},{3,2},{4,3},{5,4},{6,5},{7,6},{8,7},{9,8},{10,9},{11,1... | collective-permute-start | bytes 356360 | tf_op jit(solution)/shard_map/ppermute | solution.py:486
  10.1 5.4 %copy-start.6 = (bf16[32,64,128]{2,1,0:T(8,128)(2,1)S(1)}, bf16[32,64,128]{2,1,0:T(8,128)(2,1)}, u32[]{:S(2)}) copy-start(bf16[32,64,128]{2,1,0:T(8,128)(2,1)} %m21.3) | copy-start | bytes 1572868
  10.1 5.4 %copy-start.10 = (bf16[16,32,256]{2,1,0:T(8,128)(2,1)S(1)}, bf16[16,32,256]{2,1,0:T(8,128)(2,1)}, u32[]{:S(2)}) copy-start(bf16[16,32,256]{2,1,0:T(8,128)(2,1)} %m32.3) | copy-start | bytes 786436
  10.1 5.3 %copy-start.11 = (bf16[16,32,256]{2,1,0:T(8,128)(2,1)S(1)}, bf16[16,32,256]{2,1,0:T(8,128)(2,1)}, u32[]{:S(2)}) copy-start(bf16[16,32,256]{2,1,0:T(8,128)(2,1)} %m31.3) | copy-start | bytes 786436
  10.1 5.3 %copy-start.12 = (s32[16,4096]{1,0:T(8,128)S(1)}, s32[16,4096]{1,0:T(8,128)}, u32[]{:S(2)}) copy-start(s32[16,4096]{1,0:T(8,128)} %a2.3) | copy-start | bytes 786436
  15.5 6.8 %copy-start = (bf16[256,2304]{1,0:T(8,128)(2,1)S(1)}, bf16[256,2304]{1,0:T(8,128)(2,1)}, u32[]{:S(2)}) copy-start(bf16[256,2304]{1,0:T(8,128)(2,1)} %k33.3) | copy-start | bytes 3538948
  15.5 6.8 %copy-start.1 = (bf16[256,2304]{1,0:T(8,128)(2,1)S(1)}, bf16[256,2304]{1,0:T(8,128)(2,1)}, u32[]{:S(2)}) copy-start(bf16[256,2304]{1,0:T(8,128)(2,1)} %k32.3) | copy-start | bytes 3538948
  15.5 6.8 %copy-start.2 = (bf16[256,1152]{1,0:T(8,128)(2,1)S(1)}, bf16[256,1152]{1,0:T(8,128)(2,1)}, u32[]{:S(2)}) copy-start(bf16[256,1152]{1,0:T(8,128)(2,1)} %k31.3) | copy-start | bytes 1769476
  15.5 6.8 %copy-start.3 = (s32[32,4096]{1,0:T(8,128)S(1)}, s32[32,4096]{1,0:T(8,128)}, u32[]{:S(2)}) copy-start(s32[32,4096]{1,0:T(8,128)} %a1.3) | copy-start | bytes 1572868
  15.7 12.3 %collective-permute-start.2 = (bf16[1120,128]{1,0:T(8,128)(2,1)S(1)}, bf16[1120,128]{1,0:T(8,128)(2,1)S(1)}, u32[]{:S(2)}, u32[]{:S(2)}) collective-permute-start(bf16[1120,128]{1,0:T(8,128)(2,1)S(1)} %get-tuple-element.42), channel_id=1, source_target_pairs={{0,16},{16,32},{32,48},{48,64},{64,80},{80,96},{96,112},{112,128},... | collective-permute-start | bytes 860168 | tf_op jit(solution)/shard_map/ppermute | solution.py:485
  20.3 10.7 %collective-permute-start.3 = (bf16[1120,128]{1,0:T(8,128)(2,1)S(1)}, bf16[1120,128]{1,0:T(8,128)(2,1)S(1)}, u32[]{:S(2)}, u32[]{:S(2)}) collective-permute-start(bf16[1120,128]{1,0:T(8,128)(2,1)S(1)} %get-tuple-element.43), channel_id=1, source_target_pairs={{16,0},{32,16},{48,32},{64,48},{80,64},{96,80},{112,96},{128,112},... | collective-permute-start | bytes 860168 | tf_op jit(solution)/shard_map/ppermute | solution.py:486
